TPU v7x, 32 devices: a whole 2x2x4 slice. The times are simulated.
32 devices in a mesh: cfd: 16 (over z, x, core), ac: 2 (over y).
Axes of the slice: x: 2, y: 2, z: 4, core: 2. Of those that a mesh axis runs over, the one named last changes fastest.
Arguments:
- surface_raw: bfloat16 [5, 4096, 1024], P(None, ('cfd', 'ac')), may hold values from -6 to 6
- area_normals: bfloat16 [3, 4096], P(None, ('cfd', 'ac')), may hold values from -6 to 6
- kernel_weights: bfloat16 [2, 3, 2048, 4096], P(None, None, None, ('cfd', 'ac')), may hold values from -0.078125 to 0.078125
- block_map: int32 [2, 16, 16], P('ac', 'cfd'), may hold values from 0 to 15, as said below
- band_observers: int32 [16, 128], replicated, may hold values from 0 to 2047, as said below
- band_lags: int32 [16], replicated, may hold values from 0 to 511
Outputs:
- acoustic: float32 [2048, 512], P('cfd', 'ac')
Inputs may be any that keep to these rules, and one draw needn't show every extreme that they name: block_map[j, s, :] is a permutation of 0 to 15 for every j and s. `band_observers`: every observer appears exactly once.
All inputs are finite; a program needn't handle non-finite values.
Results may differ from a plain program's by a relative error of at most 0.0042.
Values may be sent and summed in bfloat16 or wider, within the bound.
No kernel may reach another device: no remote copies, remote signals or barrier semaphores. Data moves between devices by JAX's collectives and lax.ppermute only.
A program may use at most 64 MiB of HBM per device.

v0:
```python
import jax
import jax.numpy as jnp
from jax import lax
from jax.sharding import PartitionSpec as P


def thickness(surface, normals):
    along = surface[2].astype(jnp.float32) * normals[0].astype(jnp.float32)[:, None]
    along = along + surface[3].astype(jnp.float32) * normals[1].astype(jnp.float32)[:, None]
    along = along + surface[4].astype(jnp.float32) * normals[2].astype(jnp.float32)[:, None]
    return (surface[1].astype(jnp.float32) * along).astype(jnp.bfloat16)


def rates(series):
    step = series[:, 1:].astype(jnp.float32) - series[:, :-1].astype(jnp.float32)
    first = jnp.zeros((series.shape[0], 1), jnp.float32)
    return jnp.concatenate([first, step], axis=1).astype(jnp.bfloat16)


def reorder_blocks(array, block_order, blocks):
    lead = array.shape[0]
    rest = array.shape[2:]
    grouped = array.reshape((lead, blocks, -1))
    picked = jnp.take(grouped, block_order, axis=1)
    return picked.reshape((lead, array.shape[1]) + rest)


def local(surface_raw, area_normals, kernel_weights, block_map, band_observers, band_lags):
    blocks = lax.axis_size("cfd")
    block_order = block_map[0, 0]
    thick = thickness(surface_raw, area_normals)
    outgoing = reorder_blocks(jnp.stack([thick, surface_raw[0]]), block_order, blocks)
    arrived = lax.all_to_all(outgoing, "cfd", split_axis=1, concat_axis=1, tiled=True)
    thickness_in = arrived[0]
    pressure_in = arrived[1]
    sources = jnp.stack([rates(thickness_in), rates(pressure_in), pressure_in])
    out_len = sources.shape[2] // 2
    tap_count = kernel_weights.shape[0]
    band_count = band_observers.shape[0]
    band_width = band_observers.shape[1]
    observer_count = kernel_weights.shape[2]

    def one_band(carry, band_index):
        delay = band_lags[band_index]
        start = band_index * band_width
        chosen = lax.dynamic_slice_in_dim(kernel_weights, start, band_width, 2)
        windows = jnp.stack(
            [
                lax.dynamic_slice_in_dim(sources, out_len - delay - shift_step, out_len, 2)
                for shift_step in range(tap_count)
            ]
        )
        contribution = jnp.einsum(
            "kcof,kcft->ot", chosen, windows, preferred_element_type=jnp.float32
        )
        return (carry, contribution)

    _, banded = lax.scan(one_band, 0, jnp.arange(band_count, dtype=jnp.int32))
    banded = banded.reshape(observer_count, out_len)
    flat_ids = band_observers.reshape(-1)
    inverse = (
        jnp.zeros((observer_count,), jnp.int32)
        .at[flat_ids]
        .set(jnp.arange(observer_count, dtype=jnp.int32))
    )
    partial_value = jnp.take(banded, inverse, axis=0)
    reduced = lax.psum_scatter(partial_value, "cfd", scatter_dimension=0, tiled=True)
    result = lax.psum_scatter(reduced, "ac", scatter_dimension=1, tiled=True)
    return result


def solution(mesh):
    placed = (
        P(None, ("cfd", "ac"), None),
        P(None, ("cfd", "ac")),
        P(None, None, None, ("cfd", "ac")),
        P("ac", "cfd", None),
        P(),
        P(),
    )
    return jax.shard_map(
        local, mesh=mesh, in_specs=placed, out_specs=P("cfd", "ac"), check_vma=False
    )
```

profile of v0, /device:TPU:0, one launch (start us, length us, event | category | flops | bytes accessed | tf_op | source)
XLA Modules:
  0.0 283.1 jit_solution(15173410977402433018)
XLA Ops:
  7.2 0.7 compare_and_fusion.1
  7.9 0.8 bitcast_convert_fusion.2
  8.6 1.0 slice.49
  9.6 1.5 multiply_convert_fusion
  11.6 1.2 pad_maximum_fusion.1
  12.8 1.6 gather_fusion
  15.3 1.3 copy.23
  16.6 7.4 %all-to-all-start = ((bf16[2,128,1024]{2,0,1:T(2,128)(2,1)}), bf16[2,128,1024]{2,0,1:T(2,128)(2,1)S(1)}, u32[]{:S(2)}, u32[]{:S(2)}) async-start(bf16[2,128,1024]{2,0,1:T(2,128)(2,1)} %copy.23), calls=%async_computation | async-start | bytes 1048576 | tf_op jit(solution)/shard_map/all_to_all | solution.py:33
  24.1 8.0 %scatter_custom_fusion = s32[2048]{0:T(1024)S(1)} fusion(s32[2048]{0:T(1024)S(1)} %bitcast.65, s32[2048]{0:T(1024)S(1)} %iota.6, s32[]{:T(128)} %constant.110.clone.1), kind=kCustom, calls=%fused_computation.28 | custom fusion | bytes 8196 | tf_op jit(solution)/shard_map/scatter | solution.py:64
  32.2 6.1 %all-to-all-done = bf16[2,128,1024]{2,0,1:T(2,128)(2,1)S(1)} async-done(((bf16[2,128,1024]{2,0,1:T(2,128)(2,1)}), bf16[2,128,1024]{2,0,1:T(2,128)(2,1)S(1)}, u32[]{:S(2)}, u32[]{:S(2)}) %all-to-all-start) | async-done | bytes 524320 | tf_op jit(solution)/shard_map/all_to_all | solution.py:33
  38.3 0.7 fusion.10
  40.0 135.2 %while.14 = (s32[]{:T(128)}, f32[16,128,512]{2,1,0:T(8,128)}, s32[16]{0:T(128)S(1)}, bf16[2,3,2048,128]{3,2,1,0:T(8,128)(2,1)}, s32[16]{0:T(128)S(1)}, /*index=5...) while((s32[]{:T(128)}, f32[16,128,512]{2,1,0:T(8,128)}, ...), condition=%wide.region_2.3_spmd, body=%wide.region_1.2_spmd.sunk | while | flops 101056528 | bytes 2818909 | solution.py:58
  46.5 1.9 fusion.16
  55.0 1.9 fusion.16
  63.4 1.9 fusion.16
  71.9 1.9 fusion.16
  80.3 1.9 fusion.16
  88.8 1.9 fusion.16
  97.2 1.9 fusion.16
  105.7 1.9 fusion.16
  114.1 1.9 fusion.16
  122.6 1.9 fusion.16
  131.0 1.9 fusion.16
  139.5 1.9 fusion.16
  147.9 1.9 fusion.16
  156.4 1.9 fusion.16
  164.8 1.9 fusion.16
  173.3 1.9 fusion.16
  175.2 11.7 %gather_fusion.1 = f32[2048,512]{1,0:T(8,128)} fusion(f32[2048,512]{1,0:T(8,128)} %bitcast.60, s32[2048]{0:T(1024)S(1)} %fusion.6), kind=kCustom, calls=%fused_computation.1 | custom fusion | bytes 8396800 | tf_op jit(solution)/shard_map/jit(_take)/gather | solution.py:66
  186.9 3.8 %broadcast_select_fusion = f32[2048,512]{1,0:T(8,128)} fusion(f32[2048,512]{1,0:T(8,128)} %gather_fusion.1, pred[2048]{0:T(1024)(128)(4,1)S(1)} %compare_and_fusion), kind=kLoop, calls=%fused_computation.13 | loop fusion | flops 1048576 | bytes 8390656 | tf_op jit(solution)/shard_map/jit(_take)/select_n | solution.py:66
  190.8 72.4 %reduce-scatter.3.cloned.1.call-done = f32[128,512]{1,0:T(8,128)} async-done(((f32[2048,512]{1,0:T(8,128)}), f32[128,512]{1,0:T(8,128)}) %reduce-scatter.3.cloned.1.call-update) | async-done | bytes 262160 | tf_op jit(solution)/shard_map/reduce_scatter | solution.py:67
  263.2 13.1 %reduce-scatter.5.cloned.1.call-done = f32[128,256]{1,0:T(8,128)} async-done(((f32[128,512]{1,0:T(8,128)}), f32[128,256]{1,0:T(8,128)}) %reduce-scatter.5.cloned.1.call-update) | async-done | bytes 131088 | tf_op jit(solution)/shard_map/reduce_scatter | solution.py:68
  (78 shorter events, 28.5 us)
Async XLA Ops:
  11.3 12.7 %copy-start = (s32[16,128]{1,0:T(8,128)S(1)}, s32[16,128]{1,0:T(8,128)}, u32[]{:S(2)}) copy-start(s32[16,128]{1,0:T(8,128)} %param.12) | copy-start | bytes 24580
  16.6 21.7 %all-to-all-start = ((bf16[2,128,1024]{2,0,1:T(2,128)(2,1)}), bf16[2,128,1024]{2,0,1:T(2,128)(2,1)S(1)}, u32[]{:S(2)}, u32[]{:S(2)}) async-start(bf16[2,128,1024]{2,0,1:T(2,128)(2,1)} %copy.23), calls=%async_computation | async-start | bytes 1048576 | tf_op jit(solution)/shard_map/all_to_all | solution.py:33
  24.0 239.2 %reduce-scatter.3.cloned.1.call-start = ((), (), s32[]{:S(2)}) async-start(), calls=%async_computation.3 | async-start | bytes 4456448 | tf_op jit(solution)/shard_map/reduce_scatter | solution.py:67
  32.2 7.8 %copy-start.1 = (s32[16]{0:T(128)S(1)}, s32[16]{0:T(128)}, u32[]{:S(2)}) copy-start(s32[16]{0:T(128)} %param.13) | copy-start | bytes 196
  190.7 85.6 %reduce-scatter.5.cloned.1.call-start = ((), (), s32[]{:S(2)}) async-start(), calls=%async_computation.4 | async-start | bytes 393216 | tf_op jit(solution)/shard_map/reduce_scatter | solution.py:68
Sparse Core Ops, SparseCore 0:
  190.8 72.3 reduce-scatter.2
  265.4 10.8 reduce-scatter.4
where the time goes:
time: 285 us; the launch traced here: 283 us
  waiting for transfers between devices  91.6 us (32%)
  loops' own time  79.1 us (28%)
  local copies, waits for them, and re-layouts  51.7 us (18%)
  matrix products  30.6 us (11%)
  between operations  13.6 us (5%)
  other arithmetic  9.09 us (3%)
  starting transfers between devices  7.47 us (3%)
    another operation x1, loops' own time, local(): _, banded = lax.scan(one_band, 0, jnp.arange(band_count, dtype=jnp.int32))  79.1 us
    reduce_scatter x1, waiting for transfers between devices, local(): lax.psum_scatter(partial_value, 'cfd', scatter_dimension=0, tiled=True)  72.4 us
    dot_general x16, matrix products, one_band(): jnp.einsum('kcof,kcft->ot', chosen, windows, preferred_element_type=jnp.f...  30.6 us
    reduce_scatter x1, waiting for transfers between devices, local(): result = lax.psum_scatter(reduced, 'ac', scatter_dimension=1, tiled=True)  13.1 us
    gather x1, local copies, waits for them, and re-layouts, local(): partial_value = jnp.take(banded, inverse, axis=0)  11.7 us
    dynamic_slice x16, local copies, waits for them, and re-layouts, local(): _, banded = lax.scan(one_band, 0, jnp.arange(band_count, dtype=jnp.int32))  9.81 us
    dynamic_slice x16, local copies, waits for them, and re-layouts, one_band(): delay = band_lags[band_index]  9.56 us
    scatter x1, local copies, waits for them, and re-layouts, local(): inverse = jnp.zeros((observer_count,), jnp.int32).at[flat_ids].set(jnp.ar...  8.05 us
  transfers between devices with their start and end apart: 3, of which 3 were waited for; matrix products, arithmetic and copies ran while one was open for 3% of the time, Pallas kernels for 0%

commit v1 on v0

v1 whole, which is shorter than its diff:
```python
import functools

import jax
import jax.numpy as jnp
from jax import lax
from jax.experimental import pallas as pl
from jax.experimental.pallas import tpu as pltpu
from jax.sharding import PartitionSpec as P

LANES = 128
AXES = ("cfd", "ac")
SMEM = pl.BlockSpec(memory_space=pltpu.SMEM)
VMEM = pl.BlockSpec(memory_space=pltpu.VMEM)


def outgoing_kernel(blocks, order_ref, surface_ref, normals_ref, out_ref):
    normals = normals_ref[...].astype(jnp.float32)
    rows = surface_ref.shape[2]
    faces = normals.shape[1]
    square = jnp.concatenate([normals, jnp.zeros((faces - normals.shape[0], faces), jnp.float32)], axis=0)
    columns = jnp.transpose(square)
    picked = [columns[p * rows : (p + 1) * rows, :] for p in range(blocks)]
    for p in range(blocks):
        along = surface_ref[2, p].astype(jnp.float32) * picked[p][:, 0:1]
        along = along + surface_ref[3, p].astype(jnp.float32) * picked[p][:, 1:2]
        along = along + surface_ref[4, p].astype(jnp.float32) * picked[p][:, 2:3]
        to = order_ref[p]
        out_ref[to, 0] = (surface_ref[1, p].astype(jnp.float32) * along).astype(jnp.bfloat16)
        out_ref[to, 1] = surface_ref[0, p]


def outgoing(surface, normals, block_to):
    blocks = block_to.shape[0]
    comps, faces, steps = surface.shape
    rows = faces // blocks
    return pl.pallas_call(
        functools.partial(outgoing_kernel, blocks),
        out_shape=jax.ShapeDtypeStruct((blocks, 2, rows, steps), jnp.bfloat16),
        in_specs=[SMEM, VMEM, VMEM],
        out_specs=VMEM,
        name="outgoing",
    )(block_to, surface.reshape(comps, blocks, rows, steps), normals)


def bands_kernel(
    split, cols, me_ref, lags_ref, observers_ref, arrived_ref, weights_ref, keep_ref, send_ref,
    stacked_ref, banded_ref, select_ref,
):
    taps, terms, observers, faces = weights_ref.shape
    blocks, _, rows, steps = arrived_ref.shape
    span = stacked_ref.shape[1]
    out_len = banded_ref.shape[1]
    bands = lags_ref.shape[0]
    width = observers // bands
    wide = out_len + LANES
    pad = jnp.zeros((faces, span - steps), jnp.bfloat16)
    for kind in range(2):
        series = jnp.concatenate([arrived_ref[s, kind].astype(jnp.float32) for s in range(blocks)], axis=0)
        earlier = pltpu.roll(series, 1, 1)
        first = lax.broadcasted_iota(jnp.int32, series.shape, 1) == 0
        rate = jnp.where(first, 0.0, series - earlier)
        made = [(kind, rate)] if kind == 0 else [(1, rate), (2, series)]
        for term, value in made:
            for tap in range(taps):
                moved = pltpu.roll(value, tap, 1) if tap else value
                at = (tap * terms + term) * faces
                stacked_ref[at : at + faces, 0:steps] = moved.astype(jnp.bfloat16)
                stacked_ref[at : at + faces, steps:span] = pad

    def one_band(b, carry):
        start = out_len - lags_ref[b]
        column = pl.multiple_of((start // LANES) * LANES, LANES)
        rest = start % LANES
        at = pl.ds(pl.multiple_of(b * width, width), width)
        chosen = jnp.concatenate(
            [weights_ref[k, c, at, :] for k in range(taps) for c in range(terms)], axis=1
        )
        full = jnp.dot(chosen, stacked_ref[:, pl.ds(column, wide)], preferred_element_type=jnp.float32)
        turned = pltpu.roll(full, (wide - rest) % wide, 1)
        banded_ref[at, :] = turned[:, :out_len].astype(jnp.bfloat16)
        return carry

    lax.fori_loop(0, bands, one_band, 0)

    ranks, sides, parts = split
    each = observers // ranks
    ids = observers_ref[...]
    low = 2 if ranks % 2 == 0 else 1
    mid = 2 if ranks % 4 == 0 else 1
    rest_count = ranks // low // mid
    for c in range(low):
        out_ref = keep_ref if c == 0 else send_ref
        for x in range(mid):
            for z in range(rest_count):
                member = (z * mid + x) * low + c
                base = jnp.bitwise_xor(me_ref[0], member) * each
                row = lax.broadcasted_iota(jnp.int32, (each, observers), 0) + base
                select_ref[z * each : (z + 1) * each, :] = jnp.where(row == ids, 1.0, 0.0).astype(jnp.bfloat16)
            for y in range(parts):
                if parts == 1:
                    data = banded_ref[...]
                else:
                    piece = out_len // parts
                    at = pl.multiple_of(jnp.bitwise_xor(me_ref[1], y) * piece, piece)
                    data = banded_ref[:, pl.ds(at, piece)]
                picked = jnp.dot(select_ref[...], data, preferred_element_type=jnp.float32)
                picked = picked.astype(jnp.bfloat16)
                for z in range(rest_count):
                    out_ref[x, y, z] = picked[z * each : (z + 1) * each, :]


def bands(me, lags, observers, arrived, weights, ranks, sides):
    taps, terms, count, faces = weights.shape
    steps = arrived.shape[3]
    out_len = steps // 2
    piece = out_len // sides
    parts = sides if piece % LANES == 0 else 1
    low = 2 if ranks % 2 == 0 else 1
    mid = 2 if ranks % 4 == 0 else 1
    rest = ranks // low // mid
    each = count // ranks
    shape = jax.ShapeDtypeStruct((mid, parts, rest, each, out_len // parts), jnp.bfloat16)
    return pl.pallas_call(
        functools.partial(bands_kernel, (ranks, sides, parts), out_len),
        out_shape=(shape, shape),
        in_specs=[SMEM, SMEM, VMEM, VMEM, VMEM],
        out_specs=(VMEM, VMEM),
        scratch_shapes=[
            pltpu.VMEM((taps * terms * faces, steps + LANES), jnp.bfloat16),
            pltpu.VMEM((count, out_len), jnp.bfloat16),
            pltpu.VMEM((rest * each, count), jnp.bfloat16),
        ],
        compiler_params=pltpu.CompilerParams(vmem_limit_bytes=48 * 1024 * 1024),
        name="bands",
    )(me, lags, observers.reshape(1, -1), arrived, weights)


def swap(value, ranks, sides, rank_mask, side_mask):
    pairs = [
        (r * sides + s, (r ^ rank_mask) * sides + (s ^ side_mask)) for r in range(ranks) for s in range(sides)
    ]
    return lax.ppermute(value, AXES, pairs)


def local(surface_raw, area_normals, kernel_weights, block_map, band_observers, band_lags):
    ranks = lax.axis_size("cfd")
    sides = lax.axis_size("ac")
    me = jnp.stack([lax.axis_index("cfd"), lax.axis_index("ac")]).astype(jnp.int32)
    order = block_map[0, 0]
    count = lax.iota(jnp.int32, ranks)
    block_to = jnp.sum(jnp.where(order[None, :] == count[:, None], count[None, :], 0), axis=1)
    sent = outgoing(surface_raw, area_normals, block_to)
    arrived = lax.all_to_all(sent, "cfd", split_axis=0, concat_axis=0, tiled=True)
    keep, send = bands(me, band_lags, band_observers, arrived, kernel_weights, ranks, sides)
    mid, parts, rest, each, piece = keep.shape
    if parts != sides:
        which = jnp.bitwise_xor(lax.iota(jnp.int32, sides), me[1])

        def by_side(value):
            value = value.reshape(mid, rest, each, sides, piece // sides)
            value = jnp.take(value, which, axis=3)
            return jnp.transpose(value, (0, 3, 1, 2, 4))

        keep, send = by_side(keep), by_side(send)
    got = swap(send, ranks, sides, 1, 0)
    low_sides = min(2, sides)
    high_sides = sides // low_sides
    shape = (mid, high_sides, low_sides) + keep.shape[2:]
    keep, got = keep.reshape(shape), got.reshape(shape)

    def first(x, y):
        return keep[x, :, y].astype(jnp.float32) + got[x, :, y].astype(jnp.float32)

    total = first(0, 0)
    for x, y in [(1, 1), (1, 0), (0, 1)]:
        if x < mid and y < low_sides:
            total = total + swap(first(x, y).astype(jnp.bfloat16), ranks, sides, 2 * x, y).astype(jnp.float32)
    result = total[:, 0]
    for z in range(rest - 1, 0, -1):
        result = result + swap(total[:, z].astype(jnp.bfloat16), ranks, sides, 4 * z, 0).astype(jnp.float32)
    out = result[0]
    for y in range(high_sides - 1, 0, -1):
        out = out + swap(result[y].astype(jnp.bfloat16), ranks, sides, 0, 2 * y).astype(jnp.float32)
    return out


def solution(mesh):
    placed = (
        P(None, ("cfd", "ac"), None),
        P(None, ("cfd", "ac")),
        P(None, None, None, ("cfd", "ac")),
        P("ac", "cfd", None),
        P(),
        P(),
    )
    return jax.shard_map(
        local, mesh=mesh, in_specs=placed, out_specs=P("cfd", "ac"), check_vma=False
    )
```

time: 285 us -> 69.5 us (0.24)
  loops' own time: 79.1 us -> 0 us
  waiting for transfers between devices: 91.6 us -> 33 us
  local copies, waits for them, and re-layouts: 51.7 us -> 3.26 us
  matrix products: 30.6 us -> 0 us
  Pallas kernels: 0 us -> 14.8 us
  between operations: 13.6 us -> 0.05 us
  starting transfers between devices: 7.47 us -> 15.7 us
  other arithmetic: 9.09 us -> 2.4 us
    reduce_scatter x2 -> x0, waiting for transfers between devices: 85.5 us -> none  [the longest x1 72.4 us: local(): lax.psum_scatter(partial_value, 'cfd', scatter_dimension=0, tiled=True)]
    another operation x1 -> x0, loops' own time: 79.1 us -> none  [local(): _, banded = lax.scan(one_band, 0, jnp.arange(band_count, dtype=jnp.int32))]
    dot_general x16 -> x0, matrix products: 30.6 us -> none  [one_band(): jnp.einsum('kcof,kcft->ot', chosen, windows, preferred_element_type=jnp.f...]
    dynamic_slice x32 -> x0, local copies, waits for them, and re-layouts: 19.4 us -> none  [the longest x16 9.81 us: local(): _, banded = lax.scan(one_band, 0, jnp.arange(band_count, dtype=jnp.int32))]
    ppermute x0 -> x7, waiting for transfers between devices: none -> 18.8 us  [swap(): return lax.ppermute(value, AXES, pairs)]
    pallas_call x0 -> x2, Pallas kernels: none -> 14.8 us  [the longest x1 12.4 us: bands(): pl.pallas_call(functools.partial(bands_kernel, (ranks, sides, parts), out...]
    gather x4 -> x0, local copies, waits for them, and re-layouts: 13.9 us -> none  [the longest x1 11.7 us: local(): partial_value = jnp.take(banded, inverse, axis=0)]
    ppermute x0 -> x7, starting transfers between devices: none -> 8.28 us  [swap(): return lax.ppermute(value, AXES, pairs)]
  transfers between devices with their start and end apart: 3 -> 8, of which waited for: 3 -> 7; matrix products, arithmetic and copies ran while one was open for 3% -> 0% of each run, Pallas kernels for 0% -> 0%
where the time goes in v1:
time: 69.5 us; the launch traced here: 69.2 us
  waiting for transfers between devices  33 us (47%)
  starting transfers between devices  15.7 us (23%)
  Pallas kernels  14.8 us (21%)
  local copies, waits for them, and re-layouts  3.26 us (5%)
  other arithmetic  2.4 us (3%)
    ppermute x7, waiting for transfers between devices, swap(): return lax.ppermute(value, AXES, pairs)  18.8 us
    all_to_all x1, waiting for transfers between devices, local(): lax.all_to_all(sent, 'cfd', split_axis=0, concat_axis=0, tiled=True)  14.2 us
    pallas_call x1, Pallas kernels, bands(): pl.pallas_call(functools.partial(bands_kernel, (ranks, sides, parts), out...  12.4 us
    ppermute x7, starting transfers between devices, swap(): return lax.ppermute(value, AXES, pairs)  8.28 us
    all_to_all x1, starting transfers between devices, local(): lax.all_to_all(sent, 'cfd', split_axis=0, concat_axis=0, tiled=True)  7.39 us
    unnamed x6, local copies, waits for them, and re-layouts  3.24 us
    pallas_call x1, Pallas kernels, outgoing(): pl.pallas_call(functools.partial(outgoing_kernel, blocks), out_shape=jax....  2.45 us
  transfers between devices with their start and end apart: 8, of which 7 were waited for; matrix products, arithmetic and copies ran while one was open for 0% of the time, Pallas kernels for 0%

profile of v1, /device:TPU:0, one launch (start us, length us, event | category | flops | bytes accessed | tf_op | source)
XLA Modules:
  0.0 69.2 jit_solution(4839566749917066792)
XLA Ops:
  0.0 1.3 %select_reduce_fusion.order_ref = s32[16]{0:T(128)} fusion(s32[16]{0:T(128)} %bitcast.53), kind=kLoop, calls=%fused_computation.19 | loop fusion | flops 752 | bytes 128 | tf_op jit(solution)/shard_map/reduce_sum | solution.py:151
  1.3 2.4 %outgoing.1 = bf16[16,2,8,1024]{3,2,1,0:T(8,128)(2,1)} custom-call(s32[16]{0:T(128)} %select_reduce_fusion.order_ref, bf16[5,16,8,1024]{3,2,1,0:T(8,128)(2,1)} %bitcast.49, bf16[3,128]{1,0:T(4,128)(2,1)} %normals_ref.1), custom_call_target="tpu_custom_call" | custom-call | tf_op jit(solution)/shard_map/outgoing/pallas_call | solution.py:36
  3.7 7.4 %all-to-all-start = ((bf16[16,2,8,1024]{3,2,1,0:T(8,128)(2,1)}), bf16[16,2,8,1024]{3,2,1,0:T(8,128)(2,1)S(1)}, u32[]{:S(2)}, u32[]{:S(2)}) async-start(bf16[16,2,8,1024]{3,2,1,0:T(8,128)(2,1)} %outgoing.1), calls=%async_computation | async-start | bytes 1048576 | tf_op jit(solution)/shard_map/all_to_all | solution.py:153
  11.1 0.1 pad_add_fusion.me_ref
  11.2 14.2 %all-to-all-done.arrived_ref = bf16[16,2,8,1024]{3,2,1,0:T(8,128)(2,1)S(1)} async-done(((bf16[16,2,8,1024]{3,2,1,0:T(8,128)(2,1)}), bf16[16,2,8,1024]{3,2,1,0:T(8,128)(2,1)S(1)}, u32[]{:S(2)}, u32[]{:S(2)}) %all-to-all-start) | async-done | bytes 524320 | tf_op jit(solution)/shard_map/all_to_all | solution.py:153
  25.4 0.0 copy-start
  25.4 1.9 %copy-done = bf16[2,3,2048,128]{3,2,1,0:T(8,128)(2,1)S(1)} copy-done((bf16[2,3,2048,128]{3,2,1,0:T(8,128)(2,1)S(1)}, bf16[2,3,2048,128]{3,2,1,0:T(8,128)(2,1)}, u32[]{:S(2)}) %copy-start) | copy-done | bytes 3145752
  27.3 0.0 copy-start.1
  27.3 0.7 %copy-done.1 = s32[16,128]{1,0:T(8,128)S(1)} copy-done((s32[16,128]{1,0:T(8,128)S(1)}, s32[16,128]{1,0:T(8,128)}, u32[]{:S(2)}) %copy-start.1) | copy-done | bytes 8216
  28.0 0.0 copy-start.2
  28.0 0.7 copy-done.2
  28.6 12.4 %bands.1 = (bf16[2,2,4,128,256]{4,3,2,1,0:T(8,128)(2,1)S(1)}, bf16[2,2,4,128,256]{4,3,2,1,0:T(8,128)(2,1)S(1)}) custom-call(s32[2]{0:T(128)S(1)} %pad_add_fusion.me_ref, s32[16]{0:T(128)S(1)} %copy-done.2, s32[1,2048]{1,0:T(1,128)S(1)} %bitcast.48, bf16[16,2,8,1024]{3,2,1,0:T(8,128)(2,1)S(1)} %all-to-all-done.arrived_ref, bf16[2,3,2048,128]{3,2,1,0:T(8,128)(2,1)S(1)} %copy-done), custom_call_target="tpu_custom_call" | custom-call | tf_op jit(solution)/shard_map/bands/pallas_call | solution.py:123
  41.0 0.2 collective-permute-start
  41.2 2.5 %collective-permute-done = bf16[2,2,4,128,256]{4,3,2,1,0:T(8,128)(2,1)S(1)} collective-permute-done((bf16[2,2,4,128,256]{4,3,2,1,0:T(8,128)(2,1)S(1)}, bf16[2,2,4,128,256]{4,3,2,1,0:T(8,128)(2,1)S(1)}, u32[]{:S(2)}, u32[]{:S(2)}) %collective-permute-start) | collective-permute-done | bytes 1048608 | tf_op jit(solution)/shard_map/ppermute | solution.py:142
  43.7 0.1 fusion.5
  43.8 1.6 %collective-permute-start.3 = (bf16[1,4,128,256]{3,2,1,0:T(8,128)(2,1)S(1)}, bf16[1,4,128,256]{3,2,1,0:T(8,128)(2,1)S(1)}, u32[]{:S(2)}, u32[]{:S(2)}) collective-permute-start(bf16[1,4,128,256]{3,2,1,0:T(8,128)(2,1)S(1)} %fusion.5), channel_id=1, source_target_pairs={{0,1},{1,0},{2,3},{3,2},{4,5},{5,4},{6,7},{7,6},{8,9},{9,8},{10,11... | collective-permute-start | bytes 786440 | tf_op jit(solution)/shard_map/ppermute | solution.py:142
  45.4 0.1 fusion.3
  45.5 1.0 %collective-permute-start.1 = (bf16[1,4,128,256]{3,2,1,0:T(8,128)(2,1)S(1)}, bf16[1,4,128,256]{3,2,1,0:T(8,128)(2,1)S(1)}, u32[]{:S(2)}, u32[]{:S(2)}) collective-permute-start(bf16[1,4,128,256]{3,2,1,0:T(8,128)(2,1)S(1)} %get-tuple-element.11), channel_id=1, source_target_pairs={{0,5},{1,4},{2,7},{3,6},{4,1},{5,0},{6,3},{7,2},{8,13},{9,12},{10,... | collective-permute-start | bytes 786440 | tf_op jit(solution)/shard_map/ppermute | solution.py:142
  46.6 1.0 %collective-permute-start.2 = (bf16[1,4,128,256]{3,2,1,0:T(8,128)(2,1)S(1)}, bf16[1,4,128,256]{3,2,1,0:T(8,128)(2,1)S(1)}, u32[]{:S(2)}, u32[]{:S(2)}) collective-permute-start(bf16[1,4,128,256]{3,2,1,0:T(8,128)(2,1)S(1)} %get-tuple-element.12), channel_id=1, source_target_pairs={{0,4},{1,5},{2,6},{3,7},{4,0},{5,1},{6,2},{7,3},{8,12},{9,13},{10,... | collective-permute-start | bytes 786440 | tf_op jit(solution)/shard_map/ppermute | solution.py:142
  47.5 10.3 %collective-permute-done.3 = bf16[1,4,128,256]{3,2,1,0:T(8,128)(2,1)S(1)} collective-permute-done((bf16[1,4,128,256]{3,2,1,0:T(8,128)(2,1)S(1)}, bf16[1,4,128,256]{3,2,1,0:T(8,128)(2,1)S(1)}, u32[]{:S(2)}, u32[]{:S(2)}) %collective-permute-start.3) | collective-permute-done | bytes 262176 | tf_op jit(solution)/shard_map/ppermute | solution.py:142
  57.8 0.0 collective-permute-done.1
  57.8 1.4 %collective-permute-done.2 = bf16[1,4,128,256]{3,2,1,0:T(8,128)(2,1)S(1)} collective-permute-done((bf16[1,4,128,256]{3,2,1,0:T(8,128)(2,1)S(1)}, bf16[1,4,128,256]{3,2,1,0:T(8,128)(2,1)S(1)}, u32[]{:S(2)}, u32[]{:S(2)}) %collective-permute-start.2) | collective-permute-done | bytes 262176 | tf_op jit(solution)/shard_map/ppermute | solution.py:142
  59.3 0.2 fusion.10
  59.5 2.1 %collective-permute-start.4 = (bf16[1,128,256]{2,1,0:T(8,128)(2,1)S(1)}, bf16[1,128,256]{2,1,0:T(8,128)(2,1)S(1)}, u32[]{:S(2)}, u32[]{:S(2)}) collective-permute-start(bf16[1,128,256]{2,1,0:T(8,128)(2,1)S(1)} %get-tuple-element.13), channel_id=1, source_target_pairs={{0,24},{1,25},{2,26},{3,27},{4,28},{5,29},{6,30},{7,31},{8,16},{9,... | collective-permute-start | bytes 196616 | tf_op jit(solution)/shard_map/ppermute | solution.py:142
  61.6 0.9 %collective-permute-start.6 = (bf16[1,128,256]{2,1,0:T(8,128)(2,1)S(1)}, bf16[1,128,256]{2,1,0:T(8,128)(2,1)S(1)}, u32[]{:S(2)}, u32[]{:S(2)}) collective-permute-start(bf16[1,128,256]{2,1,0:T(8,128)(2,1)S(1)} %get-tuple-element.14), channel_id=1, source_target_pairs={{0,8},{1,9},{2,10},{3,11},{4,12},{5,13},{6,14},{7,15},{8,0},{9,1},... | collective-permute-start | bytes 196616 | tf_op jit(solution)/shard_map/ppermute | solution.py:142
  62.5 1.4 %collective-permute-start.5 = (bf16[1,128,256]{2,1,0:T(8,128)(2,1)S(1)}, bf16[1,128,256]{2,1,0:T(8,128)(2,1)S(1)}, u32[]{:S(2)}, u32[]{:S(2)}) collective-permute-start(bf16[1,128,256]{2,1,0:T(8,128)(2,1)S(1)} %get-tuple-element.15), channel_id=1, source_target_pairs={{0,16},{1,17},{2,18},{3,19},{4,20},{5,21},{6,22},{7,23},{8,24},{9,... | collective-permute-start | bytes 196616 | tf_op jit(solution)/shard_map/ppermute | solution.py:142
  63.9 2.2 %collective-permute-done.4 = bf16[1,128,256]{2,1,0:T(8,128)(2,1)S(1)} collective-permute-done((bf16[1,128,256]{2,1,0:T(8,128)(2,1)S(1)}, bf16[1,128,256]{2,1,0:T(8,128)(2,1)S(1)}, u32[]{:S(2)}, u32[]{:S(2)}) %collective-permute-start.4) | collective-permute-done | bytes 65568 | tf_op jit(solution)/shard_map/ppermute | solution.py:142
  66.1 0.4 collective-permute-done.6
  66.5 2.0 %collective-permute-done.5 = bf16[1,128,256]{2,1,0:T(8,128)(2,1)S(1)} collective-permute-done((bf16[1,128,256]{2,1,0:T(8,128)(2,1)S(1)}, bf16[1,128,256]{2,1,0:T(8,128)(2,1)S(1)}, u32[]{:S(2)}, u32[]{:S(2)}) %collective-permute-start.5) | collective-permute-done | bytes 65568 | tf_op jit(solution)/shard_map/ppermute | solution.py:142
  68.5 0.7 fusion.9
  (1 shorter events, 0.0 us)
Async XLA Ops:
  3.7 21.7 %all-to-all-start = ((bf16[16,2,8,1024]{3,2,1,0:T(8,128)(2,1)}), bf16[16,2,8,1024]{3,2,1,0:T(8,128)(2,1)S(1)}, u32[]{:S(2)}, u32[]{:S(2)}) async-start(bf16[16,2,8,1024]{3,2,1,0:T(8,128)(2,1)} %outgoing.1), calls=%async_computation | async-start | bytes 1048576 | tf_op jit(solution)/shard_map/all_to_all | solution.py:153
  25.4 1.9 %copy-start = (bf16[2,3,2048,128]{3,2,1,0:T(8,128)(2,1)S(1)}, bf16[2,3,2048,128]{3,2,1,0:T(8,128)(2,1)}, u32[]{:S(2)}) copy-start(bf16[2,3,2048,128]{3,2,1,0:T(8,128)(2,1)} %weights_ref.1) | copy-start | bytes 9437188
  27.3 0.7 %copy-start.1 = (s32[16,128]{1,0:T(8,128)S(1)}, s32[16,128]{1,0:T(8,128)}, u32[]{:S(2)}) copy-start(s32[16,128]{1,0:T(8,128)} %param.10) | copy-start | bytes 24580
  28.0 0.7 copy-start.2
  41.0 2.7 %collective-permute-start = (bf16[2,2,4,128,256]{4,3,2,1,0:T(8,128)(2,1)S(1)}, bf16[2,2,4,128,256]{4,3,2,1,0:T(8,128)(2,1)S(1)}, u32[]{:S(2)}, u32[]{:S(2)}) collective-permute-start(bf16[2,2,4,128,256]{4,3,2,1,0:T(8,128)(2,1)S(1)} %get-tuple-element.8), channel_id=1, source_target_pairs={{0,2},{1,3},{2,0},{3,1},{4,6},{5,7},{6,4},{7,5},{8,10},{9,11},{10,... | collective-permute-start | bytes 3145736 | tf_op jit(solution)/shard_map/ppermute | solution.py:142
  43.8 14.0 %collective-permute-start.3 = (bf16[1,4,128,256]{3,2,1,0:T(8,128)(2,1)S(1)}, bf16[1,4,128,256]{3,2,1,0:T(8,128)(2,1)S(1)}, u32[]{:S(2)}, u32[]{:S(2)}) collective-permute-start(bf16[1,4,128,256]{3,2,1,0:T(8,128)(2,1)S(1)} %fusion.5), channel_id=1, source_target_pairs={{0,1},{1,0},{2,3},{3,2},{4,5},{5,4},{6,7},{7,6},{8,9},{9,8},{10,11... | collective-permute-start | bytes 786440 | tf_op jit(solution)/shard_map/ppermute | solution.py:142
  45.5 12.3 %collective-permute-start.1 = (bf16[1,4,128,256]{3,2,1,0:T(8,128)(2,1)S(1)}, bf16[1,4,128,256]{3,2,1,0:T(8,128)(2,1)S(1)}, u32[]{:S(2)}, u32[]{:S(2)}) collective-permute-start(bf16[1,4,128,256]{3,2,1,0:T(8,128)(2,1)S(1)} %get-tuple-element.11), channel_id=1, source_target_pairs={{0,5},{1,4},{2,7},{3,6},{4,1},{5,0},{6,3},{7,2},{8,13},{9,12},{10,... | collective-permute-start | bytes 786440 | tf_op jit(solution)/shard_map/ppermute | solution.py:142
  46.6 12.7 %collective-permute-start.2 = (bf16[1,4,128,256]{3,2,1,0:T(8,128)(2,1)S(1)}, bf16[1,4,128,256]{3,2,1,0:T(8,128)(2,1)S(1)}, u32[]{:S(2)}, u32[]{:S(2)}) collective-permute-start(bf16[1,4,128,256]{3,2,1,0:T(8,128)(2,1)S(1)} %get-tuple-element.12), channel_id=1, source_target_pairs={{0,4},{1,5},{2,6},{3,7},{4,0},{5,1},{6,2},{7,3},{8,12},{9,13},{10,... | collective-permute-start | bytes 786440 | tf_op jit(solution)/shard_map/ppermute | solution.py:142
  59.5 6.6 %collective-permute-start.4 = (bf16[1,128,256]{2,1,0:T(8,128)(2,1)S(1)}, bf16[1,128,256]{2,1,0:T(8,128)(2,1)S(1)}, u32[]{:S(2)}, u32[]{:S(2)}) collective-permute-start(bf16[1,128,256]{2,1,0:T(8,128)(2,1)S(1)} %get-tuple-element.13), channel_id=1, source_target_pairs={{0,24},{1,25},{2,26},{3,27},{4,28},{5,29},{6,30},{7,31},{8,16},{9,... | collective-permute-start | bytes 196616 | tf_op jit(solution)/shard_map/ppermute | solution.py:142
  61.6 4.9 %collective-permute-start.6 = (bf16[1,128,256]{2,1,0:T(8,128)(2,1)S(1)}, bf16[1,128,256]{2,1,0:T(8,128)(2,1)S(1)}, u32[]{:S(2)}, u32[]{:S(2)}) collective-permute-start(bf16[1,128,256]{2,1,0:T(8,128)(2,1)S(1)} %get-tuple-element.14), channel_id=1, source_target_pairs={{0,8},{1,9},{2,10},{3,11},{4,12},{5,13},{6,14},{7,15},{8,0},{9,1},... | collective-permute-start | bytes 196616 | tf_op jit(solution)/shard_map/ppermute | solution.py:142
  62.5 6.0 %collective-permute-start.5 = (bf16[1,128,256]{2,1,0:T(8,128)(2,1)S(1)}, bf16[1,128,256]{2,1,0:T(8,128)(2,1)S(1)}, u32[]{:S(2)}, u32[]{:S(2)}) collective-permute-start(bf16[1,128,256]{2,1,0:T(8,128)(2,1)S(1)} %get-tuple-element.15), channel_id=1, source_target_pairs={{0,16},{1,17},{2,18},{3,19},{4,20},{5,21},{6,22},{7,23},{8,24},{9,... | collective-permute-start | bytes 196616 | tf_op jit(solution)/shard_map/ppermute | solution.py:142

commit v2 on v1

v2 whole, which is shorter than its diff:
```python
import functools

import jax
import jax.numpy as jnp
from jax import lax
from jax.experimental import pallas as pl
from jax.experimental.pallas import tpu as pltpu
from jax.sharding import PartitionSpec as P

LANES = 128
AXES = ("cfd", "ac")
SMEM = pl.BlockSpec(memory_space=pltpu.SMEM)
VMEM = pl.BlockSpec(memory_space=pltpu.VMEM)


def pressure_kernel(high, me_ref, order_ref, surface_ref, *out_refs):
    for z in range(high):
        for q in range(4):
            out_refs[z][q] = surface_ref[0, order_ref[jnp.bitwise_xor(me_ref[0], 4 * z + q)]]


def pressure_out(me, order, surface, high):
    comps, blocks, rows, steps = surface.shape
    shape = jax.ShapeDtypeStruct((4, rows, steps), jnp.bfloat16)
    return pl.pallas_call(
        functools.partial(pressure_kernel, high),
        grid=(1,),
        out_shape=(shape,) * high,
        in_specs=[SMEM, SMEM, pl.BlockSpec((1, blocks, rows, steps), lambda i: (0, 0, 0, 0))],
        out_specs=(pl.BlockSpec((4, rows, steps), lambda i: (0, 0, 0)),) * high,
        compiler_params=pltpu.CompilerParams(vmem_limit_bytes=8 * 1024 * 1024),
        name="pressure_out",
    )(me, order, surface)


def thickness_kernel(high, me_ref, order_ref, surface_ref, normals_ref, *refs):
    out_refs, columns_ref = refs[:4], refs[4]
    rows = surface_ref.shape[2]
    normals = normals_ref[...].astype(jnp.float32)
    faces = normals.shape[1]
    square = jnp.concatenate([normals, jnp.zeros((faces - normals.shape[0], faces), jnp.float32)], axis=0)
    columns_ref[...] = jnp.transpose(square).reshape(columns_ref.shape)
    for q in range(4):
        for z in range(high):
            block = order_ref[jnp.bitwise_xor(me_ref[0], 4 * z + q)]
            normal = columns_ref[block]
            along = surface_ref[2, block].astype(jnp.float32) * normal[:, 0:1]
            along = along + surface_ref[3, block].astype(jnp.float32) * normal[:, 1:2]
            along = along + surface_ref[4, block].astype(jnp.float32) * normal[:, 2:3]
            out_refs[q][z] = (surface_ref[1, block].astype(jnp.float32) * along).astype(jnp.bfloat16)


def thickness_out(me, order, surface, normals, high):
    comps, blocks, rows, steps = surface.shape
    shape = jax.ShapeDtypeStruct((high, rows, steps), jnp.bfloat16)
    return pl.pallas_call(
        functools.partial(thickness_kernel, high),
        out_shape=(shape,) * 4,
        in_specs=[SMEM, SMEM, VMEM, VMEM],
        out_specs=(VMEM,) * 4,
        scratch_shapes=[pltpu.VMEM((blocks, rows, blocks * rows), jnp.float32)],
        compiler_params=pltpu.CompilerParams(vmem_limit_bytes=8 * 1024 * 1024),
        name="thickness_out",
    )(me, order, surface, normals)


def prepare_kernel(ranks, layout, me_ref, observers_ref, weights_ref, select_ref, joined_ref):
    taps, terms, observers, faces = weights_ref.shape
    for k in range(taps):
        for c in range(terms):
            at = (k * terms + c) * faces
            joined_ref[:, at : at + faces] = weights_ref[k, c]
    each = observers // ranks
    ids = observers_ref[...]
    local_row = lax.broadcasted_iota(jnp.int32, (each, observers), 0)
    for position, member in enumerate(layout):
        base = jnp.bitwise_xor(me_ref[0], member) * each
        chosen = jnp.where(local_row == ids - base, 1.0, 0.0).astype(jnp.bfloat16)
        select_ref[position * each : (position + 1) * each, :] = chosen


def prepare(me, observers, weights, ranks, layout):
    taps, terms, count, faces = weights.shape
    return pl.pallas_call(
        functools.partial(prepare_kernel, ranks, layout),
        out_shape=(
            jax.ShapeDtypeStruct((count, count), jnp.bfloat16),
            jax.ShapeDtypeStruct((count, taps * terms * faces), jnp.bfloat16),
        ),
        in_specs=[SMEM, VMEM, VMEM],
        out_specs=(VMEM, VMEM),
        cost_estimate=pl.CostEstimate(flops=4 * 10**9, bytes_accessed=weights.size * 4, transcendentals=0),
        compiler_params=pltpu.CompilerParams(vmem_limit_bytes=24 * 1024 * 1024),
        name="prepare",
    )(me, observers.reshape(1, -1), weights)


def order_rows(me_ref, select_ref, first_row, banded_ref, out_refs):
    rows = out_refs[0].shape[1]
    parts = out_refs[0].shape[0]
    piece = out_refs[0].shape[2]
    for c, out_ref in enumerate(out_refs):
        at = first_row + c * rows
        chosen = select_ref[at : at + rows, :]
        for y in range(parts):
            if parts == 1:
                data = banded_ref[...]
            else:
                column = pl.multiple_of(jnp.bitwise_xor(me_ref[1], y) * piece, piece)
                data = banded_ref[:, pl.ds(column, piece)]
            out_ref[y] = jnp.dot(chosen, data, preferred_element_type=jnp.float32).astype(jnp.bfloat16)


def place_blocks(me_ref, series_ref, blocks):
    for distance, value in blocks:
        rows = value.shape[0]
        source = jnp.bitwise_xor(me_ref[0], distance)
        value = value.astype(jnp.float32)
        if rows % 8 == 0:
            series_ref[pl.ds(pl.multiple_of(source * rows, 8), rows), :] = value
        else:
            for r in range(rows):
                series_ref[pl.ds(source * rows + r, 1), :] = value[r : r + 1]


def bands_kernel(taps, high, me_ref, lags_ref, joined_ref, select_ref, *refs):
    pressure_refs, refs = refs[: high + 3], refs[high + 3 :]
    thick_refs, refs = refs[: high + 3], refs[high + 3 :]
    banded_ref, keep_ref, send_ref, stacked_ref, series_ref = refs
    faces, steps = series_ref.shape
    terms = joined_ref.shape[1] // faces // taps
    span = stacked_ref.shape[1]
    observers, out_len = banded_ref.shape
    bands = lags_ref.shape[0]
    width = observers // bands
    wide = out_len + LANES
    pairs = [(z, q) for z in range(high) for q in range(4)]
    thick = [(4 * z + q, thick_refs[3 + z][q] if z else thick_refs[q][0]) for z, q in pairs]
    pressure = [(4 * z + q, pressure_refs[high - 1 + q][z] if q else pressure_refs[z][0]) for z, q in pairs]
    pad = jnp.zeros((faces, span - steps), jnp.bfloat16)
    for kind, blocks in enumerate((thick, pressure)):
        place_blocks(me_ref, series_ref, blocks)
        series = series_ref[...]
        earlier = pltpu.roll(series, 1, 1)
        first = lax.broadcasted_iota(jnp.int32, series.shape, 1) == 0
        rate = jnp.where(first, 0.0, series - earlier)
        made = [(kind, rate)] if kind == 0 else [(1, rate), (2, series)]
        for term, value in made:
            for tap in range(taps):
                moved = pltpu.roll(value, tap, 1) if tap else value
                at = (tap * terms + term) * faces
                stacked_ref[at : at + faces, 0:steps] = moved.astype(jnp.bfloat16)
                stacked_ref[at : at + faces, steps:span] = pad

    def one_band(b, carry):
        start = out_len - lags_ref[b]
        column = pl.multiple_of((start // LANES) * LANES, LANES)
        rest = start % LANES
        at = pl.ds(pl.multiple_of(b * width, width), width)
        full = jnp.dot(joined_ref[at, :], stacked_ref[:, pl.ds(column, wide)], preferred_element_type=jnp.float32)
        turned = pltpu.roll(full, (wide - rest) % wide, 1)
        banded_ref[at, :] = turned[:, :out_len].astype(jnp.bfloat16)
        return carry

    lax.fori_loop(0, bands, one_band, 0, unroll=4)
    order_rows(me_ref, select_ref, 0, banded_ref, (keep_ref, send_ref))


def bands(me, lags, pressure, thick, joined, select, taps, parts, rows):
    count = joined.shape[0]
    steps = thick[0].shape[2]
    out_len = steps // 2
    high = len(thick) - 3
    faces = 4 * high * thick[0].shape[1]
    shape = jax.ShapeDtypeStruct((parts, rows, out_len // parts), jnp.bfloat16)
    return pl.pallas_call(
        functools.partial(bands_kernel, taps, high),
        out_shape=(jax.ShapeDtypeStruct((count, out_len), jnp.bfloat16), shape, shape),
        in_specs=[SMEM, SMEM, VMEM, VMEM] + [VMEM] * (2 * (high + 3)),
        out_specs=(VMEM, VMEM, VMEM),
        scratch_shapes=[
            pltpu.VMEM((joined.shape[1], steps + LANES), jnp.bfloat16),
            pltpu.VMEM((faces, steps), jnp.float32),
        ],
        cost_estimate=pl.CostEstimate(flops=4 * 10**9, bytes_accessed=10**7, transcendentals=0),
        compiler_params=pltpu.CompilerParams(vmem_limit_bytes=24 * 1024 * 1024),
        name="bands",
    )(me, lags, joined, select, *pressure, *thick)


def order_kernel(first_row, me_ref, banded_ref, select_ref, keep_ref, send_ref):
    order_rows(me_ref, select_ref, first_row, banded_ref, (keep_ref, send_ref))


def order_more(me, banded, select, first_row, parts, rows):
    shape = jax.ShapeDtypeStruct((parts, rows, banded.shape[1] // parts), jnp.bfloat16)
    return pl.pallas_call(
        functools.partial(order_kernel, first_row),
        out_shape=(shape, shape),
        in_specs=[SMEM, VMEM, VMEM],
        out_specs=(VMEM, VMEM),
        cost_estimate=pl.CostEstimate(flops=2 * 10**9, bytes_accessed=10**7, transcendentals=0),
        compiler_params=pltpu.CompilerParams(vmem_limit_bytes=24 * 1024 * 1024),
        name="order",
    )(me, banded, select)


def swap(value, ranks, sides, rank_mask, side_mask):
    pairs = [
        (r * sides + s, (r ^ rank_mask) * sides + (s ^ side_mask)) for r in range(ranks) for s in range(sides)
    ]
    return lax.ppermute(value, AXES, pairs)


def local(surface_raw, area_normals, kernel_weights, block_map, band_observers, band_lags):
    ranks = lax.axis_size("cfd")
    sides = lax.axis_size("ac")
    me = jnp.stack([lax.axis_index("cfd"), lax.axis_index("ac")]).astype(jnp.int32)
    order = block_map[0, 0]
    high = ranks // 4
    comps, faces, steps = surface_raw.shape
    surface = surface_raw.reshape(comps, ranks, faces // ranks, steps)
    pressure = list(pressure_out(me, order, surface, high))
    thick = list(thickness_out(me, order, surface, area_normals, high))
    for z in range(high - 1, 0, -1):
        pressure[z] = swap(pressure[z], ranks, sides, 4 * z, 0)
    for q in range(3, 0, -1):
        thick[q] = swap(thick[q], ranks, sides, q, 0)
    for q in range(1, 4):
        pressure.append(swap(jnp.stack([pressure[z][q] for z in range(high)]), ranks, sides, q, 0))
    onward = [swap(jnp.stack([thick[q][z] for q in range(4)]), ranks, sides, 4 * z, 0) for z in range(high - 1, 0, -1)]
    thick.extend(reversed(onward))
    taps, _, count_rows, _ = kernel_weights.shape
    out_len = surface_raw.shape[2] // 2
    each = count_rows // ranks
    rest = ranks // 4
    near = rest // 2
    chunks = (range(near, rest), range(near))
    layout = [(z * 2 + x) * 2 + c for zs in chunks for c in range(2) for x in range(2) for z in zs]
    parts = sides if out_len // sides % LANES == 0 else 1
    rows = near * 2 * each
    select, joined = prepare(me, band_observers, kernel_weights, ranks, layout)
    banded, *far = bands(me, band_lags, pressure, thick, joined, select, taps, parts, rows)
    which = jnp.bitwise_xor(lax.iota(jnp.int32, sides), me[1])

    def by_side(value):
        if parts != sides:
            value = value.reshape(rows, sides, out_len // sides)
            value = jnp.transpose(jnp.take(value, which, axis=1), (1, 0, 2))
        return value.reshape(sides // 2, 2, 2, near, each, out_len // sides)

    def exchange(keep, send):
        got = by_side(swap(send, ranks, sides, 1, 0))
        keep = by_side(keep)

        def first(x, y):
            return keep[:, y, x].astype(jnp.float32) + got[:, y, x].astype(jnp.float32)

        total = first(0, 0)
        for x, y in [(1, 1), (1, 0), (0, 1)]:
            total = total + swap(first(x, y).astype(jnp.bfloat16), ranks, sides, 2 * x, y).astype(jnp.float32)
        return total

    def over_z(result, total, zs):
        for z in reversed(zs):
            moved = total[:, z - zs[0]]
            if z:
                moved = swap(moved.astype(jnp.bfloat16), ranks, sides, 4 * z, 0).astype(jnp.float32)
            result = moved if result is None else result + moved
        return result

    result = over_z(None, exchange(*far), chunks[0])
    result = over_z(result, exchange(*order_more(me, banded, select, 2 * rows, parts, rows)), chunks[1])
    out = result[0]
    for y in range(sides // 2 - 1, 0, -1):
        out = out + swap(result[y].astype(jnp.bfloat16), ranks, sides, 0, 2 * y).astype(jnp.float32)
    return out


def solution(mesh):
    placed = (
        P(None, ("cfd", "ac"), None),
        P(None, ("cfd", "ac")),
        P(None, None, None, ("cfd", "ac")),
        P("ac", "cfd", None),
        P(),
        P(),
    )
    return jax.shard_map(
        local, mesh=mesh, in_specs=placed, out_specs=P("cfd", "ac"), check_vma=False
    )
```

time: 69.5 us -> 57.5 us (0.83)
  waiting for transfers between devices: 33 us -> 8 us
  starting transfers between devices: 15.7 us -> 31.1 us
  other arithmetic: 2.4 us -> 1.21 us
  Pallas kernels: 14.8 us -> 14.1 us
    ppermute x7 -> x23, starting transfers between devices: 8.28 us -> 31.1 us  [swap(): return lax.ppermute(value, AXES, pairs)]
    all_to_all x1 -> x0, waiting for transfers between devices: 14.2 us -> none  [local(): lax.all_to_all(sent, 'cfd', split_axis=0, concat_axis=0, tiled=True)]
    ppermute x7 -> x23, waiting for transfers between devices: 18.8 us -> 8 us  [swap(): return lax.ppermute(value, AXES, pairs)]
    all_to_all x1 -> x0, starting transfers between devices: 7.39 us -> none  [local(): lax.all_to_all(sent, 'cfd', split_axis=0, concat_axis=0, tiled=True)]
    reduce_sum x1 -> x0, other arithmetic: 1.28 us -> none  [local(): jnp.sum(jnp.where(order[None, :] == count[:, None], count[None, :], 0), a...]
    pallas_call x2 -> x5, Pallas kernels: 14.8 us -> 14.1 us  [the longest x1 7.25 us: bands(): pl.pallas_call(functools.partial(bands_kernel, taps, high), out_shape=(ja...]
    unnamed x6 -> x12, local copies, waits for them, and re-layouts: 3.24 us -> 2.66 us
  transfers between devices with their start and end apart: 8 -> 23, of which waited for: 7 -> 6; matrix products, arithmetic and copies ran while one was open for 0% -> 1% of each run, Pallas kernels for 0% -> 10%
where the time goes in v2:
time: 57.5 us; the launch traced here: 57.3 us
  starting transfers between devices  31.1 us (54%)
  Pallas kernels  14.1 us (25%)
  waiting for transfers between devices  8 us (14%)
  local copies, waits for them, and re-layouts  2.72 us (5%)
  other arithmetic  1.21 us (2%)
    ppermute x23, starting transfers between devices, swap(): return lax.ppermute(value, AXES, pairs)  31.1 us
    ppermute x23, waiting for transfers between devices, swap(): return lax.ppermute(value, AXES, pairs)  8 us
    pallas_call x1, Pallas kernels, bands(): pl.pallas_call(functools.partial(bands_kernel, taps, high), out_shape=(ja...  7.25 us
    pallas_call x1, Pallas kernels, order_more(): pl.pallas_call(functools.partial(order_kernel, first_row), out_shape=(sha...  2.87 us
    unnamed x12, local copies, waits for them, and re-layouts  2.66 us
    pallas_call x1, Pallas kernels, prepare(): pl.pallas_call(functools.partial(prepare_kernel, ranks, layout), out_shap...  2.49 us
  transfers between devices with their start and end apart: 23, of which 6 were waited for; matrix products, arithmetic and copies ran while one was open for 1% of the time, Pallas kernels for 10%

profile of v2, /device:TPU:0, one launch (start us, length us, event | category | flops | bytes accessed | tf_op | source)
XLA Modules:
  0.0 57.3 jit_solution(3453451567923228012)
XLA Ops:
  0.1 1.3 %copy-done = bf16[5,128,1024]{2,1,0:T(8,128)(2,1)S(1)} copy-done((bf16[5,128,1024]{2,1,0:T(8,128)(2,1)S(1)}, bf16[5,128,1024]{2,1,0:T(8,128)(2,1)}, u32[]{:S(2)}) %copy-start) | copy-done | bytes 1310744
  1.4 0.7 %copy-done.1 = s32[1,1,16]{2,1,0:T(1,128)S(1)} copy-done((s32[1,1,16]{2,1,0:T(1,128)S(1)}, s32[1,1,16]{2,1,0:T(1,128)}, u32[]{:S(2)}) %copy-start.1) | copy-done | bytes 88
  2.1 0.7 %copy-done.2 = bf16[3,128]{1,0:T(4,128)(2,1)S(1)} copy-done((bf16[3,128]{1,0:T(4,128)(2,1)S(1)}, bf16[3,128]{1,0:T(4,128)(2,1)}, u32[]{:S(2)}) %copy-start.2) | copy-done | bytes 792
  2.7 0.9 %thickness_out.1 = (bf16[4,8,1024]{2,1,0:T(8,128)(2,1)S(1)}, bf16[4,8,1024]{2,1,0:T(8,128)(2,1)S(1)}, bf16[4,8,1024]{2,1,0:T(8,128)(2,1)S(1)}, bf16[4,8,1024]{2,1,0:T(8,128)(2,1)S(1)}) custom-call(s32[2]{0:T(128)S(1)} %pad_add_fusion.me_ref, s32[16]{0:T(128)S(1)} %bitcast.55, bf16[5,16,8,1024]{3,2,1,0:T(8,128)(2,1)S(1)} %bitcast.49, bf16[3,128]{1,0:T(4,128)(2,1)S(1)} %copy-done.2), custom_call_target="tpu_custom_call" | custom-call | tf_op jit(solution)/shard_map/thickness_out/pallas_call | solution.py:56
  3.6 0.6 collective-permute-start.6
  4.2 2.6 %collective-permute-start.7 = (bf16[4,8,1024]{2,1,0:T(8,128)(2,1)S(1)}, bf16[4,8,1024]{2,1,0:T(8,128)(2,1)S(1)}, u32[]{:S(2)}, u32[]{:S(2)}) collective-permute-start(bf16[4,8,1024]{2,1,0:T(8,128)(2,1)S(1)} %get-tuple-element.28), channel_id=1, source_target_pairs={{0,4},{1,5},{2,6},{3,7},{4,0},{5,1},{6,2},{7,3},{8,12},{9,13},{10,... | collective-permute-start | bytes 196616 | tf_op jit(solution)/shard_map/ppermute | solution.py:212
  6.8 0.6 pressure_out.1
  7.4 1.9 %collective-permute-start = (bf16[4,8,1024]{2,1,0:T(8,128)(2,1)S(1)}, bf16[4,8,1024]{2,1,0:T(8,128)(2,1)S(1)}, u32[]{:S(2)}, u32[]{:S(2)}) collective-permute-start(bf16[4,8,1024]{2,1,0:T(8,128)(2,1)S(1)} %get-tuple-element.23), channel_id=1, source_target_pairs={{0,8},{1,9},{2,10},{3,11},{4,12},{5,13},{6,14},{7,15},{8,0},{9,1},... | collective-permute-start | bytes 196616 | tf_op jit(solution)/shard_map/ppermute | solution.py:212
  9.3 2.6 %collective-permute-start.1 = (bf16[4,8,1024]{2,1,0:T(8,128)(2,1)S(1)}, bf16[4,8,1024]{2,1,0:T(8,128)(2,1)S(1)}, u32[]{:S(2)}, u32[]{:S(2)}) collective-permute-start(bf16[4,8,1024]{2,1,0:T(8,128)(2,1)S(1)} %get-tuple-element.24), channel_id=1, source_target_pairs={{0,16},{1,17},{2,18},{3,19},{4,20},{5,21},{6,22},{7,23},{8,24},{9,... | collective-permute-start | bytes 196616 | tf_op jit(solution)/shard_map/ppermute | solution.py:212
  12.0 0.9 %collective-permute-start.9 = (bf16[4,8,1024]{2,1,0:T(8,128)(2,1)S(1)}, bf16[4,8,1024]{2,1,0:T(8,128)(2,1)S(1)}, u32[]{:S(2)}, u32[]{:S(2)}) collective-permute-start(bf16[4,8,1024]{2,1,0:T(8,128)(2,1)S(1)} %pad_maximum_fusion.3), channel_id=1, source_target_pairs={{0,8},{1,9},{2,10},{3,11},{4,12},{5,13},{6,14},{7,15},{8,0},{9,1},... | collective-permute-start | bytes 196616 | tf_op jit(solution)/shard_map/ppermute | solution.py:212
  13.0 3.6 %collective-permute-start.10 = (bf16[4,8,1024]{2,1,0:T(8,128)(2,1)S(1)}, bf16[4,8,1024]{2,1,0:T(8,128)(2,1)S(1)}, u32[]{:S(2)}, u32[]{:S(2)}) collective-permute-start(bf16[4,8,1024]{2,1,0:T(8,128)(2,1)S(1)} %pad_maximum_fusion.4), channel_id=1, source_target_pairs={{0,16},{1,17},{2,18},{3,19},{4,20},{5,21},{6,22},{7,23},{8,24},{9,... | collective-permute-start | bytes 196616 | tf_op jit(solution)/shard_map/ppermute | solution.py:212
  16.7 2.0 %collective-permute-done.2.refs_3_ = bf16[4,8,1024]{2,1,0:T(8,128)(2,1)S(1)} collective-permute-done((bf16[4,8,1024]{2,1,0:T(8,128)(2,1)S(1)}, bf16[4,8,1024]{2,1,0:T(8,128)(2,1)S(1)}, u32[]{:S(2)}, u32[]{:S(2)}) %collective-permute-start.2) | collective-permute-done | bytes 65568 | tf_op jit(solution)/shard_map/ppermute | solution.py:212
  18.8 1.6 %collective-permute-start.4 = (bf16[4,8,1024]{2,1,0:T(8,128)(2,1)S(1)}, bf16[4,8,1024]{2,1,0:T(8,128)(2,1)S(1)}, u32[]{:S(2)}, u32[]{:S(2)}) collective-permute-start(bf16[4,8,1024]{2,1,0:T(8,128)(2,1)S(1)} %pad_maximum_fusion.1), channel_id=1, source_target_pairs={{0,4},{1,5},{2,6},{3,7},{4,0},{5,1},{6,2},{7,3},{8,12},{9,13},{10,... | collective-permute-start | bytes 196616 | tf_op jit(solution)/shard_map/ppermute | solution.py:212
  20.4 0.4 collective-permute-start.5
  20.8 2.5 %prepare.1 = (bf16[2048,2048]{1,0:T(8,128)(2,1)S(1)}, bf16[2048,768]{1,0:T(8,128)(2,1)S(1)}) custom-call(s32[2]{0:T(128)S(1)} %pad_add_fusion.me_ref, s32[1,2048]{1,0:T(1,128)S(1)} %bitcast.57, bf16[2,3,2048,128]{3,2,1,0:T(8,128)(2,1)S(1)} %copy-done.3), custom_call_target="tpu_custom_call" | custom-call | flops 4000000000 | bytes 6291456 | tf_op jit(solution)/shard_map/prepare/pallas_call | solution.py:84
  23.4 1.1 %collective-permute-done.5.refs_6_ = bf16[4,8,1024]{2,1,0:T(8,128)(2,1)S(1)} collective-permute-done((bf16[4,8,1024]{2,1,0:T(8,128)(2,1)S(1)}, bf16[4,8,1024]{2,1,0:T(8,128)(2,1)S(1)}, u32[]{:S(2)}, u32[]{:S(2)}) %collective-permute-start.5) | collective-permute-done | bytes 65568 | tf_op jit(solution)/shard_map/ppermute | solution.py:212
  24.5 7.3 %bands.1 = (bf16[2048,512]{1,0:T(8,128)(2,1)S(1)}, bf16[2,512,256]{2,1,0:T(8,128)(2,1)S(1)}, bf16[2,512,256]{2,1,0:T(8,128)(2,1)S(1)}) custom-call(s32[2]{0:T(128)S(1)} %pad_add_fusion.me_ref, s32[16]{0:T(128)S(1)} %copy-done.5, bf16[2048,768]{1,0:T(8,128)(2,1)S(1)} %get-tuple-element.20.joined_ref, bf16[2048,2048]{1,0:T(8,128)(2,1)S(1)} %get-tuple-element.21.select_ref, ...), custom_call_target="tpu_custom_call" | custom-call | flops 4000000000 | bytes 10000000 | tf_op jit(solution)/shard_map/bands/pallas_call | solution.py:176
  32.0 2.9 %order.1 = (bf16[2,512,256]{2,1,0:T(8,128)(2,1)S(1)}, bf16[2,512,256]{2,1,0:T(8,128)(2,1)S(1)}) custom-call(s32[2]{0:T(128)S(1)} %pad_add_fusion.me_ref, bf16[2048,512]{1,0:T(8,128)(2,1)S(1)} %get-tuple-element.32.banded_ref, bf16[2048,2048]{1,0:T(8,128)(2,1)S(1)} %get-tuple-element.21.select_ref), custom_call_target="tpu_custom_call" | custom-call | flops 2000000000 | bytes 10000000 | tf_op jit(solution)/shard_map/order/pallas_call | solution.py:197
  35.4 2.4 %collective-permute-start.13 = (bf16[1,2,128,256]{3,2,1,0:T(8,128)(2,1)S(1)}, bf16[1,2,128,256]{3,2,1,0:T(8,128)(2,1)S(1)}, u32[]{:S(2)}, u32[]{:S(2)}) collective-permute-start(bf16[1,2,128,256]{3,2,1,0:T(8,128)(2,1)S(1)} %get-tuple-element.35), channel_id=1, source_target_pairs={{0,5},{1,4},{2,7},{3,6},{4,1},{5,0},{6,3},{7,2},{8,13},{9,12},{10,... | collective-permute-start | bytes 393224 | tf_op jit(solution)/shard_map/ppermute | solution.py:212
  37.8 0.5 collective-permute-start.15
  38.2 0.7 %collective-permute-start.14 = (bf16[1,2,128,256]{3,2,1,0:T(8,128)(2,1)S(1)}, bf16[1,2,128,256]{3,2,1,0:T(8,128)(2,1)S(1)}, u32[]{:S(2)}, u32[]{:S(2)}) collective-permute-start(bf16[1,2,128,256]{3,2,1,0:T(8,128)(2,1)S(1)} %get-tuple-element.37), channel_id=1, source_target_pairs={{0,4},{1,5},{2,6},{3,7},{4,0},{5,1},{6,2},{7,3},{8,12},{9,13},{10,... | collective-permute-start | bytes 393224 | tf_op jit(solution)/shard_map/ppermute | solution.py:212
  39.0 2.4 %collective-permute-start.19 = (bf16[1,2,128,256]{3,2,1,0:T(8,128)(2,1)S(1)}, bf16[1,2,128,256]{3,2,1,0:T(8,128)(2,1)S(1)}, u32[]{:S(2)}, u32[]{:S(2)}) collective-permute-start(bf16[1,2,128,256]{3,2,1,0:T(8,128)(2,1)S(1)} %get-tuple-element.38), channel_id=1, source_target_pairs={{0,5},{1,4},{2,7},{3,6},{4,1},{5,0},{6,3},{7,2},{8,13},{9,12},{10,... | collective-permute-start | bytes 393224 | tf_op jit(solution)/shard_map/ppermute | solution.py:212
  41.4 0.5 collective-permute-start.21
  41.9 0.4 collective-permute-done.13
  42.3 1.7 %collective-permute-start.20 = (bf16[1,2,128,256]{3,2,1,0:T(8,128)(2,1)S(1)}, bf16[1,2,128,256]{3,2,1,0:T(8,128)(2,1)S(1)}, u32[]{:S(2)}, u32[]{:S(2)}) collective-permute-start(bf16[1,2,128,256]{3,2,1,0:T(8,128)(2,1)S(1)} %get-tuple-element.40), channel_id=1, source_target_pairs={{0,4},{1,5},{2,6},{3,7},{4,0},{5,1},{6,2},{7,3},{8,12},{9,13},{10,... | collective-permute-start | bytes 393224 | tf_op jit(solution)/shard_map/ppermute | solution.py:212
  44.1 1.6 %collective-permute-done.15 = bf16[1,2,128,256]{3,2,1,0:T(8,128)(2,1)S(1)} collective-permute-done((bf16[1,2,128,256]{3,2,1,0:T(8,128)(2,1)S(1)}, bf16[1,2,128,256]{3,2,1,0:T(8,128)(2,1)S(1)}, u32[]{:S(2)}, u32[]{:S(2)}) %collective-permute-start.15) | collective-permute-done | bytes 131104 | tf_op jit(solution)/shard_map/ppermute | solution.py:212
  45.8 2.0 %collective-permute-start.16 = (bf16[1,128,256]{2,1,0:T(8,128)(2,1)S(1)}, bf16[1,128,256]{2,1,0:T(8,128)(2,1)S(1)}, u32[]{:S(2)}, u32[]{:S(2)}) collective-permute-start(bf16[1,128,256]{2,1,0:T(8,128)(2,1)S(1)} %get-tuple-element.41), channel_id=1, source_target_pairs={{0,24},{1,25},{2,26},{3,27},{4,28},{5,29},{6,30},{7,31},{8,16},{9,... | collective-permute-start | bytes 196616 | tf_op jit(solution)/shard_map/ppermute | solution.py:212
  47.8 3.1 %collective-permute-start.17 = (bf16[1,128,256]{2,1,0:T(8,128)(2,1)S(1)}, bf16[1,128,256]{2,1,0:T(8,128)(2,1)S(1)}, u32[]{:S(2)}, u32[]{:S(2)}) collective-permute-start(bf16[1,128,256]{2,1,0:T(8,128)(2,1)S(1)} %get-tuple-element.42), channel_id=1, source_target_pairs={{0,16},{1,17},{2,18},{3,19},{4,20},{5,21},{6,22},{7,23},{8,24},{9,... | collective-permute-start | bytes 196616 | tf_op jit(solution)/shard_map/ppermute | solution.py:212
  51.1 2.8 %collective-permute-start.22 = (bf16[1,128,256]{2,1,0:T(8,128)(2,1)S(1)}, bf16[1,128,256]{2,1,0:T(8,128)(2,1)S(1)}, u32[]{:S(2)}, u32[]{:S(2)}) collective-permute-start(bf16[1,128,256]{2,1,0:T(8,128)(2,1)S(1)} %fusion.13), channel_id=1, source_target_pairs={{0,8},{1,9},{2,10},{3,11},{4,12},{5,13},{6,14},{7,15},{8,0},{9,1},... | collective-permute-start | bytes 196616 | tf_op jit(solution)/shard_map/ppermute | solution.py:212
  53.9 1.7 %collective-permute-done.17 = bf16[1,128,256]{2,1,0:T(8,128)(2,1)S(1)} collective-permute-done((bf16[1,128,256]{2,1,0:T(8,128)(2,1)S(1)}, bf16[1,128,256]{2,1,0:T(8,128)(2,1)S(1)}, u32[]{:S(2)}, u32[]{:S(2)}) %collective-permute-start.17) | collective-permute-done | bytes 65568 | tf_op jit(solution)/shard_map/ppermute | solution.py:212
  55.5 1.1 %collective-permute-done.22 = bf16[1,128,256]{2,1,0:T(8,128)(2,1)S(1)} collective-permute-done((bf16[1,128,256]{2,1,0:T(8,128)(2,1)S(1)}, bf16[1,128,256]{2,1,0:T(8,128)(2,1)S(1)}, u32[]{:S(2)}, u32[]{:S(2)}) %collective-permute-start.22) | collective-permute-done | bytes 65568 | tf_op jit(solution)/shard_map/ppermute | solution.py:212
  56.6 0.7 %fusion.12 = f32[128,256]{1,0:T(8,128)} fusion(f32[1,2,128,256]{3,2,1,0:T(8,128)S(1)} %fusion.1, bf16[1,128,256]{2,1,0:T(8,128)(2,1)S(1)} %collective-permute-done.22, bf16[1,128,256]{2,1,0:T(8,128)(2,1)S(1)} %collective-permute-done.17, bf16[1,128,256]{2,1,0:T(8,128)(2,1)S(1)} %collective-permute-done.16), kind=kLoop, calls=%fused_computation.21 | loop fusion | flops 196608 | bytes 458752 | tf_op jit(solution)/shard_map/squeeze | solution.py:274
  (53 shorter events, 1.6 us)
Async XLA Ops:
  0.0 20.8 %copy-start.4 = (s32[16,128]{1,0:T(8,128)S(1)}, s32[16,128]{1,0:T(8,128)}, u32[]{:S(2)}) copy-start(s32[16,128]{1,0:T(8,128)} %param.10) | copy-start | bytes 24580
  0.1 1.3 %copy-start = (bf16[5,128,1024]{2,1,0:T(8,128)(2,1)S(1)}, bf16[5,128,1024]{2,1,0:T(8,128)(2,1)}, u32[]{:S(2)}) copy-start(bf16[5,128,1024]{2,1,0:T(8,128)(2,1)} %param.6) | copy-start | bytes 3932164
  1.4 0.7 %copy-start.1 = (s32[1,1,16]{2,1,0:T(1,128)S(1)}, s32[1,1,16]{2,1,0:T(1,128)}, u32[]{:S(2)}) copy-start(s32[1,1,16]{2,1,0:T(1,128)} %param.9) | copy-start | bytes 196
  2.1 0.7 %copy-start.2 = (bf16[3,128]{1,0:T(4,128)(2,1)S(1)}, bf16[3,128]{1,0:T(4,128)(2,1)}, u32[]{:S(2)}) copy-start(bf16[3,128]{1,0:T(4,128)(2,1)} %normals_ref.1) | copy-start | bytes 2308
  2.7 18.1 %copy-start.3 = (bf16[2,3,2048,128]{3,2,1,0:T(8,128)(2,1)S(1)}, bf16[2,3,2048,128]{3,2,1,0:T(8,128)(2,1)}, u32[]{:S(2)}) copy-start(bf16[2,3,2048,128]{3,2,1,0:T(8,128)(2,1)} %weights_ref.1) | copy-start | bytes 9437188
  3.6 8.2 %collective-permute-start.6 = (bf16[4,8,1024]{2,1,0:T(8,128)(2,1)S(1)}, bf16[4,8,1024]{2,1,0:T(8,128)(2,1)S(1)}, u32[]{:S(2)}, u32[]{:S(2)}) collective-permute-start(bf16[4,8,1024]{2,1,0:T(8,128)(2,1)S(1)} %get-tuple-element.27), channel_id=1, source_target_pairs={{0,2},{1,3},{2,0},{3,1},{4,6},{5,7},{6,4},{7,5},{8,10},{9,11},{10,... | collective-permute-start | bytes 196616 | tf_op jit(solution)/shard_map/ppermute | solution.py:212
  4.2 7.8 %collective-permute-start.7 = (bf16[4,8,1024]{2,1,0:T(8,128)(2,1)S(1)}, bf16[4,8,1024]{2,1,0:T(8,128)(2,1)S(1)}, u32[]{:S(2)}, u32[]{:S(2)}) collective-permute-start(bf16[4,8,1024]{2,1,0:T(8,128)(2,1)S(1)} %get-tuple-element.28), channel_id=1, source_target_pairs={{0,4},{1,5},{2,6},{3,7},{4,0},{5,1},{6,2},{7,3},{8,12},{9,13},{10,... | collective-permute-start | bytes 196616 | tf_op jit(solution)/shard_map/ppermute | solution.py:212
  6.7 5.2 %collective-permute-start.8 = (bf16[4,8,1024]{2,1,0:T(8,128)(2,1)S(1)}, bf16[4,8,1024]{2,1,0:T(8,128)(2,1)S(1)}, u32[]{:S(2)}, u32[]{:S(2)}) collective-permute-start(bf16[4,8,1024]{2,1,0:T(8,128)(2,1)S(1)} %get-tuple-element.29), channel_id=1, source_target_pairs={{0,6},{1,7},{2,4},{3,5},{4,2},{5,3},{6,0},{7,1},{8,14},{9,15},{10,... | collective-permute-start | bytes 196616 | tf_op jit(solution)/shard_map/ppermute | solution.py:212
  7.4 9.2 %collective-permute-start = (bf16[4,8,1024]{2,1,0:T(8,128)(2,1)S(1)}, bf16[4,8,1024]{2,1,0:T(8,128)(2,1)S(1)}, u32[]{:S(2)}, u32[]{:S(2)}) collective-permute-start(bf16[4,8,1024]{2,1,0:T(8,128)(2,1)S(1)} %get-tuple-element.23), channel_id=1, source_target_pairs={{0,8},{1,9},{2,10},{3,11},{4,12},{5,13},{6,14},{7,15},{8,0},{9,1},... | collective-permute-start | bytes 196616 | tf_op jit(solution)/shard_map/ppermute | solution.py:212
  9.3 7.4 %collective-permute-start.1 = (bf16[4,8,1024]{2,1,0:T(8,128)(2,1)S(1)}, bf16[4,8,1024]{2,1,0:T(8,128)(2,1)S(1)}, u32[]{:S(2)}, u32[]{:S(2)}) collective-permute-start(bf16[4,8,1024]{2,1,0:T(8,128)(2,1)S(1)} %get-tuple-element.24), channel_id=1, source_target_pairs={{0,16},{1,17},{2,18},{3,19},{4,20},{5,21},{6,22},{7,23},{8,24},{9,... | collective-permute-start | bytes 196616 | tf_op jit(solution)/shard_map/ppermute | solution.py:212
  11.9 6.8 %collective-permute-start.2 = (bf16[4,8,1024]{2,1,0:T(8,128)(2,1)S(1)}, bf16[4,8,1024]{2,1,0:T(8,128)(2,1)S(1)}, u32[]{:S(2)}, u32[]{:S(2)}) collective-permute-start(bf16[4,8,1024]{2,1,0:T(8,128)(2,1)S(1)} %get-tuple-element.25), channel_id=1, source_target_pairs={{0,24},{1,25},{2,26},{3,27},{4,28},{5,29},{6,30},{7,31},{8,16},{9,... | collective-permute-start | bytes 196616 | tf_op jit(solution)/shard_map/ppermute | solution.py:212
  12.0 8.4 %collective-permute-start.9 = (bf16[4,8,1024]{2,1,0:T(8,128)(2,1)S(1)}, bf16[4,8,1024]{2,1,0:T(8,128)(2,1)S(1)}, u32[]{:S(2)}, u32[]{:S(2)}) collective-permute-start(bf16[4,8,1024]{2,1,0:T(8,128)(2,1)S(1)} %pad_maximum_fusion.3), channel_id=1, source_target_pairs={{0,8},{1,9},{2,10},{3,11},{4,12},{5,13},{6,14},{7,15},{8,0},{9,1},... | collective-permute-start | bytes 196616 | tf_op jit(solution)/shard_map/ppermute | solution.py:212
  13.0 10.3 %collective-permute-start.10 = (bf16[4,8,1024]{2,1,0:T(8,128)(2,1)S(1)}, bf16[4,8,1024]{2,1,0:T(8,128)(2,1)S(1)}, u32[]{:S(2)}, u32[]{:S(2)}) collective-permute-start(bf16[4,8,1024]{2,1,0:T(8,128)(2,1)S(1)} %pad_maximum_fusion.4), channel_id=1, source_target_pairs={{0,16},{1,17},{2,18},{3,19},{4,20},{5,21},{6,22},{7,23},{8,24},{9,... | collective-permute-start | bytes 196616 | tf_op jit(solution)/shard_map/ppermute | solution.py:212
  16.6 6.8 %collective-permute-start.11 = (bf16[4,8,1024]{2,1,0:T(8,128)(2,1)S(1)}, bf16[4,8,1024]{2,1,0:T(8,128)(2,1)S(1)}, u32[]{:S(2)}, u32[]{:S(2)}) collective-permute-start(bf16[4,8,1024]{2,1,0:T(8,128)(2,1)S(1)} %pad_maximum_fusion.5), channel_id=1, source_target_pairs={{0,24},{1,25},{2,26},{3,27},{4,28},{5,29},{6,30},{7,31},{8,16},{9,... | collective-permute-start | bytes 196616 | tf_op jit(solution)/shard_map/ppermute | solution.py:212
  18.7 4.6 %collective-permute-start.3 = (bf16[4,8,1024]{2,1,0:T(8,128)(2,1)S(1)}, bf16[4,8,1024]{2,1,0:T(8,128)(2,1)S(1)}, u32[]{:S(2)}, u32[]{:S(2)}) collective-permute-start(bf16[4,8,1024]{2,1,0:T(8,128)(2,1)S(1)} %pad_maximum_fusion), channel_id=1, source_target_pairs={{0,2},{1,3},{2,0},{3,1},{4,6},{5,7},{6,4},{7,5},{8,10},{9,11},{10,... | collective-permute-start | bytes 196616 | tf_op jit(solution)/shard_map/ppermute | solution.py:212
  18.8 4.6 %collective-permute-start.4 = (bf16[4,8,1024]{2,1,0:T(8,128)(2,1)S(1)}, bf16[4,8,1024]{2,1,0:T(8,128)(2,1)S(1)}, u32[]{:S(2)}, u32[]{:S(2)}) collective-permute-start(bf16[4,8,1024]{2,1,0:T(8,128)(2,1)S(1)} %pad_maximum_fusion.1), channel_id=1, source_target_pairs={{0,4},{1,5},{2,6},{3,7},{4,0},{5,1},{6,2},{7,3},{8,12},{9,13},{10,... | collective-permute-start | bytes 196616 | tf_op jit(solution)/shard_map/ppermute | solution.py:212
  20.4 4.1 %collective-permute-start.5 = (bf16[4,8,1024]{2,1,0:T(8,128)(2,1)S(1)}, bf16[4,8,1024]{2,1,0:T(8,128)(2,1)S(1)}, u32[]{:S(2)}, u32[]{:S(2)}) collective-permute-start(bf16[4,8,1024]{2,1,0:T(8,128)(2,1)S(1)} %pad_maximum_fusion.2), channel_id=1, source_target_pairs={{0,6},{1,7},{2,4},{3,5},{4,2},{5,3},{6,0},{7,1},{8,14},{9,15},{10,... | collective-permute-start | bytes 196616 | tf_op jit(solution)/shard_map/ppermute | solution.py:212
  20.8 3.6 %copy-start.5 = (s32[16]{0:T(128)S(1)}, s32[16]{0:T(128)}, u32[]{:S(2)}) copy-start(s32[16]{0:T(128)} %lags_ref.1) | copy-start | bytes 196
  31.7 3.5 %collective-permute-start.12 = (bf16[2,512,256]{2,1,0:T(8,128)(2,1)S(1)}, bf16[2,512,256]{2,1,0:T(8,128)(2,1)S(1)}, u32[]{:S(2)}, u32[]{:S(2)}) collective-permute-start(bf16[2,512,256]{2,1,0:T(8,128)(2,1)S(1)} %get-tuple-element.31), channel_id=1, source_target_pairs={{0,2},{1,3},{2,0},{3,1},{4,6},{5,7},{6,4},{7,5},{8,10},{9,11},{10,... | collective-permute-start | bytes 1572872 | tf_op jit(solution)/shard_map/ppermute | solution.py:212
  34.9 4.0 %collective-permute-start.18 = (bf16[2,512,256]{2,1,0:T(8,128)(2,1)S(1)}, bf16[2,512,256]{2,1,0:T(8,128)(2,1)S(1)}, u32[]{:S(2)}, u32[]{:S(2)}) collective-permute-start(bf16[2,512,256]{2,1,0:T(8,128)(2,1)S(1)} %get-tuple-element.34), channel_id=1, source_target_pairs={{0,2},{1,3},{2,0},{3,1},{4,6},{5,7},{6,4},{7,5},{8,10},{9,11},{10,... | collective-permute-start | bytes 1572872 | tf_op jit(solution)/shard_map/ppermute | solution.py:212
  35.4 7.0 %collective-permute-start.13 = (bf16[1,2,128,256]{3,2,1,0:T(8,128)(2,1)S(1)}, bf16[1,2,128,256]{3,2,1,0:T(8,128)(2,1)S(1)}, u32[]{:S(2)}, u32[]{:S(2)}) collective-permute-start(bf16[1,2,128,256]{3,2,1,0:T(8,128)(2,1)S(1)} %get-tuple-element.35), channel_id=1, source_target_pairs={{0,5},{1,4},{2,7},{3,6},{4,1},{5,0},{6,3},{7,2},{8,13},{9,12},{10,... | collective-permute-start | bytes 393224 | tf_op jit(solution)/shard_map/ppermute | solution.py:212
  37.8 7.9 %collective-permute-start.15 = (bf16[1,2,128,256]{3,2,1,0:T(8,128)(2,1)S(1)}, bf16[1,2,128,256]{3,2,1,0:T(8,128)(2,1)S(1)}, u32[]{:S(2)}, u32[]{:S(2)}) collective-permute-start(bf16[1,2,128,256]{3,2,1,0:T(8,128)(2,1)S(1)} %get-tuple-element.36), channel_id=1, source_target_pairs={{0,1},{1,0},{2,3},{3,2},{4,5},{5,4},{6,7},{7,6},{8,9},{9,8},{10,11... | collective-permute-start | bytes 393224 | tf_op jit(solution)/shard_map/ppermute | solution.py:212
  38.2 7.5 %collective-permute-start.14 = (bf16[1,2,128,256]{3,2,1,0:T(8,128)(2,1)S(1)}, bf16[1,2,128,256]{3,2,1,0:T(8,128)(2,1)S(1)}, u32[]{:S(2)}, u32[]{:S(2)}) collective-permute-start(bf16[1,2,128,256]{3,2,1,0:T(8,128)(2,1)S(1)} %get-tuple-element.37), channel_id=1, source_target_pairs={{0,4},{1,5},{2,6},{3,7},{4,0},{5,1},{6,2},{7,3},{8,12},{9,13},{10,... | collective-permute-start | bytes 393224 | tf_op jit(solution)/shard_map/ppermute | solution.py:212
  39.0 11.9 %collective-permute-start.19 = (bf16[1,2,128,256]{3,2,1,0:T(8,128)(2,1)S(1)}, bf16[1,2,128,256]{3,2,1,0:T(8,128)(2,1)S(1)}, u32[]{:S(2)}, u32[]{:S(2)}) collective-permute-start(bf16[1,2,128,256]{3,2,1,0:T(8,128)(2,1)S(1)} %get-tuple-element.38), channel_id=1, source_target_pairs={{0,5},{1,4},{2,7},{3,6},{4,1},{5,0},{6,3},{7,2},{8,13},{9,12},{10,... | collective-permute-start | bytes 393224 | tf_op jit(solution)/shard_map/ppermute | solution.py:212
  41.4 9.6 %collective-permute-start.21 = (bf16[1,2,128,256]{3,2,1,0:T(8,128)(2,1)S(1)}, bf16[1,2,128,256]{3,2,1,0:T(8,128)(2,1)S(1)}, u32[]{:S(2)}, u32[]{:S(2)}) collective-permute-start(bf16[1,2,128,256]{3,2,1,0:T(8,128)(2,1)S(1)} %get-tuple-element.39), channel_id=1, source_target_pairs={{0,1},{1,0},{2,3},{3,2},{4,5},{5,4},{6,7},{7,6},{8,9},{9,8},{10,11... | collective-permute-start | bytes 393224 | tf_op jit(solution)/shard_map/ppermute | solution.py:212
  42.3 8.7 %collective-permute-start.20 = (bf16[1,2,128,256]{3,2,1,0:T(8,128)(2,1)S(1)}, bf16[1,2,128,256]{3,2,1,0:T(8,128)(2,1)S(1)}, u32[]{:S(2)}, u32[]{:S(2)}) collective-permute-start(bf16[1,2,128,256]{3,2,1,0:T(8,128)(2,1)S(1)} %get-tuple-element.40), channel_id=1, source_target_pairs={{0,4},{1,5},{2,6},{3,7},{4,0},{5,1},{6,2},{7,3},{8,12},{9,13},{10,... | collective-permute-start | bytes 393224 | tf_op jit(solution)/shard_map/ppermute | solution.py:212
  45.8 8.1 %collective-permute-start.16 = (bf16[1,128,256]{2,1,0:T(8,128)(2,1)S(1)}, bf16[1,128,256]{2,1,0:T(8,128)(2,1)S(1)}, u32[]{:S(2)}, u32[]{:S(2)}) collective-permute-start(bf16[1,128,256]{2,1,0:T(8,128)(2,1)S(1)} %get-tuple-element.41), channel_id=1, source_target_pairs={{0,24},{1,25},{2,26},{3,27},{4,28},{5,29},{6,30},{7,31},{8,16},{9,... | collective-permute-start | bytes 196616 | tf_op jit(solution)/shard_map/ppermute | solution.py:212
  47.8 7.7 %collective-permute-start.17 = (bf16[1,128,256]{2,1,0:T(8,128)(2,1)S(1)}, bf16[1,128,256]{2,1,0:T(8,128)(2,1)S(1)}, u32[]{:S(2)}, u32[]{:S(2)}) collective-permute-start(bf16[1,128,256]{2,1,0:T(8,128)(2,1)S(1)} %get-tuple-element.42), channel_id=1, source_target_pairs={{0,16},{1,17},{2,18},{3,19},{4,20},{5,21},{6,22},{7,23},{8,24},{9,... | collective-permute-start | bytes 196616 | tf_op jit(solution)/shard_map/ppermute | solution.py:212
  51.1 5.5 %collective-permute-start.22 = (bf16[1,128,256]{2,1,0:T(8,128)(2,1)S(1)}, bf16[1,128,256]{2,1,0:T(8,128)(2,1)S(1)}, u32[]{:S(2)}, u32[]{:S(2)}) collective-permute-start(bf16[1,128,256]{2,1,0:T(8,128)(2,1)S(1)} %fusion.13), channel_id=1, source_target_pairs={{0,8},{1,9},{2,10},{3,11},{4,12},{5,13},{6,14},{7,15},{8,0},{9,1},... | collective-permute-start | bytes 196616 | tf_op jit(solution)/shard_map/ppermute | solution.py:212

commit v3 on v2

v3 whole, which is shorter than its diff:
```python
import functools

import jax
import jax.numpy as jnp
from jax import lax
from jax.experimental import pallas as pl
from jax.experimental.pallas import tpu as pltpu
from jax.sharding import PartitionSpec as P

LANES = 128
AXES = ("cfd", "ac")
MIDDLE = ((1, 1), (1, 0), (0, 1))
MIB = 1024 * 1024
SMEM = pl.BlockSpec(memory_space=pltpu.SMEM)
VMEM = pl.BlockSpec(memory_space=pltpu.VMEM)
HBM = pl.BlockSpec(memory_space=pltpu.HBM)


def params(mib):
    return pltpu.CompilerParams(vmem_limit_bytes=mib * MIB)


def distance_from_me(distance):
    return jnp.bitwise_xor(lax.axis_index("cfd"), distance)


def outgoing_kernel(direct, high, order_hbm, surface_hbm, normals_hbm, *refs):
    direct_refs, refs = refs[:direct], refs[direct:]
    early_refs, (order_ref, surface_ref, normals_ref, columns_ref, sems) = refs[:4], refs[4:]
    loads = [
        pltpu.make_async_copy(order_hbm, order_ref, sems.at[0]),
        pltpu.make_async_copy(normals_hbm, normals_ref, sems.at[1]),
        pltpu.make_async_copy(surface_hbm, surface_ref, sems.at[2]),
    ]
    for load in loads:
        load.start()
    loads[1].wait()
    normals = normals_ref[...].astype(jnp.float32)
    faces = normals.shape[1]
    square = jnp.concatenate([normals, jnp.zeros((faces - normals.shape[0], faces), jnp.float32)], axis=0)
    columns_ref[...] = jnp.transpose(square).reshape(columns_ref.shape)
    loads[0].wait()
    loads[2].wait()
    for z in range(high):
        for q in range(4):
            block = order_ref[0, distance_from_me(4 * z + q)]
            normal = columns_ref[block]
            along = surface_ref[2, block].astype(jnp.float32) * normal[:, 0:1]
            along = along + surface_ref[3, block].astype(jnp.float32) * normal[:, 1:2]
            along = along + surface_ref[4, block].astype(jnp.float32) * normal[:, 2:3]
            out = direct_refs[z].at[q] if z < direct else early_refs[q].at[z - direct]
            out[0] = (surface_ref[1, block].astype(jnp.float32) * along).astype(jnp.bfloat16)
            out[1] = surface_ref[0, block]


def outgoing(order, surface, normals, direct, high):
    comps, blocks, rows, steps = surface.shape
    shape = lambda lead: jax.ShapeDtypeStruct((lead, 2, rows, steps), jnp.bfloat16)
    return pl.pallas_call(
        functools.partial(outgoing_kernel, direct, high),
        out_shape=(shape(4),) * direct + (shape(high - direct),) * 4,
        in_specs=[HBM, HBM, HBM],
        out_specs=(VMEM,) * (direct + 4),
        scratch_shapes=[
            pltpu.SMEM(order.shape, jnp.int32),
            pltpu.VMEM(surface.shape, jnp.bfloat16),
            pltpu.VMEM(normals.shape, jnp.bfloat16),
            pltpu.VMEM((blocks, rows, blocks * rows), jnp.float32),
            pltpu.SemaphoreType.DMA((3,)),
        ],
        compiler_params=params(8),
        name="outgoing",
    )(*(pltpu.with_memory_space_constraint(x, pltpu.HBM) for x in (order, surface, normals)))


def prepare_kernel(ranks, layout, observers_ref, weights_ref, select_ref, joined_ref):
    taps, terms, observers, faces = weights_ref.shape
    for k in range(taps):
        for c in range(terms):
            at = (k * terms + c) * faces
            joined_ref[:, at : at + faces] = weights_ref[k, c]
    each = observers // ranks
    ids = observers_ref[...]
    local_row = lax.broadcasted_iota(jnp.int32, (each, observers), 0)
    for position, member in enumerate(layout):
        base = distance_from_me(member) * each
        chosen = jnp.where(local_row == ids - base, 1.0, 0.0).astype(jnp.bfloat16)
        select_ref[position * each : (position + 1) * each, :] = chosen


def prepare(observers, weights, ranks, layout):
    taps, terms, count, faces = weights.shape
    return pl.pallas_call(
        functools.partial(prepare_kernel, ranks, layout),
        out_shape=(
            jax.ShapeDtypeStruct((count, count), jnp.bfloat16),
            jax.ShapeDtypeStruct((count, taps * terms * faces), jnp.bfloat16),
        ),
        in_specs=[VMEM, VMEM],
        out_specs=(VMEM, VMEM),
        cost_estimate=pl.CostEstimate(flops=2 * 10**9, bytes_accessed=10**7, transcendentals=0),
        compiler_params=params(24),
        name="prepare",
    )(observers.reshape(1, -1), weights)


def place_block(series_ref, distance, block):
    rows = block.shape[1]
    source = distance_from_me(distance)
    for kind in range(2):
        value = block[kind].astype(jnp.float32)
        if rows % 8 == 0:
            series_ref[kind, pl.ds(pl.multiple_of(source * rows, 8), rows), :] = value
        else:
            for r in range(rows):
                series_ref[kind, pl.ds(source * rows + r, 1), :] = value[r : r + 1]


def order_rows(select_ref, first_row, banded_ref, out_ref):
    parts, rows, piece = out_ref.shape
    chosen = select_ref[first_row : first_row + rows, :]
    for y in range(parts):
        if parts == 1:
            data = banded_ref[...]
        else:
            column = pl.multiple_of(jnp.bitwise_xor(lax.axis_index("ac"), y) * piece, piece)
            data = banded_ref[:, pl.ds(column, piece)]
        out_ref[y] = jnp.dot(chosen, data, preferred_element_type=jnp.float32).astype(jnp.bfloat16)


def bands_kernel(taps, direct, high, first_row, lags_ref, joined_ref, select_ref, *refs):
    near_refs, refs = refs[:direct], refs[direct:]
    post_refs, refs = refs[:3], refs[3:]
    late_refs, refs = refs[: high - direct], refs[high - direct :]
    banded_ref, send_ref, stacked_ref, series_ref = refs
    _, faces, steps = series_ref.shape
    terms = joined_ref.shape[1] // faces // taps
    span = stacked_ref.shape[1]
    observers, out_len = banded_ref.shape
    bands = lags_ref.shape[0]
    width = observers // bands
    wide = out_len + LANES
    for z in range(high):
        for q in range(4):
            if z >= direct:
                block = late_refs[z - direct][q]
            else:
                block = post_refs[q - 1][z] if q else near_refs[z][0]
            place_block(series_ref, 4 * z + q, block)
    stacked_ref[:, steps:span] = jnp.zeros((stacked_ref.shape[0], span - steps), jnp.bfloat16)
    first = lax.broadcasted_iota(jnp.int32, (faces, steps), 1) == 0
    for kind in range(2):
        series = series_ref[kind]
        rate = jnp.where(first, 0.0, series - pltpu.roll(series, 1, 1))
        for term, value in [(0, rate)] if kind == 0 else [(1, rate), (2, series)]:
            for tap in range(taps):
                moved = pltpu.roll(value, tap, 1) if tap else value
                at = (tap * terms + term) * faces
                stacked_ref[at : at + faces, 0:steps] = moved.astype(jnp.bfloat16)

    def one_band(b, carry):
        start = out_len - lags_ref[b]
        column = pl.multiple_of((start // LANES) * LANES, LANES)
        rest = start % LANES
        at = pl.ds(pl.multiple_of(b * width, width), width)
        full = jnp.dot(joined_ref[at, :], stacked_ref[:, pl.ds(column, wide)], preferred_element_type=jnp.float32)
        turned = pltpu.roll(full, (wide - rest) % wide, 1)
        banded_ref[at, :] = turned[:, :out_len].astype(jnp.bfloat16)
        return carry

    lax.fori_loop(0, bands, one_band, 0, unroll=4)
    order_rows(select_ref, first_row, banded_ref, send_ref)


def bands(lags, near, post, late, joined, select, first_row, taps, shape):
    count = joined.shape[0]
    steps = near[0].shape[-1]
    out_len = steps // 2
    direct, high = len(near), len(near) + len(late)
    faces = 4 * high * near[0].shape[2]
    return pl.pallas_call(
        functools.partial(bands_kernel, taps, direct, high, first_row),
        out_shape=(jax.ShapeDtypeStruct((count, out_len), jnp.bfloat16), shape),
        in_specs=[SMEM] + [VMEM] * (high + 5),
        out_specs=(VMEM, VMEM),
        scratch_shapes=[
            pltpu.VMEM((joined.shape[1], steps + LANES), jnp.bfloat16),
            pltpu.VMEM((2, faces, steps), jnp.float32),
        ],
        cost_estimate=pl.CostEstimate(flops=4 * 10**9, bytes_accessed=10**7, transcendentals=0),
        compiler_params=params(24),
        name="bands",
    )(lags, joined, select, *near, *post, *late)


def order_kernel(first_row, banded_ref, select_ref, *refs):
    out_ref = refs[-1]
    order_rows(select_ref, first_row, banded_ref, out_ref)


def order_more(banded, select, first_row, shape, after=()):
    return pl.pallas_call(
        functools.partial(order_kernel, first_row),
        out_shape=shape,
        in_specs=[VMEM] * (2 + len(after)),
        out_specs=VMEM,
        cost_estimate=pl.CostEstimate(flops=10**9, bytes_accessed=5 * 10**6, transcendentals=0),
        compiler_params=params(16),
        name="order",
    )(banded, select, *after)


def swap(value, ranks, sides, rank_mask, side_mask=0):
    pairs = [
        (r * sides + s, (r ^ rank_mask) * sides + (s ^ side_mask)) for r in range(ranks) for s in range(sides)
    ]
    return lax.ppermute(value, AXES, pairs)


def local(surface_raw, area_normals, kernel_weights, block_map, band_observers, band_lags):
    ranks = lax.axis_size("cfd")
    sides = lax.axis_size("ac")
    high = ranks // 4
    direct = high - max(1, high // 4)
    comps, faces, steps = surface_raw.shape
    surface = surface_raw.reshape(comps, ranks, faces // ranks, steps)
    made = outgoing(block_map.reshape(1, ranks), surface, area_normals, direct, high)
    near, early = list(made[:direct]), list(made[direct:])
    for z in range(direct - 1, 0, -1):
        near[z] = swap(near[z], ranks, sides, 4 * z)
    for q in range(3, 0, -1):
        early[q] = swap(early[q], ranks, sides, q)
    late = [
        swap(jnp.stack([early[q][z - direct] for q in range(4)]), ranks, sides, 4 * z) for z in range(direct, high)
    ]
    post = [swap(jnp.stack([near[z][q] for z in range(direct)]), ranks, sides, q) for q in range(1, 4)]

    taps, _, count, _ = kernel_weights.shape
    out_len = steps // 2
    each = count // ranks
    half = high // 2
    chunks = (range(half, high), range(half))
    layout = [(z * 2 + x) * 2 + c for zs in chunks for c in (1, 0) for x in range(2) for z in zs]
    parts = sides if out_len // sides % LANES == 0 else 1
    rows = half * 2 * each
    shape = jax.ShapeDtypeStruct((parts, rows, out_len // parts), jnp.bfloat16)
    select, joined = prepare(band_observers, kernel_weights, ranks, layout)
    banded, far_send = bands(band_lags, near, post, late, joined, select, 0, taps, shape)
    which = jnp.bitwise_xor(lax.iota(jnp.int32, sides), lax.axis_index("ac"))

    def by_side(value):
        if parts != sides:
            value = value.reshape(rows, sides, out_len // sides)
            value = jnp.transpose(jnp.take(value, which, axis=1), (1, 0, 2))
        return value.reshape(sides // 2, 2, 2, half, each, out_len // sides)

    def over_core(send, keep_from):
        got = by_side(swap(send, ranks, sides, 1))
        keep = by_side(order_more(banded, select, keep_from, shape))
        total = lambda x, y: keep[:, y, x].astype(jnp.float32) + got[:, y, x].astype(jnp.float32)
        return total(0, 0), [total(x, y).astype(jnp.bfloat16) for x, y in MIDDLE]

    def over_middle(total, sends):
        for (x, y), send in zip(MIDDLE, sends):
            total = total + swap(send, ranks, sides, 2 * x, y).astype(jnp.float32)
        return total

    def over_z(result, total, zs):
        for z in reversed(zs):
            moved = total[:, z - zs[0]]
            if z:
                moved = swap(moved.astype(jnp.bfloat16), ranks, sides, 4 * z).astype(jnp.float32)
            result = moved if result is None else result + moved
        return result

    far_total, far_sends = over_core(far_send, rows)
    near_send = order_more(banded, select, 2 * rows, shape, far_sends)
    near_total, near_sends = over_core(near_send, 3 * rows)
    result = over_z(None, over_middle(far_total, far_sends), chunks[0])
    result = over_z(result, over_middle(near_total, near_sends), chunks[1])
    out = result[0]
    for y in range(sides // 2 - 1, 0, -1):
        out = out + swap(result[y].astype(jnp.bfloat16), ranks, sides, 0, 2 * y).astype(jnp.float32)
    return out


def solution(mesh):
    placed = (
        P(None, ("cfd", "ac"), None),
        P(None, ("cfd", "ac")),
        P(None, None, None, ("cfd", "ac")),
        P("ac", "cfd", None),
        P(),
        P(),
    )
    return jax.shard_map(
        local, mesh=mesh, in_specs=placed, out_specs=P("cfd", "ac"), check_vma=False
    )
```

time: 57.5 us -> 60.3 us (1.049)
  waiting for transfers between devices: 8 us -> 20 us
  starting transfers between devices: 31.1 us -> 22.5 us
    ppermute x23 -> x20, waiting for transfers between devices: 8 us -> 20 us  [swap(): return lax.ppermute(value, AXES, pairs)]
    ppermute x23 -> x20, starting transfers between devices: 31.1 us -> 22.5 us  [swap(): return lax.ppermute(value, AXES, pairs)]
    unnamed x12 -> x6, local copies, waits for them, and re-layouts: 2.66 us -> 2.59 us
    pallas_call x4 -> x5, Pallas kernels: 11.6 us -> 11.7 us  [the longest x1 6.29 us: bands(): pl.pallas_call(functools.partial(bands_kernel, taps, direct, high, first_...]
  transfers between devices with their start and end apart: 23 -> 20, of which waited for: 6 -> 12; matrix products, arithmetic and copies ran while one was open for 1% -> 0% of each run, Pallas kernels for 10% -> 7%
where the time goes in v3:
time: 60.3 us; the launch traced here: 60.1 us
  starting transfers between devices  22.5 us (37%)
  waiting for transfers between devices  20 us (33%)
  Pallas kernels  13.6 us (23%)
  local copies, waits for them, and re-layouts  2.63 us (4%)
  other arithmetic  1.12 us (2%)
    ppermute x20, starting transfers between devices, swap(): return lax.ppermute(value, AXES, pairs)  22.5 us
    ppermute x20, waiting for transfers between devices, swap(): return lax.ppermute(value, AXES, pairs)  20 us
    pallas_call x1, Pallas kernels, bands(): pl.pallas_call(functools.partial(bands_kernel, taps, direct, high, first_...  6.29 us
    pallas_call x3, Pallas kernels, order_more(): pl.pallas_call(functools.partial(order_kernel, first_row), out_shape=shap...  3.76 us
    unnamed x6, local copies, waits for them, and re-layouts  2.59 us
    pallas_call x1, Pallas kernels, prepare(): pl.pallas_call(functools.partial(prepare_kernel, ranks, layout), out_shap...  1.95 us
    pallas_call x1, Pallas kernels, outgoing(): pl.pallas_call(functools.partial(outgoing_kernel, direct, high), out_shap...  1.6 us
  transfers between devices with their start and end apart: 20, of which 12 were waited for; matrix products, arithmetic and copies ran while one was open for 0% of the time, Pallas kernels for 7%

profile of v3, /device:TPU:0, one launch (start us, length us, event | category | flops | bytes accessed | tf_op | source)
XLA Modules:
  0.0 60.1 jit_solution(10181032698033830193)
XLA Ops:
  0.0 1.6 %outgoing.1 = (bf16[4,2,8,1024]{3,2,1,0:T(8,128)(2,1)S(1)}, bf16[4,2,8,1024]{3,2,1,0:T(8,128)(2,1)S(1)}, bf16[4,2,8,1024]{3,2,1,0:T(8,128)(2,1)S(1)}, bf16[1,2,8...) custom-call(s32[1,16]{1,0:T(1,128)} %bitcast.57, ...), custom_call_target="tpu_custom_call" | custom-call | tf_op jit(solution)/shard_map/outgoing/pallas_call | solution.py:59
  1.6 0.6 collective-permute-start.5
  2.2 2.6 %collective-permute-start.6 = (bf16[1,2,8,1024]{3,2,1,0:T(8,128)(2,1)S(1)}, bf16[1,2,8,1024]{3,2,1,0:T(8,128)(2,1)S(1)}, u32[]{:S(2)}, u32[]{:S(2)}) collective-permute-start(bf16[1,2,8,1024]{3,2,1,0:T(8,128)(2,1)S(1)} %get-tuple-element.23), channel_id=1, source_target_pairs={{0,4},{1,5},{2,6},{3,7},{4,0},{5,1},{6,2},{7,3},{8,12},{9,13},{10,... | collective-permute-start | bytes 98312 | tf_op jit(solution)/shard_map/ppermute | solution.py:217
  4.8 1.8 %collective-permute-start = (bf16[4,2,8,1024]{3,2,1,0:T(8,128)(2,1)S(1)}, bf16[4,2,8,1024]{3,2,1,0:T(8,128)(2,1)S(1)}, u32[]{:S(2)}, u32[]{:S(2)}) collective-permute-start(bf16[4,2,8,1024]{3,2,1,0:T(8,128)(2,1)S(1)} %get-tuple-element.19), channel_id=1, source_target_pairs={{0,8},{1,9},{2,10},{3,11},{4,12},{5,13},{6,14},{7,15},{8,0},{9,1},... | collective-permute-start | bytes 393224 | tf_op jit(solution)/shard_map/ppermute | solution.py:217
  6.6 2.6 %collective-permute-start.1 = (bf16[4,2,8,1024]{3,2,1,0:T(8,128)(2,1)S(1)}, bf16[4,2,8,1024]{3,2,1,0:T(8,128)(2,1)S(1)}, u32[]{:S(2)}, u32[]{:S(2)}) collective-permute-start(bf16[4,2,8,1024]{3,2,1,0:T(8,128)(2,1)S(1)} %get-tuple-element.20), channel_id=1, source_target_pairs={{0,16},{1,17},{2,18},{3,19},{4,20},{5,21},{6,22},{7,23},{8,24},{9,... | collective-permute-start | bytes 393224 | tf_op jit(solution)/shard_map/ppermute | solution.py:217
  9.2 2.5 %collective-permute-start.8 = (bf16[4,2,8,1024]{3,2,1,0:T(8,128)(2,1)S(1)}, bf16[4,2,8,1024]{3,2,1,0:T(8,128)(2,1)S(1)}, u32[]{:S(2)}, u32[]{:S(2)}) collective-permute-start(bf16[4,2,8,1024]{3,2,1,0:T(8,128)(2,1)S(1)} %pad_maximum_fusion), channel_id=1, source_target_pairs={{0,24},{1,25},{2,26},{3,27},{4,28},{5,29},{6,30},{7,31},{8,16},{9,... | collective-permute-start | bytes 393224 | tf_op jit(solution)/shard_map/ppermute | solution.py:217
  11.8 0.9 %collective-permute-done.refs_1_ = bf16[4,2,8,1024]{3,2,1,0:T(8,128)(2,1)S(1)} collective-permute-done((bf16[4,2,8,1024]{3,2,1,0:T(8,128)(2,1)S(1)}, bf16[4,2,8,1024]{3,2,1,0:T(8,128)(2,1)S(1)}, u32[]{:S(2)}, u32[]{:S(2)}) %collective-permute-start) | collective-permute-done | bytes 131104 | tf_op jit(solution)/shard_map/ppermute | solution.py:217
  12.7 6.8 %collective-permute-done.1.refs_2_ = bf16[4,2,8,1024]{3,2,1,0:T(8,128)(2,1)S(1)} collective-permute-done((bf16[4,2,8,1024]{3,2,1,0:T(8,128)(2,1)S(1)}, bf16[4,2,8,1024]{3,2,1,0:T(8,128)(2,1)S(1)}, u32[]{:S(2)}, u32[]{:S(2)}) %collective-permute-start.1) | collective-permute-done | bytes 131104 | tf_op jit(solution)/shard_map/ppermute | solution.py:217
  19.7 1.6 %collective-permute-start.3 = (bf16[3,2,8,1024]{3,2,1,0:T(8,128)(2,1)S(1)}, bf16[3,2,8,1024]{3,2,1,0:T(8,128)(2,1)S(1)}, u32[]{:S(2)}, u32[]{:S(2)}) collective-permute-start(bf16[3,2,8,1024]{3,2,1,0:T(8,128)(2,1)S(1)} %pad_maximum_fusion.2), channel_id=1, source_target_pairs={{0,4},{1,5},{2,6},{3,7},{4,0},{5,1},{6,2},{7,3},{8,12},{9,13},{10,... | collective-permute-start | bytes 294920 | tf_op jit(solution)/shard_map/ppermute | solution.py:217
  21.7 1.9 %copy-done = bf16[2,3,2048,128]{3,2,1,0:T(8,128)(2,1)S(1)} copy-done((bf16[2,3,2048,128]{3,2,1,0:T(8,128)(2,1)S(1)}, bf16[2,3,2048,128]{3,2,1,0:T(8,128)(2,1)}, u32[]{:S(2)}) %copy-start) | copy-done | bytes 3145752
  23.5 0.7 %copy-done.1 = s32[16,128]{1,0:T(8,128)S(1)} copy-done((s32[16,128]{1,0:T(8,128)S(1)}, s32[16,128]{1,0:T(8,128)}, u32[]{:S(2)}) %copy-start.1) | copy-done | bytes 8216
  24.2 1.9 %prepare.1 = (bf16[2048,2048]{1,0:T(8,128)(2,1)S(1)}, bf16[2048,768]{1,0:T(8,128)(2,1)S(1)}) custom-call(s32[1,2048]{1,0:T(1,128)S(1)} %bitcast.51, bf16[2,3,2048,128]{3,2,1,0:T(8,128)(2,1)S(1)} %copy-done), custom_call_target="tpu_custom_call" | custom-call | flops 2000000000 | bytes 10000000 | tf_op jit(solution)/shard_map/prepare/pallas_call | solution.py:93
  26.5 6.3 %bands.1 = (bf16[2048,512]{1,0:T(8,128)(2,1)S(1)}, bf16[2,512,256]{2,1,0:T(8,128)(2,1)S(1)}) custom-call(s32[16]{0:T(128)S(1)} %copy-done.2, bf16[2048,768]{1,0:T(8,128)(2,1)S(1)} %get-tuple-element.16.joined_ref, bf16[2048,2048]{1,0:T(8,128)(2,1)S(1)} %get-tuple-element.17.select_ref, bf16[4,2,8,1024]{3,2,1,0:T(8,128)(2,1)S(1)} %get-tuple-element.18.refs_0_, ...), custom_call_target="tpu_custom_call" | custom-call | flops 4000000000 | bytes 10000000 | tf_op jit(solution)/shard_map/bands/pallas_call | solution.py:181
  33.2 1.3 %order.3 = bf16[2,512,256]{2,1,0:T(8,128)(2,1)S(1)} custom-call(bf16[2048,512]{1,0:T(8,128)(2,1)S(1)} %get-tuple-element.25.banded_ref, bf16[2048,2048]{1,0:T(8,128)(2,1)S(1)} %get-tuple-element.17.select_ref), custom_call_target="tpu_custom_call" | custom-call | flops 1000000000 | bytes 5000000 | tf_op jit(solution)/shard_map/order/pallas_call | solution.py:202
  34.9 1.3 %order.5 = bf16[2,512,256]{2,1,0:T(8,128)(2,1)S(1)} custom-call(bf16[2048,512]{1,0:T(8,128)(2,1)S(1)} %get-tuple-element.25.banded_ref, bf16[2048,2048]{1,0:T(8,128)(2,1)S(1)} %get-tuple-element.17.select_ref, bf16[1,2,128,256]{3,2,1,0:T(8,128)(2,1)S(1)} %get-tuple-element.32.refs_0_, bf16[1,2,128,256]{3,2,1,0:T(8,128)(2,1)S(1)} %get-tuple-element.31.refs_1_, ...), custom_call_target="tpu_custom_call" | custom-call | flops 1000000000 | bytes 5000000 | tf_op jit(solution)/shard_map/order/pallas_call | solution.py:202
  36.5 1.5 %collective-permute-start.12 = (bf16[1,2,128,256]{3,2,1,0:T(8,128)(2,1)S(1)}, bf16[1,2,128,256]{3,2,1,0:T(8,128)(2,1)S(1)}, u32[]{:S(2)}, u32[]{:S(2)}) collective-permute-start(bf16[1,2,128,256]{3,2,1,0:T(8,128)(2,1)S(1)} %get-tuple-element.30.refs_2_), channel_id=1, source_target_pairs={{0,1},{1,0},{2,3},{3,2},{4,5},{5,4},{6,7},{7,6},{8,9},{9,8},{10,11... | collective-permute-start | bytes 393224 | tf_op jit(solution)/shard_map/ppermute | solution.py:217
  38.1 1.5 %collective-permute-start.11 = (bf16[1,2,128,256]{3,2,1,0:T(8,128)(2,1)S(1)}, bf16[1,2,128,256]{3,2,1,0:T(8,128)(2,1)S(1)}, u32[]{:S(2)}, u32[]{:S(2)}) collective-permute-start(bf16[1,2,128,256]{3,2,1,0:T(8,128)(2,1)S(1)} %get-tuple-element.31.refs_1_), channel_id=1, source_target_pairs={{0,4},{1,5},{2,6},{3,7},{4,0},{5,1},{6,2},{7,3},{8,12},{9,13},{10,... | collective-permute-start | bytes 393224 | tf_op jit(solution)/shard_map/ppermute | solution.py:217
  39.6 0.5 collective-permute-start.10
  40.0 1.2 %order.4 = bf16[2,512,256]{2,1,0:T(8,128)(2,1)S(1)} custom-call(bf16[2048,512]{1,0:T(8,128)(2,1)S(1)} %get-tuple-element.25.banded_ref, bf16[2048,2048]{1,0:T(8,128)(2,1)S(1)} %get-tuple-element.17.select_ref), custom_call_target="tpu_custom_call" | custom-call | flops 1000000000 | bytes 5000000 | tf_op jit(solution)/shard_map/order/pallas_call | solution.py:202
  41.3 0.9 %collective-permute-done.12 = bf16[1,2,128,256]{3,2,1,0:T(8,128)(2,1)S(1)} collective-permute-done((bf16[1,2,128,256]{3,2,1,0:T(8,128)(2,1)S(1)}, bf16[1,2,128,256]{3,2,1,0:T(8,128)(2,1)S(1)}, u32[]{:S(2)}, u32[]{:S(2)}) %collective-permute-start.12) | collective-permute-done | bytes 131104 | tf_op jit(solution)/shard_map/ppermute | solution.py:217
  42.2 2.3 %collective-permute-done.11 = bf16[1,2,128,256]{3,2,1,0:T(8,128)(2,1)S(1)} collective-permute-done((bf16[1,2,128,256]{3,2,1,0:T(8,128)(2,1)S(1)}, bf16[1,2,128,256]{3,2,1,0:T(8,128)(2,1)S(1)}, u32[]{:S(2)}, u32[]{:S(2)}) %collective-permute-start.11) | collective-permute-done | bytes 131104 | tf_op jit(solution)/shard_map/ppermute | solution.py:217
  44.5 1.7 %collective-permute-done.10 = bf16[1,2,128,256]{3,2,1,0:T(8,128)(2,1)S(1)} collective-permute-done((bf16[1,2,128,256]{3,2,1,0:T(8,128)(2,1)S(1)}, bf16[1,2,128,256]{3,2,1,0:T(8,128)(2,1)S(1)}, u32[]{:S(2)}, u32[]{:S(2)}) %collective-permute-start.10) | collective-permute-done | bytes 131104 | tf_op jit(solution)/shard_map/ppermute | solution.py:217
  46.4 2.5 %collective-permute-start.16 = (bf16[1,2,128,256]{3,2,1,0:T(8,128)(2,1)S(1)}, bf16[1,2,128,256]{3,2,1,0:T(8,128)(2,1)S(1)}, u32[]{:S(2)}, u32[]{:S(2)}) collective-permute-start(bf16[1,2,128,256]{3,2,1,0:T(8,128)(2,1)S(1)} %get-tuple-element.27), channel_id=1, source_target_pairs={{0,5},{1,4},{2,7},{3,6},{4,1},{5,0},{6,3},{7,2},{8,13},{9,12},{10,... | collective-permute-start | bytes 393224 | tf_op jit(solution)/shard_map/ppermute | solution.py:217
  48.9 0.5 collective-permute-start.18
  49.4 0.5 collective-permute-start.17
  49.9 2.5 %collective-permute-start.13 = (bf16[1,128,256]{2,1,0:T(8,128)(2,1)S(1)}, bf16[1,128,256]{2,1,0:T(8,128)(2,1)S(1)}, u32[]{:S(2)}, u32[]{:S(2)}) collective-permute-start(bf16[1,128,256]{2,1,0:T(8,128)(2,1)S(1)} %get-tuple-element.33), channel_id=1, source_target_pairs={{0,24},{1,25},{2,26},{3,27},{4,28},{5,29},{6,30},{7,31},{8,16},{9,... | collective-permute-start | bytes 196616 | tf_op jit(solution)/shard_map/ppermute | solution.py:217
  52.5 0.7 %collective-permute-done.16 = bf16[1,2,128,256]{3,2,1,0:T(8,128)(2,1)S(1)} collective-permute-done((bf16[1,2,128,256]{3,2,1,0:T(8,128)(2,1)S(1)}, bf16[1,2,128,256]{3,2,1,0:T(8,128)(2,1)S(1)}, u32[]{:S(2)}, u32[]{:S(2)}) %collective-permute-start.16) | collective-permute-done | bytes 131104 | tf_op jit(solution)/shard_map/ppermute | solution.py:217
  53.1 1.8 %collective-permute-done.18 = bf16[1,2,128,256]{3,2,1,0:T(8,128)(2,1)S(1)} collective-permute-done((bf16[1,2,128,256]{3,2,1,0:T(8,128)(2,1)S(1)}, bf16[1,2,128,256]{3,2,1,0:T(8,128)(2,1)S(1)}, u32[]{:S(2)}, u32[]{:S(2)}) %collective-permute-start.18) | collective-permute-done | bytes 131104 | tf_op jit(solution)/shard_map/ppermute | solution.py:217
  55.1 1.0 %collective-permute-done.13 = bf16[1,128,256]{2,1,0:T(8,128)(2,1)S(1)} collective-permute-done((bf16[1,128,256]{2,1,0:T(8,128)(2,1)S(1)}, bf16[1,128,256]{2,1,0:T(8,128)(2,1)S(1)}, u32[]{:S(2)}, u32[]{:S(2)}) %collective-permute-start.13) | collective-permute-done | bytes 65568 | tf_op jit(solution)/shard_map/ppermute | solution.py:217
  56.2 1.5 %collective-permute-done.14 = bf16[1,128,256]{2,1,0:T(8,128)(2,1)S(1)} collective-permute-done((bf16[1,128,256]{2,1,0:T(8,128)(2,1)S(1)}, bf16[1,128,256]{2,1,0:T(8,128)(2,1)S(1)}, u32[]{:S(2)}, u32[]{:S(2)}) %collective-permute-start.14) | collective-permute-done | bytes 65568 | tf_op jit(solution)/shard_map/ppermute | solution.py:217
  57.7 1.7 %collective-permute-done.19 = bf16[1,128,256]{2,1,0:T(8,128)(2,1)S(1)} collective-permute-done((bf16[1,128,256]{2,1,0:T(8,128)(2,1)S(1)}, bf16[1,128,256]{2,1,0:T(8,128)(2,1)S(1)}, u32[]{:S(2)}, u32[]{:S(2)}) %collective-permute-start.19) | collective-permute-done | bytes 65568 | tf_op jit(solution)/shard_map/ppermute | solution.py:217
  59.4 0.7 %fusion.12 = f32[128,256]{1,0:T(8,128)} fusion(f32[1,2,128,256]{3,2,1,0:T(8,128)S(1)} %fusion.1, bf16[1,128,256]{2,1,0:T(8,128)(2,1)S(1)} %collective-permute-done.19, bf16[1,128,256]{2,1,0:T(8,128)(2,1)S(1)} %collective-permute-done.14, bf16[1,128,256]{2,1,0:T(8,128)(2,1)S(1)} %collective-permute-done.13), kind=kLoop, calls=%fused_computation.21 | loop fusion | flops 196608 | bytes 458752 | tf_op jit(solution)/shard_map/squeeze | solution.py:281
  (34 shorter events, 2.5 us)
Async XLA Ops:
  1.6 7.6 %collective-permute-start.5 = (bf16[1,2,8,1024]{3,2,1,0:T(8,128)(2,1)S(1)}, bf16[1,2,8,1024]{3,2,1,0:T(8,128)(2,1)S(1)}, u32[]{:S(2)}, u32[]{:S(2)}) collective-permute-start(bf16[1,2,8,1024]{3,2,1,0:T(8,128)(2,1)S(1)} %get-tuple-element.22), channel_id=1, source_target_pairs={{0,2},{1,3},{2,0},{3,1},{4,6},{5,7},{6,4},{7,5},{8,10},{9,11},{10,... | collective-permute-start | bytes 98312 | tf_op jit(solution)/shard_map/ppermute | solution.py:217
  2.2 7.0 %collective-permute-start.6 = (bf16[1,2,8,1024]{3,2,1,0:T(8,128)(2,1)S(1)}, bf16[1,2,8,1024]{3,2,1,0:T(8,128)(2,1)S(1)}, u32[]{:S(2)}, u32[]{:S(2)}) collective-permute-start(bf16[1,2,8,1024]{3,2,1,0:T(8,128)(2,1)S(1)} %get-tuple-element.23), channel_id=1, source_target_pairs={{0,4},{1,5},{2,6},{3,7},{4,0},{5,1},{6,2},{7,3},{8,12},{9,13},{10,... | collective-permute-start | bytes 98312 | tf_op jit(solution)/shard_map/ppermute | solution.py:217
  4.7 4.5 %collective-permute-start.7 = (bf16[1,2,8,1024]{3,2,1,0:T(8,128)(2,1)S(1)}, bf16[1,2,8,1024]{3,2,1,0:T(8,128)(2,1)S(1)}, u32[]{:S(2)}, u32[]{:S(2)}) collective-permute-start(bf16[1,2,8,1024]{3,2,1,0:T(8,128)(2,1)S(1)} %get-tuple-element.24), channel_id=1, source_target_pairs={{0,6},{1,7},{2,4},{3,5},{4,2},{5,3},{6,0},{7,1},{8,14},{9,15},{10,... | collective-permute-start | bytes 98312 | tf_op jit(solution)/shard_map/ppermute | solution.py:217
  4.8 7.9 %collective-permute-start = (bf16[4,2,8,1024]{3,2,1,0:T(8,128)(2,1)S(1)}, bf16[4,2,8,1024]{3,2,1,0:T(8,128)(2,1)S(1)}, u32[]{:S(2)}, u32[]{:S(2)}) collective-permute-start(bf16[4,2,8,1024]{3,2,1,0:T(8,128)(2,1)S(1)} %get-tuple-element.19), channel_id=1, source_target_pairs={{0,8},{1,9},{2,10},{3,11},{4,12},{5,13},{6,14},{7,15},{8,0},{9,1},... | collective-permute-start | bytes 393224 | tf_op jit(solution)/shard_map/ppermute | solution.py:217
  6.6 12.9 %collective-permute-start.1 = (bf16[4,2,8,1024]{3,2,1,0:T(8,128)(2,1)S(1)}, bf16[4,2,8,1024]{3,2,1,0:T(8,128)(2,1)S(1)}, u32[]{:S(2)}, u32[]{:S(2)}) collective-permute-start(bf16[4,2,8,1024]{3,2,1,0:T(8,128)(2,1)S(1)} %get-tuple-element.20), channel_id=1, source_target_pairs={{0,16},{1,17},{2,18},{3,19},{4,20},{5,21},{6,22},{7,23},{8,24},{9,... | collective-permute-start | bytes 393224 | tf_op jit(solution)/shard_map/ppermute | solution.py:217
  9.2 17.0 %collective-permute-start.8 = (bf16[4,2,8,1024]{3,2,1,0:T(8,128)(2,1)S(1)}, bf16[4,2,8,1024]{3,2,1,0:T(8,128)(2,1)S(1)}, u32[]{:S(2)}, u32[]{:S(2)}) collective-permute-start(bf16[4,2,8,1024]{3,2,1,0:T(8,128)(2,1)S(1)} %pad_maximum_fusion), channel_id=1, source_target_pairs={{0,24},{1,25},{2,26},{3,27},{4,28},{5,29},{6,30},{7,31},{8,16},{9,... | collective-permute-start | bytes 393224 | tf_op jit(solution)/shard_map/ppermute | solution.py:217
  19.6 6.7 %collective-permute-start.2 = (bf16[3,2,8,1024]{3,2,1,0:T(8,128)(2,1)S(1)}, bf16[3,2,8,1024]{3,2,1,0:T(8,128)(2,1)S(1)}, u32[]{:S(2)}, u32[]{:S(2)}) collective-permute-start(bf16[3,2,8,1024]{3,2,1,0:T(8,128)(2,1)S(1)} %pad_maximum_fusion.1), channel_id=1, source_target_pairs={{0,2},{1,3},{2,0},{3,1},{4,6},{5,7},{6,4},{7,5},{8,10},{9,11},{10,... | collective-permute-start | bytes 294920 | tf_op jit(solution)/shard_map/ppermute | solution.py:217
  19.7 6.6 %collective-permute-start.3 = (bf16[3,2,8,1024]{3,2,1,0:T(8,128)(2,1)S(1)}, bf16[3,2,8,1024]{3,2,1,0:T(8,128)(2,1)S(1)}, u32[]{:S(2)}, u32[]{:S(2)}) collective-permute-start(bf16[3,2,8,1024]{3,2,1,0:T(8,128)(2,1)S(1)} %pad_maximum_fusion.2), channel_id=1, source_target_pairs={{0,4},{1,5},{2,6},{3,7},{4,0},{5,1},{6,2},{7,3},{8,12},{9,13},{10,... | collective-permute-start | bytes 294920 | tf_op jit(solution)/shard_map/ppermute | solution.py:217
  21.2 5.3 %collective-permute-start.4 = (bf16[3,2,8,1024]{3,2,1,0:T(8,128)(2,1)S(1)}, bf16[3,2,8,1024]{3,2,1,0:T(8,128)(2,1)S(1)}, u32[]{:S(2)}, u32[]{:S(2)}) collective-permute-start(bf16[3,2,8,1024]{3,2,1,0:T(8,128)(2,1)S(1)} %pad_maximum_fusion.3), channel_id=1, source_target_pairs={{0,6},{1,7},{2,4},{3,5},{4,2},{5,3},{6,0},{7,1},{8,14},{9,15},{10,... | collective-permute-start | bytes 294920 | tf_op jit(solution)/shard_map/ppermute | solution.py:217
  21.6 1.9 %copy-start = (bf16[2,3,2048,128]{3,2,1,0:T(8,128)(2,1)S(1)}, bf16[2,3,2048,128]{3,2,1,0:T(8,128)(2,1)}, u32[]{:S(2)}) copy-start(bf16[2,3,2048,128]{3,2,1,0:T(8,128)(2,1)} %weights_ref.1) | copy-start | bytes 9437188
  23.5 0.7 %copy-start.1 = (s32[16,128]{1,0:T(8,128)S(1)}, s32[16,128]{1,0:T(8,128)}, u32[]{:S(2)}) copy-start(s32[16,128]{1,0:T(8,128)} %param.10) | copy-start | bytes 24580
  24.2 2.3 %copy-start.2 = (s32[16]{0:T(128)S(1)}, s32[16]{0:T(128)}, u32[]{:S(2)}) copy-start(s32[16]{0:T(128)} %lags_ref.1) | copy-start | bytes 196
  32.8 2.0 %collective-permute-start.9 = (bf16[2,512,256]{2,1,0:T(8,128)(2,1)S(1)}, bf16[2,512,256]{2,1,0:T(8,128)(2,1)S(1)}, u32[]{:S(2)}, u32[]{:S(2)}) collective-permute-start(bf16[2,512,256]{2,1,0:T(8,128)(2,1)S(1)} %get-tuple-element.26), channel_id=1, source_target_pairs={{0,2},{1,3},{2,0},{3,1},{4,6},{5,7},{6,4},{7,5},{8,10},{9,11},{10,... | collective-permute-start | bytes 1572872 | tf_op jit(solution)/shard_map/ppermute | solution.py:217
  36.2 10.1 %collective-permute-start.15 = (bf16[2,512,256]{2,1,0:T(8,128)(2,1)S(1)}, bf16[2,512,256]{2,1,0:T(8,128)(2,1)S(1)}, u32[]{:S(2)}, u32[]{:S(2)}) collective-permute-start(bf16[2,512,256]{2,1,0:T(8,128)(2,1)S(1)} %order.5), channel_id=1, source_target_pairs={{0,2},{1,3},{2,0},{3,1},{4,6},{5,7},{6,4},{7,5},{8,10},{9,11},{10,... | collective-permute-start | bytes 1572872 | tf_op jit(solution)/shard_map/ppermute | solution.py:217
  36.5 5.6 %collective-permute-start.12 = (bf16[1,2,128,256]{3,2,1,0:T(8,128)(2,1)S(1)}, bf16[1,2,128,256]{3,2,1,0:T(8,128)(2,1)S(1)}, u32[]{:S(2)}, u32[]{:S(2)}) collective-permute-start(bf16[1,2,128,256]{3,2,1,0:T(8,128)(2,1)S(1)} %get-tuple-element.30.refs_2_), channel_id=1, source_target_pairs={{0,1},{1,0},{2,3},{3,2},{4,5},{5,4},{6,7},{7,6},{8,9},{9,8},{10,11... | collective-permute-start | bytes 393224 | tf_op jit(solution)/shard_map/ppermute | solution.py:217
  38.1 6.4 %collective-permute-start.11 = (bf16[1,2,128,256]{3,2,1,0:T(8,128)(2,1)S(1)}, bf16[1,2,128,256]{3,2,1,0:T(8,128)(2,1)S(1)}, u32[]{:S(2)}, u32[]{:S(2)}) collective-permute-start(bf16[1,2,128,256]{3,2,1,0:T(8,128)(2,1)S(1)} %get-tuple-element.31.refs_1_), channel_id=1, source_target_pairs={{0,4},{1,5},{2,6},{3,7},{4,0},{5,1},{6,2},{7,3},{8,12},{9,13},{10,... | collective-permute-start | bytes 393224 | tf_op jit(solution)/shard_map/ppermute | solution.py:217
  39.6 6.6 %collective-permute-start.10 = (bf16[1,2,128,256]{3,2,1,0:T(8,128)(2,1)S(1)}, bf16[1,2,128,256]{3,2,1,0:T(8,128)(2,1)S(1)}, u32[]{:S(2)}, u32[]{:S(2)}) collective-permute-start(bf16[1,2,128,256]{3,2,1,0:T(8,128)(2,1)S(1)} %get-tuple-element.32.refs_0_), channel_id=1, source_target_pairs={{0,5},{1,4},{2,7},{3,6},{4,1},{5,0},{6,3},{7,2},{8,13},{9,12},{10,... | collective-permute-start | bytes 393224 | tf_op jit(solution)/shard_map/ppermute | solution.py:217
  46.4 6.8 %collective-permute-start.16 = (bf16[1,2,128,256]{3,2,1,0:T(8,128)(2,1)S(1)}, bf16[1,2,128,256]{3,2,1,0:T(8,128)(2,1)S(1)}, u32[]{:S(2)}, u32[]{:S(2)}) collective-permute-start(bf16[1,2,128,256]{3,2,1,0:T(8,128)(2,1)S(1)} %get-tuple-element.27), channel_id=1, source_target_pairs={{0,5},{1,4},{2,7},{3,6},{4,1},{5,0},{6,3},{7,2},{8,13},{9,12},{10,... | collective-permute-start | bytes 393224 | tf_op jit(solution)/shard_map/ppermute | solution.py:217
  48.9 6.1 %collective-permute-start.18 = (bf16[1,2,128,256]{3,2,1,0:T(8,128)(2,1)S(1)}, bf16[1,2,128,256]{3,2,1,0:T(8,128)(2,1)S(1)}, u32[]{:S(2)}, u32[]{:S(2)}) collective-permute-start(bf16[1,2,128,256]{3,2,1,0:T(8,128)(2,1)S(1)} %get-tuple-element.28), channel_id=1, source_target_pairs={{0,1},{1,0},{2,3},{3,2},{4,5},{5,4},{6,7},{7,6},{8,9},{9,8},{10,11... | collective-permute-start | bytes 393224 | tf_op jit(solution)/shard_map/ppermute | solution.py:217
  49.4 5.6 %collective-permute-start.17 = (bf16[1,2,128,256]{3,2,1,0:T(8,128)(2,1)S(1)}, bf16[1,2,128,256]{3,2,1,0:T(8,128)(2,1)S(1)}, u32[]{:S(2)}, u32[]{:S(2)}) collective-permute-start(bf16[1,2,128,256]{3,2,1,0:T(8,128)(2,1)S(1)} %get-tuple-element.29), channel_id=1, source_target_pairs={{0,4},{1,5},{2,6},{3,7},{4,0},{5,1},{6,2},{7,3},{8,12},{9,13},{10,... | collective-permute-start | bytes 393224 | tf_op jit(solution)/shard_map/ppermute | solution.py:217
  49.9 6.2 %collective-permute-start.13 = (bf16[1,128,256]{2,1,0:T(8,128)(2,1)S(1)}, bf16[1,128,256]{2,1,0:T(8,128)(2,1)S(1)}, u32[]{:S(2)}, u32[]{:S(2)}) collective-permute-start(bf16[1,128,256]{2,1,0:T(8,128)(2,1)S(1)} %get-tuple-element.33), channel_id=1, source_target_pairs={{0,24},{1,25},{2,26},{3,27},{4,28},{5,29},{6,30},{7,31},{8,16},{9,... | collective-permute-start | bytes 196616 | tf_op jit(solution)/shard_map/ppermute | solution.py:217
  52.5 5.2 %collective-permute-start.14 = (bf16[1,128,256]{2,1,0:T(8,128)(2,1)S(1)}, bf16[1,128,256]{2,1,0:T(8,128)(2,1)S(1)}, u32[]{:S(2)}, u32[]{:S(2)}) collective-permute-start(bf16[1,128,256]{2,1,0:T(8,128)(2,1)S(1)} %get-tuple-element.34), channel_id=1, source_target_pairs={{0,16},{1,17},{2,18},{3,19},{4,20},{5,21},{6,22},{7,23},{8,24},{9,... | collective-permute-start | bytes 196616 | tf_op jit(solution)/shard_map/ppermute | solution.py:217
  55.1 4.3 %collective-permute-start.19 = (bf16[1,128,256]{2,1,0:T(8,128)(2,1)S(1)}, bf16[1,128,256]{2,1,0:T(8,128)(2,1)S(1)}, u32[]{:S(2)}, u32[]{:S(2)}) collective-permute-start(bf16[1,128,256]{2,1,0:T(8,128)(2,1)S(1)} %fusion.13), channel_id=1, source_target_pairs={{0,8},{1,9},{2,10},{3,11},{4,12},{5,13},{6,14},{7,15},{8,0},{9,1},... | collective-permute-start | bytes 196616 | tf_op jit(solution)/shard_map/ppermute | solution.py:217

commit v4 on v3

--- a/solution.py
+++ b/solution.py
@@ -6,6 +6,7 @@
 from jax.experimental import pallas as pl
 from jax.experimental.pallas import tpu as pltpu
 from jax.sharding import PartitionSpec as P
+
 
 LANES = 128
 AXES = ("cfd", "ac")
@@ -54,7 +55,7 @@
 
 
 def outgoing(order, surface, normals, direct, high):
-    comps, blocks, rows, steps = surface.shape
+    _, blocks, rows, steps = surface.shape
     shape = lambda lead: jax.ShapeDtypeStruct((lead, 2, rows, steps), jnp.bfloat16)
     return pl.pallas_call(
         functools.partial(outgoing_kernel, direct, high),
@@ -73,35 +74,50 @@
     )(*(pltpu.with_memory_space_constraint(x, pltpu.HBM) for x in (order, surface, normals)))
 
 
-def prepare_kernel(ranks, layout, observers_ref, weights_ref, select_ref, joined_ref):
-    taps, terms, observers, faces = weights_ref.shape
+def prepare_kernel(ranks, layout, observers_hbm, weights_hbm, select_ref, joined_ref, ids_ref, sems):
+    taps, terms, observers, faces = weights_hbm.shape
+    loads = [pltpu.make_async_copy(observers_hbm, ids_ref, sems.at[0])]
     for k in range(taps):
         for c in range(terms):
             at = (k * terms + c) * faces
-            joined_ref[:, at : at + faces] = weights_ref[k, c]
+            loads.append(
+                pltpu.make_async_copy(
+                    weights_hbm.at[k, c], joined_ref.at[:, pl.ds(at, faces)], sems.at[1 + k * terms + c]
+                )
+            )
+    for load in loads:
+        load.start()
+    loads[0].wait()
     each = observers // ranks
-    ids = observers_ref[...]
+    ids = ids_ref[...]
     local_row = lax.broadcasted_iota(jnp.int32, (each, observers), 0)
     for position, member in enumerate(layout):
         base = distance_from_me(member) * each
         chosen = jnp.where(local_row == ids - base, 1.0, 0.0).astype(jnp.bfloat16)
         select_ref[position * each : (position + 1) * each, :] = chosen
+    for load in loads[1:]:
+        load.wait()
 
 
 def prepare(observers, weights, ranks, layout):
     taps, terms, count, faces = weights.shape
+    operands = (observers.reshape(1, -1), weights)
     return pl.pallas_call(
         functools.partial(prepare_kernel, ranks, layout),
         out_shape=(
             jax.ShapeDtypeStruct((count, count), jnp.bfloat16),
             jax.ShapeDtypeStruct((count, taps * terms * faces), jnp.bfloat16),
         ),
-        in_specs=[VMEM, VMEM],
+        in_specs=[HBM, HBM],
         out_specs=(VMEM, VMEM),
+        scratch_shapes=[
+            pltpu.VMEM((1, count), jnp.int32),
+            pltpu.SemaphoreType.DMA((1 + taps * terms,)),
+        ],
         cost_estimate=pl.CostEstimate(flops=2 * 10**9, bytes_accessed=10**7, transcendentals=0),
         compiler_params=params(24),
         name="prepare",
-    )(observers.reshape(1, -1), weights)
+    )(*(pltpu.with_memory_space_constraint(x, pltpu.HBM) for x in operands))
 
 
 def place_block(series_ref, distance, block):
@@ -210,6 +226,28 @@
     )(banded, select, *after)
 
 
+def total_kernel(keep_ref, got_ref, *refs):
+    moved_refs, out_refs = refs[: len(MIDDLE)], refs[-keep_ref.shape[3] :]
+    for z, out_ref in enumerate(out_refs):
+        total = keep_ref[:, 0, 0, z].astype(jnp.float32) + got_ref[:, 0, 0, z].astype(jnp.float32)
+        for moved_ref in moved_refs:
+            total = total + moved_ref[:, z].astype(jnp.float32)
+        out_ref[...] = total.astype(out_ref.dtype)
+
+
+def total_far(keep, got, moved, after):
+    shape = jax.ShapeDtypeStruct(keep.shape[:1] + keep.shape[4:], jnp.bfloat16)
+    half = keep.shape[3]
+    return pl.pallas_call(
+        total_kernel,
+        out_shape=(shape,) * half,
+        in_specs=[VMEM] * (2 + len(moved) + len(after)),
+        out_specs=(VMEM,) * half,
+        compiler_params=params(16),
+        name="total_far",
+    )(keep, got, *moved, *after)
+
+
 def swap(value, ranks, sides, rank_mask, side_mask=0):
     pairs = [
         (r * sides + s, (r ^ rank_mask) * sides + (s ^ side_mask)) for r in range(ranks) for s in range(sides)
@@ -226,13 +264,11 @@
     surface = surface_raw.reshape(comps, ranks, faces // ranks, steps)
     made = outgoing(block_map.reshape(1, ranks), surface, area_normals, direct, high)
     near, early = list(made[:direct]), list(made[direct:])
-    for z in range(direct - 1, 0, -1):
+    for z in range(1, direct):
         near[z] = swap(near[z], ranks, sides, 4 * z)
     for q in range(3, 0, -1):
         early[q] = swap(early[q], ranks, sides, q)
-    late = [
-        swap(jnp.stack([early[q][z - direct] for q in range(4)]), ranks, sides, 4 * z) for z in range(direct, high)
-    ]
+    late = [swap(jnp.stack([early[q][z - direct] for q in range(4)]), ranks, sides, 4 * z) for z in range(direct, high)]
     post = [swap(jnp.stack([near[z][q] for z in range(direct)]), ranks, sides, q) for q in range(1, 4)]
 
     taps, _, count, _ = kernel_weights.shape
@@ -258,26 +294,22 @@
         got = by_side(swap(send, ranks, sides, 1))
         keep = by_side(order_more(banded, select, keep_from, shape))
         total = lambda x, y: keep[:, y, x].astype(jnp.float32) + got[:, y, x].astype(jnp.float32)
-        return total(0, 0), [total(x, y).astype(jnp.bfloat16) for x, y in MIDDLE]
-
-    def over_middle(total, sends):
-        for (x, y), send in zip(MIDDLE, sends):
-            total = total + swap(send, ranks, sides, 2 * x, y).astype(jnp.float32)
-        return total
-
-    def over_z(result, total, zs):
-        for z in reversed(zs):
-            moved = total[:, z - zs[0]]
-            if z:
-                moved = swap(moved.astype(jnp.bfloat16), ranks, sides, 4 * z).astype(jnp.float32)
-            result = moved if result is None else result + moved
-        return result
-
-    far_total, far_sends = over_core(far_send, rows)
+        return keep, got, total(0, 0), [total(x, y).astype(jnp.bfloat16) for x, y in MIDDLE]
+
+    def over_middle(sends):
+        return [swap(send, ranks, sides, 2 * x, y) for (x, y), send in zip(MIDDLE, sends)]
+
+    keep, got, _, far_sends = over_core(far_send, rows)
     near_send = order_more(banded, select, 2 * rows, shape, far_sends)
-    near_total, near_sends = over_core(near_send, 3 * rows)
-    result = over_z(None, over_middle(far_total, far_sends), chunks[0])
-    result = over_z(result, over_middle(near_total, near_sends), chunks[1])
+    _, _, total, near_sends = over_core(near_send, 3 * rows)
+    moved = over_middle(far_sends)
+    far = total_far(keep, got, moved, near_sends)
+    for moved in over_middle(near_sends):
+        total = total + moved.astype(jnp.float32)
+    result = total[:, 0]
+    for z in range(high - 1, 0, -1):
+        send = far[z - half] if z >= half else total[:, z].astype(jnp.bfloat16)
+        result = result + swap(send, ranks, sides, 4 * z).astype(jnp.float32)
     out = result[0]
     for y in range(sides // 2 - 1, 0, -1):
         out = out + swap(result[y].astype(jnp.bfloat16), ranks, sides, 0, 2 * y).astype(jnp.float32)
@@ -293,6 +325,5 @@
         P(),
         P(),
     )
-    return jax.shard_map(
-        local, mesh=mesh, in_specs=placed, out_specs=P("cfd", "ac"), check_vma=False
-    )
+
+    return jax.shard_map(local, mesh=mesh, in_specs=placed, out_specs=P("cfd", "ac"), check_vma=False)

time: 60.3 us -> 58.4 us (0.968)
  local copies, waits for them, and re-layouts: 2.63 us -> 0.04 us
    unnamed x6 -> x2, local copies, waits for them, and re-layouts: 2.59 us -> 0.01 us
  transfers between devices with their start and end apart: 20 -> 20, of which waited for: 12 -> 13; matrix products, arithmetic and copies ran while one was open for 0% -> 0% of each run, Pallas kernels for 7% -> 8%
where the time goes in v4:
time: 58.4 us; the launch traced here: 58.3 us
  starting transfers between devices  22.6 us (39%)
  waiting for transfers between devices  20.6 us (35%)
  Pallas kernels  13.9 us (24%)
  other arithmetic  1.03 us (2%)
    ppermute x20, starting transfers between devices, swap(): return lax.ppermute(value, AXES, pairs)  22.6 us
    ppermute x20, waiting for transfers between devices, swap(): return lax.ppermute(value, AXES, pairs)  20.6 us
    pallas_call x1, Pallas kernels, bands(): pl.pallas_call(functools.partial(bands_kernel, taps, direct, high, first_...  6.22 us
    pallas_call x3, Pallas kernels, order_more(): pl.pallas_call(functools.partial(order_kernel, first_row), out_shape=shap...  3.77 us
    pallas_call x1, Pallas kernels, prepare(): pl.pallas_call(functools.partial(prepare_kernel, ranks, layout), out_shap...  2.19 us
    pallas_call x1, Pallas kernels, outgoing(): pl.pallas_call(functools.partial(outgoing_kernel, direct, high), out_shap...  1.6 us
  transfers between devices with their start and end apart: 20, of which 13 were waited for; matrix products, arithmetic and copies ran while one was open for 0% of the time, Pallas kernels for 8%

profile of v4, /device:TPU:0, one launch (start us, length us, event | category | flops | bytes accessed | tf_op | source)
XLA Modules:
  0.0 58.3 jit_solution(5681658245271410683)
XLA Ops:
  0.0 1.6 %outgoing.1 = (bf16[4,2,8,1024]{3,2,1,0:T(8,128)(2,1)S(1)}, bf16[4,2,8,1024]{3,2,1,0:T(8,128)(2,1)S(1)}, bf16[4,2,8,1024]{3,2,1,0:T(8,128)(2,1)S(1)}, bf16[1,2,8...) custom-call(s32[1,16]{1,0:T(1,128)} %bitcast.48, ...), custom_call_target="tpu_custom_call" | custom-call | tf_op jit(solution)/shard_map/outgoing/pallas_call | solution.py:60
  1.6 0.6 collective-permute-start.5
  2.2 2.6 %collective-permute-start.6 = (bf16[1,2,8,1024]{3,2,1,0:T(8,128)(2,1)S(1)}, bf16[1,2,8,1024]{3,2,1,0:T(8,128)(2,1)S(1)}, u32[]{:S(2)}, u32[]{:S(2)}) collective-permute-start(bf16[1,2,8,1024]{3,2,1,0:T(8,128)(2,1)S(1)} %get-tuple-element.25), channel_id=1, source_target_pairs={{0,4},{1,5},{2,6},{3,7},{4,0},{5,1},{6,2},{7,3},{8,12},{9,13},{10,... | collective-permute-start | bytes 98312 | tf_op jit(solution)/shard_map/ppermute | solution.py:255
  4.8 1.8 %collective-permute-start = (bf16[4,2,8,1024]{3,2,1,0:T(8,128)(2,1)S(1)}, bf16[4,2,8,1024]{3,2,1,0:T(8,128)(2,1)S(1)}, u32[]{:S(2)}, u32[]{:S(2)}) collective-permute-start(bf16[4,2,8,1024]{3,2,1,0:T(8,128)(2,1)S(1)} %get-tuple-element.21), channel_id=1, source_target_pairs={{0,8},{1,9},{2,10},{3,11},{4,12},{5,13},{6,14},{7,15},{8,0},{9,1},... | collective-permute-start | bytes 393224 | tf_op jit(solution)/shard_map/ppermute | solution.py:255
  6.6 2.6 %collective-permute-start.1 = (bf16[4,2,8,1024]{3,2,1,0:T(8,128)(2,1)S(1)}, bf16[4,2,8,1024]{3,2,1,0:T(8,128)(2,1)S(1)}, u32[]{:S(2)}, u32[]{:S(2)}) collective-permute-start(bf16[4,2,8,1024]{3,2,1,0:T(8,128)(2,1)S(1)} %get-tuple-element.22), channel_id=1, source_target_pairs={{0,16},{1,17},{2,18},{3,19},{4,20},{5,21},{6,22},{7,23},{8,24},{9,... | collective-permute-start | bytes 393224 | tf_op jit(solution)/shard_map/ppermute | solution.py:255
  9.2 2.5 %collective-permute-start.8 = (bf16[4,2,8,1024]{3,2,1,0:T(8,128)(2,1)S(1)}, bf16[4,2,8,1024]{3,2,1,0:T(8,128)(2,1)S(1)}, u32[]{:S(2)}, u32[]{:S(2)}) collective-permute-start(bf16[4,2,8,1024]{3,2,1,0:T(8,128)(2,1)S(1)} %pad_maximum_fusion), channel_id=1, source_target_pairs={{0,24},{1,25},{2,26},{3,27},{4,28},{5,29},{6,30},{7,31},{8,16},{9,... | collective-permute-start | bytes 393224 | tf_op jit(solution)/shard_map/ppermute | solution.py:255
  11.8 0.9 %collective-permute-done.refs_1_ = bf16[4,2,8,1024]{3,2,1,0:T(8,128)(2,1)S(1)} collective-permute-done((bf16[4,2,8,1024]{3,2,1,0:T(8,128)(2,1)S(1)}, bf16[4,2,8,1024]{3,2,1,0:T(8,128)(2,1)S(1)}, u32[]{:S(2)}, u32[]{:S(2)}) %collective-permute-start) | collective-permute-done | bytes 131104 | tf_op jit(solution)/shard_map/ppermute | solution.py:255
  12.7 6.8 %collective-permute-done.1.refs_2_ = bf16[4,2,8,1024]{3,2,1,0:T(8,128)(2,1)S(1)} collective-permute-done((bf16[4,2,8,1024]{3,2,1,0:T(8,128)(2,1)S(1)}, bf16[4,2,8,1024]{3,2,1,0:T(8,128)(2,1)S(1)}, u32[]{:S(2)}, u32[]{:S(2)}) %collective-permute-start.1) | collective-permute-done | bytes 131104 | tf_op jit(solution)/shard_map/ppermute | solution.py:255
  19.7 1.6 %collective-permute-start.3 = (bf16[3,2,8,1024]{3,2,1,0:T(8,128)(2,1)S(1)}, bf16[3,2,8,1024]{3,2,1,0:T(8,128)(2,1)S(1)}, u32[]{:S(2)}, u32[]{:S(2)}) collective-permute-start(bf16[3,2,8,1024]{3,2,1,0:T(8,128)(2,1)S(1)} %pad_maximum_fusion.2), channel_id=1, source_target_pairs={{0,4},{1,5},{2,6},{3,7},{4,0},{5,1},{6,2},{7,3},{8,12},{9,13},{10,... | collective-permute-start | bytes 294920 | tf_op jit(solution)/shard_map/ppermute | solution.py:255
  21.2 0.4 collective-permute-start.4
  21.7 2.2 %prepare.1 = (bf16[2048,2048]{1,0:T(8,128)(2,1)S(1)}, bf16[2048,768]{1,0:T(8,128)(2,1)S(1)}) custom-call(s32[1,2048]{1,0:T(1,128)} %bitcast.49, bf16[2,3,2048,128]{3,2,1,0:T(8,128)(2,1)} %weights_hbm.1), custom_call_target="tpu_custom_call" | custom-call | flops 2000000000 | bytes 10000000 | tf_op jit(solution)/shard_map/prepare/pallas_call | solution.py:105
  23.9 1.5 %collective-permute-done.3.refs_4_ = bf16[3,2,8,1024]{3,2,1,0:T(8,128)(2,1)S(1)} collective-permute-done((bf16[3,2,8,1024]{3,2,1,0:T(8,128)(2,1)S(1)}, bf16[3,2,8,1024]{3,2,1,0:T(8,128)(2,1)S(1)}, u32[]{:S(2)}, u32[]{:S(2)}) %collective-permute-start.3) | collective-permute-done | bytes 98336 | tf_op jit(solution)/shard_map/ppermute | solution.py:255
  25.4 1.1 %collective-permute-done.4.refs_5_ = bf16[3,2,8,1024]{3,2,1,0:T(8,128)(2,1)S(1)} collective-permute-done((bf16[3,2,8,1024]{3,2,1,0:T(8,128)(2,1)S(1)}, bf16[3,2,8,1024]{3,2,1,0:T(8,128)(2,1)S(1)}, u32[]{:S(2)}, u32[]{:S(2)}) %collective-permute-start.4) | collective-permute-done | bytes 98336 | tf_op jit(solution)/shard_map/ppermute | solution.py:255
  26.5 6.2 %bands.1 = (bf16[2048,512]{1,0:T(8,128)(2,1)S(1)}, bf16[2,512,256]{2,1,0:T(8,128)(2,1)S(1)}) custom-call(s32[16]{0:T(128)S(1)} %copy-done, bf16[2048,768]{1,0:T(8,128)(2,1)S(1)} %get-tuple-element.18.joined_ref, bf16[2048,2048]{1,0:T(8,128)(2,1)S(1)} %get-tuple-element.19.select_ref, bf16[4,2,8,1024]{3,2,1,0:T(8,128)(2,1)S(1)} %get-tuple-element.20.refs_0_, ...), custom_call_target="tpu_custom_call" | custom-call | flops 4000000000 | bytes 10000000 | tf_op jit(solution)/shard_map/bands/pallas_call | solution.py:197
  32.8 0.4 collective-permute-start.9
  33.1 1.3 %order.4 = bf16[2,512,256]{2,1,0:T(8,128)(2,1)S(1)} custom-call(bf16[2048,512]{1,0:T(8,128)(2,1)S(1)} %get-tuple-element.27.banded_ref, bf16[2048,2048]{1,0:T(8,128)(2,1)S(1)} %get-tuple-element.19.select_ref), custom_call_target="tpu_custom_call" | custom-call | flops 1000000000 | bytes 5000000 | tf_op jit(solution)/shard_map/order/pallas_call | solution.py:218
  34.9 1.3 %order.5 = bf16[2,512,256]{2,1,0:T(8,128)(2,1)S(1)} custom-call(bf16[2048,512]{1,0:T(8,128)(2,1)S(1)} %get-tuple-element.27.banded_ref, bf16[2048,2048]{1,0:T(8,128)(2,1)S(1)} %get-tuple-element.19.select_ref, bf16[1,2,128,256]{3,2,1,0:T(8,128)(2,1)S(1)} %get-tuple-element.36.refs_0_, bf16[1,2,128,256]{3,2,1,0:T(8,128)(2,1)S(1)} %get-tuple-element.35.refs_1_, ...), custom_call_target="tpu_custom_call" | custom-call | flops 1000000000 | bytes 5000000 | tf_op jit(solution)/shard_map/order/pallas_call | solution.py:218
  36.5 1.3 %order.3 = bf16[2,512,256]{2,1,0:T(8,128)(2,1)S(1)} custom-call(bf16[2048,512]{1,0:T(8,128)(2,1)S(1)} %get-tuple-element.27.banded_ref, bf16[2048,2048]{1,0:T(8,128)(2,1)S(1)} %get-tuple-element.19.select_ref), custom_call_target="tpu_custom_call" | custom-call | flops 1000000000 | bytes 5000000 | tf_op jit(solution)/shard_map/order/pallas_call | solution.py:218
  37.8 1.6 %collective-permute-start.16 = (bf16[1,2,128,256]{3,2,1,0:T(8,128)(2,1)S(1)}, bf16[1,2,128,256]{3,2,1,0:T(8,128)(2,1)S(1)}, u32[]{:S(2)}, u32[]{:S(2)}) collective-permute-start(bf16[1,2,128,256]{3,2,1,0:T(8,128)(2,1)S(1)} %get-tuple-element.34.refs_2_), channel_id=1, source_target_pairs={{0,1},{1,0},{2,3},{3,2},{4,5},{5,4},{6,7},{7,6},{8,9},{9,8},{10,11... | collective-permute-start | bytes 393224 | tf_op jit(solution)/shard_map/ppermute | solution.py:255
  39.4 1.5 %collective-permute-start.15 = (bf16[1,2,128,256]{3,2,1,0:T(8,128)(2,1)S(1)}, bf16[1,2,128,256]{3,2,1,0:T(8,128)(2,1)S(1)}, u32[]{:S(2)}, u32[]{:S(2)}) collective-permute-start(bf16[1,2,128,256]{3,2,1,0:T(8,128)(2,1)S(1)} %get-tuple-element.35.refs_1_), channel_id=1, source_target_pairs={{0,4},{1,5},{2,6},{3,7},{4,0},{5,1},{6,2},{7,3},{8,12},{9,13},{10,... | collective-permute-start | bytes 393224 | tf_op jit(solution)/shard_map/ppermute | solution.py:255
  40.9 0.5 collective-permute-start.14
  41.4 2.5 %collective-permute-start.11 = (bf16[1,2,128,256]{3,2,1,0:T(8,128)(2,1)S(1)}, bf16[1,2,128,256]{3,2,1,0:T(8,128)(2,1)S(1)}, u32[]{:S(2)}, u32[]{:S(2)}) collective-permute-start(bf16[1,2,128,256]{3,2,1,0:T(8,128)(2,1)S(1)} %get-tuple-element.31.refs_3_), channel_id=1, source_target_pairs={{0,5},{1,4},{2,7},{3,6},{4,1},{5,0},{6,3},{7,2},{8,13},{9,12},{10,... | collective-permute-start | bytes 393224 | tf_op jit(solution)/shard_map/ppermute | solution.py:255
  44.0 0.5 collective-permute-start.13
  44.4 0.5 collective-permute-start.12
  45.0 0.8 %collective-permute-done.15.refs_1_ = bf16[1,2,128,256]{3,2,1,0:T(8,128)(2,1)S(1)} collective-permute-done((bf16[1,2,128,256]{3,2,1,0:T(8,128)(2,1)S(1)}, bf16[1,2,128,256]{3,2,1,0:T(8,128)(2,1)S(1)}, u32[]{:S(2)}, u32[]{:S(2)}) %collective-permute-start.15) | collective-permute-done | bytes 131104 | tf_op jit(solution)/shard_map/ppermute | solution.py:255
  45.7 2.5 %collective-permute-done.14.refs_0_ = bf16[1,2,128,256]{3,2,1,0:T(8,128)(2,1)S(1)} collective-permute-done((bf16[1,2,128,256]{3,2,1,0:T(8,128)(2,1)S(1)}, bf16[1,2,128,256]{3,2,1,0:T(8,128)(2,1)S(1)}, u32[]{:S(2)}, u32[]{:S(2)}) %collective-permute-start.14) | collective-permute-done | bytes 131104 | tf_op jit(solution)/shard_map/ppermute | solution.py:255
  48.3 2.5 %collective-permute-start.17 = (bf16[1,128,256]{2,1,0:T(8,128)(2,1)S(1)}, bf16[1,128,256]{2,1,0:T(8,128)(2,1)S(1)}, u32[]{:S(2)}, u32[]{:S(2)}) collective-permute-start(bf16[1,128,256]{2,1,0:T(8,128)(2,1)S(1)} %get-tuple-element.29), channel_id=1, source_target_pairs={{0,24},{1,25},{2,26},{3,27},{4,28},{5,29},{6,30},{7,31},{8,16},{9,... | collective-permute-start | bytes 196616 | tf_op jit(solution)/shard_map/ppermute | solution.py:255
  51.0 2.1 %collective-permute-done.13 = bf16[1,2,128,256]{3,2,1,0:T(8,128)(2,1)S(1)} collective-permute-done((bf16[1,2,128,256]{3,2,1,0:T(8,128)(2,1)S(1)}, bf16[1,2,128,256]{3,2,1,0:T(8,128)(2,1)S(1)}, u32[]{:S(2)}, u32[]{:S(2)}) %collective-permute-start.13) | collective-permute-done | bytes 131104 | tf_op jit(solution)/shard_map/ppermute | solution.py:255
  53.4 1.2 %collective-permute-done.17 = bf16[1,128,256]{2,1,0:T(8,128)(2,1)S(1)} collective-permute-done((bf16[1,128,256]{2,1,0:T(8,128)(2,1)S(1)}, bf16[1,128,256]{2,1,0:T(8,128)(2,1)S(1)}, u32[]{:S(2)}, u32[]{:S(2)}) %collective-permute-start.17) | collective-permute-done | bytes 65568 | tf_op jit(solution)/shard_map/ppermute | solution.py:255
  54.5 1.5 %collective-permute-done.18 = bf16[1,128,256]{2,1,0:T(8,128)(2,1)S(1)} collective-permute-done((bf16[1,128,256]{2,1,0:T(8,128)(2,1)S(1)}, bf16[1,128,256]{2,1,0:T(8,128)(2,1)S(1)}, u32[]{:S(2)}, u32[]{:S(2)}) %collective-permute-start.18) | collective-permute-done | bytes 65568 | tf_op jit(solution)/shard_map/ppermute | solution.py:255
  56.0 1.6 %collective-permute-done.19 = bf16[1,128,256]{2,1,0:T(8,128)(2,1)S(1)} collective-permute-done((bf16[1,128,256]{2,1,0:T(8,128)(2,1)S(1)}, bf16[1,128,256]{2,1,0:T(8,128)(2,1)S(1)}, u32[]{:S(2)}, u32[]{:S(2)}) %collective-permute-start.19) | collective-permute-done | bytes 65568 | tf_op jit(solution)/shard_map/ppermute | solution.py:255
  57.6 0.7 %fusion.11 = f32[128,256]{1,0:T(8,128)} fusion(f32[1,2,128,256]{3,2,1,0:T(8,128)S(1)} %fusion.1, bf16[1,128,256]{2,1,0:T(8,128)(2,1)S(1)} %collective-permute-done.19, bf16[1,128,256]{2,1,0:T(8,128)(2,1)S(1)} %collective-permute-done.18, bf16[1,128,256]{2,1,0:T(8,128)(2,1)S(1)} %collective-permute-done.17), kind=kLoop, calls=%fused_computation.20 | loop fusion | flops 196608 | bytes 458752 | tf_op jit(solution)/shard_map/squeeze | solution.py:313
  (29 shorter events, 1.6 us)
Async XLA Ops:
  1.6 7.6 %collective-permute-start.5 = (bf16[1,2,8,1024]{3,2,1,0:T(8,128)(2,1)S(1)}, bf16[1,2,8,1024]{3,2,1,0:T(8,128)(2,1)S(1)}, u32[]{:S(2)}, u32[]{:S(2)}) collective-permute-start(bf16[1,2,8,1024]{3,2,1,0:T(8,128)(2,1)S(1)} %get-tuple-element.24), channel_id=1, source_target_pairs={{0,2},{1,3},{2,0},{3,1},{4,6},{5,7},{6,4},{7,5},{8,10},{9,11},{10,... | collective-permute-start | bytes 98312 | tf_op jit(solution)/shard_map/ppermute | solution.py:255
  2.2 7.0 %collective-permute-start.6 = (bf16[1,2,8,1024]{3,2,1,0:T(8,128)(2,1)S(1)}, bf16[1,2,8,1024]{3,2,1,0:T(8,128)(2,1)S(1)}, u32[]{:S(2)}, u32[]{:S(2)}) collective-permute-start(bf16[1,2,8,1024]{3,2,1,0:T(8,128)(2,1)S(1)} %get-tuple-element.25), channel_id=1, source_target_pairs={{0,4},{1,5},{2,6},{3,7},{4,0},{5,1},{6,2},{7,3},{8,12},{9,13},{10,... | collective-permute-start | bytes 98312 | tf_op jit(solution)/shard_map/ppermute | solution.py:255
  4.7 4.5 %collective-permute-start.7 = (bf16[1,2,8,1024]{3,2,1,0:T(8,128)(2,1)S(1)}, bf16[1,2,8,1024]{3,2,1,0:T(8,128)(2,1)S(1)}, u32[]{:S(2)}, u32[]{:S(2)}) collective-permute-start(bf16[1,2,8,1024]{3,2,1,0:T(8,128)(2,1)S(1)} %get-tuple-element.26), channel_id=1, source_target_pairs={{0,6},{1,7},{2,4},{3,5},{4,2},{5,3},{6,0},{7,1},{8,14},{9,15},{10,... | collective-permute-start | bytes 98312 | tf_op jit(solution)/shard_map/ppermute | solution.py:255
  4.8 7.9 %collective-permute-start = (bf16[4,2,8,1024]{3,2,1,0:T(8,128)(2,1)S(1)}, bf16[4,2,8,1024]{3,2,1,0:T(8,128)(2,1)S(1)}, u32[]{:S(2)}, u32[]{:S(2)}) collective-permute-start(bf16[4,2,8,1024]{3,2,1,0:T(8,128)(2,1)S(1)} %get-tuple-element.21), channel_id=1, source_target_pairs={{0,8},{1,9},{2,10},{3,11},{4,12},{5,13},{6,14},{7,15},{8,0},{9,1},... | collective-permute-start | bytes 393224 | tf_op jit(solution)/shard_map/ppermute | solution.py:255
  6.6 12.9 %collective-permute-start.1 = (bf16[4,2,8,1024]{3,2,1,0:T(8,128)(2,1)S(1)}, bf16[4,2,8,1024]{3,2,1,0:T(8,128)(2,1)S(1)}, u32[]{:S(2)}, u32[]{:S(2)}) collective-permute-start(bf16[4,2,8,1024]{3,2,1,0:T(8,128)(2,1)S(1)} %get-tuple-element.22), channel_id=1, source_target_pairs={{0,16},{1,17},{2,18},{3,19},{4,20},{5,21},{6,22},{7,23},{8,24},{9,... | collective-permute-start | bytes 393224 | tf_op jit(solution)/shard_map/ppermute | solution.py:255
  9.2 14.6 %collective-permute-start.8 = (bf16[4,2,8,1024]{3,2,1,0:T(8,128)(2,1)S(1)}, bf16[4,2,8,1024]{3,2,1,0:T(8,128)(2,1)S(1)}, u32[]{:S(2)}, u32[]{:S(2)}) collective-permute-start(bf16[4,2,8,1024]{3,2,1,0:T(8,128)(2,1)S(1)} %pad_maximum_fusion), channel_id=1, source_target_pairs={{0,24},{1,25},{2,26},{3,27},{4,28},{5,29},{6,30},{7,31},{8,16},{9,... | collective-permute-start | bytes 393224 | tf_op jit(solution)/shard_map/ppermute | solution.py:255
  19.6 4.3 %collective-permute-start.2 = (bf16[3,2,8,1024]{3,2,1,0:T(8,128)(2,1)S(1)}, bf16[3,2,8,1024]{3,2,1,0:T(8,128)(2,1)S(1)}, u32[]{:S(2)}, u32[]{:S(2)}) collective-permute-start(bf16[3,2,8,1024]{3,2,1,0:T(8,128)(2,1)S(1)} %pad_maximum_fusion.1), channel_id=1, source_target_pairs={{0,2},{1,3},{2,0},{3,1},{4,6},{5,7},{6,4},{7,5},{8,10},{9,11},{10,... | collective-permute-start | bytes 294920 | tf_op jit(solution)/shard_map/ppermute | solution.py:255
  19.7 5.7 %collective-permute-start.3 = (bf16[3,2,8,1024]{3,2,1,0:T(8,128)(2,1)S(1)}, bf16[3,2,8,1024]{3,2,1,0:T(8,128)(2,1)S(1)}, u32[]{:S(2)}, u32[]{:S(2)}) collective-permute-start(bf16[3,2,8,1024]{3,2,1,0:T(8,128)(2,1)S(1)} %pad_maximum_fusion.2), channel_id=1, source_target_pairs={{0,4},{1,5},{2,6},{3,7},{4,0},{5,1},{6,2},{7,3},{8,12},{9,13},{10,... | collective-permute-start | bytes 294920 | tf_op jit(solution)/shard_map/ppermute | solution.py:255
  21.2 5.3 %collective-permute-start.4 = (bf16[3,2,8,1024]{3,2,1,0:T(8,128)(2,1)S(1)}, bf16[3,2,8,1024]{3,2,1,0:T(8,128)(2,1)S(1)}, u32[]{:S(2)}, u32[]{:S(2)}) collective-permute-start(bf16[3,2,8,1024]{3,2,1,0:T(8,128)(2,1)S(1)} %pad_maximum_fusion.3), channel_id=1, source_target_pairs={{0,6},{1,7},{2,4},{3,5},{4,2},{5,3},{6,0},{7,1},{8,14},{9,15},{10,... | collective-permute-start | bytes 294920 | tf_op jit(solution)/shard_map/ppermute | solution.py:255
  21.6 4.9 %copy-start = (s32[16]{0:T(128)S(1)}, s32[16]{0:T(128)}, u32[]{:S(2)}) copy-start(s32[16]{0:T(128)} %lags_ref.1) | copy-start | bytes 196
  32.8 2.0 %collective-permute-start.9 = (bf16[2,512,256]{2,1,0:T(8,128)(2,1)S(1)}, bf16[2,512,256]{2,1,0:T(8,128)(2,1)S(1)}, u32[]{:S(2)}, u32[]{:S(2)}) collective-permute-start(bf16[2,512,256]{2,1,0:T(8,128)(2,1)S(1)} %get-tuple-element.28), channel_id=1, source_target_pairs={{0,2},{1,3},{2,0},{3,1},{4,6},{5,7},{6,4},{7,5},{8,10},{9,11},{10,... | collective-permute-start | bytes 1572872 | tf_op jit(solution)/shard_map/ppermute | solution.py:255
  36.1 5.2 %collective-permute-start.10 = (bf16[2,512,256]{2,1,0:T(8,128)(2,1)S(1)}, bf16[2,512,256]{2,1,0:T(8,128)(2,1)S(1)}, u32[]{:S(2)}, u32[]{:S(2)}) collective-permute-start(bf16[2,512,256]{2,1,0:T(8,128)(2,1)S(1)} %order.5), channel_id=1, source_target_pairs={{0,2},{1,3},{2,0},{3,1},{4,6},{5,7},{6,4},{7,5},{8,10},{9,11},{10,... | collective-permute-start | bytes 1572872 | tf_op jit(solution)/shard_map/ppermute | solution.py:255
  37.8 6.7 %collective-permute-start.16 = (bf16[1,2,128,256]{3,2,1,0:T(8,128)(2,1)S(1)}, bf16[1,2,128,256]{3,2,1,0:T(8,128)(2,1)S(1)}, u32[]{:S(2)}, u32[]{:S(2)}) collective-permute-start(bf16[1,2,128,256]{3,2,1,0:T(8,128)(2,1)S(1)} %get-tuple-element.34.refs_2_), channel_id=1, source_target_pairs={{0,1},{1,0},{2,3},{3,2},{4,5},{5,4},{6,7},{7,6},{8,9},{9,8},{10,11... | collective-permute-start | bytes 393224 | tf_op jit(solution)/shard_map/ppermute | solution.py:255
  39.4 6.4 %collective-permute-start.15 = (bf16[1,2,128,256]{3,2,1,0:T(8,128)(2,1)S(1)}, bf16[1,2,128,256]{3,2,1,0:T(8,128)(2,1)S(1)}, u32[]{:S(2)}, u32[]{:S(2)}) collective-permute-start(bf16[1,2,128,256]{3,2,1,0:T(8,128)(2,1)S(1)} %get-tuple-element.35.refs_1_), channel_id=1, source_target_pairs={{0,4},{1,5},{2,6},{3,7},{4,0},{5,1},{6,2},{7,3},{8,12},{9,13},{10,... | collective-permute-start | bytes 393224 | tf_op jit(solution)/shard_map/ppermute | solution.py:255
  40.9 7.4 %collective-permute-start.14 = (bf16[1,2,128,256]{3,2,1,0:T(8,128)(2,1)S(1)}, bf16[1,2,128,256]{3,2,1,0:T(8,128)(2,1)S(1)}, u32[]{:S(2)}, u32[]{:S(2)}) collective-permute-start(bf16[1,2,128,256]{3,2,1,0:T(8,128)(2,1)S(1)} %get-tuple-element.36.refs_0_), channel_id=1, source_target_pairs={{0,5},{1,4},{2,7},{3,6},{4,1},{5,0},{6,3},{7,2},{8,13},{9,12},{10,... | collective-permute-start | bytes 393224 | tf_op jit(solution)/shard_map/ppermute | solution.py:255
  41.4 9.6 %collective-permute-start.11 = (bf16[1,2,128,256]{3,2,1,0:T(8,128)(2,1)S(1)}, bf16[1,2,128,256]{3,2,1,0:T(8,128)(2,1)S(1)}, u32[]{:S(2)}, u32[]{:S(2)}) collective-permute-start(bf16[1,2,128,256]{3,2,1,0:T(8,128)(2,1)S(1)} %get-tuple-element.31.refs_3_), channel_id=1, source_target_pairs={{0,5},{1,4},{2,7},{3,6},{4,1},{5,0},{6,3},{7,2},{8,13},{9,12},{10,... | collective-permute-start | bytes 393224 | tf_op jit(solution)/shard_map/ppermute | solution.py:255
  44.0 9.1 %collective-permute-start.13 = (bf16[1,2,128,256]{3,2,1,0:T(8,128)(2,1)S(1)}, bf16[1,2,128,256]{3,2,1,0:T(8,128)(2,1)S(1)}, u32[]{:S(2)}, u32[]{:S(2)}) collective-permute-start(bf16[1,2,128,256]{3,2,1,0:T(8,128)(2,1)S(1)} %get-tuple-element.32.refs_5_), channel_id=1, source_target_pairs={{0,1},{1,0},{2,3},{3,2},{4,5},{5,4},{6,7},{7,6},{8,9},{9,8},{10,11... | collective-permute-start | bytes 393224 | tf_op jit(solution)/shard_map/ppermute | solution.py:255
  44.4 8.7 %collective-permute-start.12 = (bf16[1,2,128,256]{3,2,1,0:T(8,128)(2,1)S(1)}, bf16[1,2,128,256]{3,2,1,0:T(8,128)(2,1)S(1)}, u32[]{:S(2)}, u32[]{:S(2)}) collective-permute-start(bf16[1,2,128,256]{3,2,1,0:T(8,128)(2,1)S(1)} %get-tuple-element.33.refs_4_), channel_id=1, source_target_pairs={{0,4},{1,5},{2,6},{3,7},{4,0},{5,1},{6,2},{7,3},{8,12},{9,13},{10,... | collective-permute-start | bytes 393224 | tf_op jit(solution)/shard_map/ppermute | solution.py:255
  48.3 6.2 %collective-permute-start.17 = (bf16[1,128,256]{2,1,0:T(8,128)(2,1)S(1)}, bf16[1,128,256]{2,1,0:T(8,128)(2,1)S(1)}, u32[]{:S(2)}, u32[]{:S(2)}) collective-permute-start(bf16[1,128,256]{2,1,0:T(8,128)(2,1)S(1)} %get-tuple-element.29), channel_id=1, source_target_pairs={{0,24},{1,25},{2,26},{3,27},{4,28},{5,29},{6,30},{7,31},{8,16},{9,... | collective-permute-start | bytes 196616 | tf_op jit(solution)/shard_map/ppermute | solution.py:255
  50.9 5.2 %collective-permute-start.18 = (bf16[1,128,256]{2,1,0:T(8,128)(2,1)S(1)}, bf16[1,128,256]{2,1,0:T(8,128)(2,1)S(1)}, u32[]{:S(2)}, u32[]{:S(2)}) collective-permute-start(bf16[1,128,256]{2,1,0:T(8,128)(2,1)S(1)} %get-tuple-element.30), channel_id=1, source_target_pairs={{0,16},{1,17},{2,18},{3,19},{4,20},{5,21},{6,22},{7,23},{8,24},{9,... | collective-permute-start | bytes 196616 | tf_op jit(solution)/shard_map/ppermute | solution.py:255
  53.3 4.3 %collective-permute-start.19 = (bf16[1,128,256]{2,1,0:T(8,128)(2,1)S(1)}, bf16[1,128,256]{2,1,0:T(8,128)(2,1)S(1)}, u32[]{:S(2)}, u32[]{:S(2)}) collective-permute-start(bf16[1,128,256]{2,1,0:T(8,128)(2,1)S(1)} %fusion.12), channel_id=1, source_target_pairs={{0,8},{1,9},{2,10},{3,11},{4,12},{5,13},{6,14},{7,15},{8,0},{9,1},... | collective-permute-start | bytes 196616 | tf_op jit(solution)/shard_map/ppermute | solution.py:255

commit v5 on v4

--- a/solution.py
+++ b/solution.py
@@ -184,7 +184,7 @@
         banded_ref[at, :] = turned[:, :out_len].astype(jnp.bfloat16)
         return carry
 
-    lax.fori_loop(0, bands, one_band, 0, unroll=4)
+    lax.fori_loop(0, bands, one_band, 0, unroll=True)
     order_rows(select_ref, first_row, banded_ref, send_ref)
 
 
@@ -274,23 +274,24 @@
     taps, _, count, _ = kernel_weights.shape
     out_len = steps // 2
     each = count // ranks
-    half = high // 2
-    chunks = (range(half, high), range(half))
+    chunks = (range(1, high), range(1))
     layout = [(z * 2 + x) * 2 + c for zs in chunks for c in (1, 0) for x in range(2) for z in zs]
     parts = sides if out_len // sides % LANES == 0 else 1
-    rows = half * 2 * each
-    shape = jax.ShapeDtypeStruct((parts, rows, out_len // parts), jnp.bfloat16)
+    far_rows, near_rows = [len(zs) * 2 * each for zs in chunks]
+    far_shape, near_shape = [
+        jax.ShapeDtypeStruct((parts, rows, out_len // parts), jnp.bfloat16) for rows in (far_rows, near_rows)
+    ]
     select, joined = prepare(band_observers, kernel_weights, ranks, layout)
-    banded, far_send = bands(band_lags, near, post, late, joined, select, 0, taps, shape)
+    banded, far_send = bands(band_lags, near, post, late, joined, select, 0, taps, far_shape)
     which = jnp.bitwise_xor(lax.iota(jnp.int32, sides), lax.axis_index("ac"))
 
     def by_side(value):
         if parts != sides:
-            value = value.reshape(rows, sides, out_len // sides)
+            value = value.reshape(-1, sides, out_len // sides)
             value = jnp.transpose(jnp.take(value, which, axis=1), (1, 0, 2))
-        return value.reshape(sides // 2, 2, 2, half, each, out_len // sides)
-
-    def over_core(send, keep_from):
+        return value.reshape(sides // 2, 2, 2, -1, each, out_len // sides)
+
+    def over_core(send, keep_from, shape):
         got = by_side(swap(send, ranks, sides, 1))
         keep = by_side(order_more(banded, select, keep_from, shape))
         total = lambda x, y: keep[:, y, x].astype(jnp.float32) + got[:, y, x].astype(jnp.float32)
@@ -299,17 +300,16 @@
     def over_middle(sends):
         return [swap(send, ranks, sides, 2 * x, y) for (x, y), send in zip(MIDDLE, sends)]
 
-    keep, got, _, far_sends = over_core(far_send, rows)
-    near_send = order_more(banded, select, 2 * rows, shape, far_sends)
-    _, _, total, near_sends = over_core(near_send, 3 * rows)
+    keep, got, _, far_sends = over_core(far_send, far_rows, far_shape)
+    near_send = order_more(banded, select, 2 * far_rows, near_shape, far_sends)
+    _, _, total, near_sends = over_core(near_send, 2 * far_rows + near_rows, near_shape)
     moved = over_middle(far_sends)
     far = total_far(keep, got, moved, near_sends)
     for moved in over_middle(near_sends):
         total = total + moved.astype(jnp.float32)
     result = total[:, 0]
     for z in range(high - 1, 0, -1):
-        send = far[z - half] if z >= half else total[:, z].astype(jnp.bfloat16)
-        result = result + swap(send, ranks, sides, 4 * z).astype(jnp.float32)
+        result = result + swap(far[z - 1], ranks, sides, 4 * z).astype(jnp.float32)
     out = result[0]
     for y in range(sides // 2 - 1, 0, -1):
         out = out + swap(result[y].astype(jnp.bfloat16), ranks, sides, 0, 2 * y).astype(jnp.float32)

time: 58.4 us -> 62.9 us (1.077)
  waiting for transfers between devices: 20.6 us -> 23.4 us
  starting transfers between devices: 22.6 us -> 25.1 us
  Pallas kernels: 13.9 us -> 13.1 us
    ppermute x20, waiting for transfers between devices: 20.6 us -> 23.4 us  [swap(): return lax.ppermute(value, AXES, pairs)]
    ppermute x20, starting transfers between devices: 22.6 us -> 25.1 us  [swap(): return lax.ppermute(value, AXES, pairs)]
  transfers between devices with their start and end apart: 20 -> 20, of which waited for: 13 -> 11; matrix products, arithmetic and copies ran while one was open for 0% -> 0% of each run, Pallas kernels for 8% -> 8%
where the time goes in v5:
time: 62.9 us; the launch traced here: 62.8 us
  starting transfers between devices  25.1 us (40%)
  waiting for transfers between devices  23.4 us (37%)
  Pallas kernels  13.1 us (21%)
  other arithmetic  1 us (2%)
    ppermute x20, starting transfers between devices, swap(): return lax.ppermute(value, AXES, pairs)  25.1 us
    ppermute x20, waiting for transfers between devices, swap(): return lax.ppermute(value, AXES, pairs)  23.4 us
    pallas_call x1, Pallas kernels, bands(): pl.pallas_call(functools.partial(bands_kernel, taps, direct, high, first_...  5.94 us
    pallas_call x3, Pallas kernels, order_more(): pl.pallas_call(functools.partial(order_kernel, first_row), out_shape=shap...  3.24 us
    pallas_call x1, Pallas kernels, prepare(): pl.pallas_call(functools.partial(prepare_kernel, ranks, layout), out_shap...  2.19 us
    pallas_call x1, Pallas kernels, outgoing(): pl.pallas_call(functools.partial(outgoing_kernel, direct, high), out_shap...  1.6 us
  transfers between devices with their start and end apart: 20, of which 11 were waited for; matrix products, arithmetic and copies ran while one was open for 0% of the time, Pallas kernels for 8%

profile of v5, /device:TPU:0, one launch (start us, length us, event | category | flops | bytes accessed | tf_op | source)
XLA Modules:
  0.0 62.8 jit_solution(14374554878065944024)
XLA Ops:
  0.0 1.6 %outgoing.1 = (bf16[4,2,8,1024]{3,2,1,0:T(8,128)(2,1)S(1)}, bf16[4,2,8,1024]{3,2,1,0:T(8,128)(2,1)S(1)}, bf16[4,2,8,1024]{3,2,1,0:T(8,128)(2,1)S(1)}, bf16[1,2,8...) custom-call(s32[1,16]{1,0:T(1,128)} %bitcast.46, ...), custom_call_target="tpu_custom_call" | custom-call | tf_op jit(solution)/shard_map/outgoing/pallas_call | solution.py:60
  1.6 0.6 collective-permute-start.5
  2.2 2.6 %collective-permute-start.6 = (bf16[1,2,8,1024]{3,2,1,0:T(8,128)(2,1)S(1)}, bf16[1,2,8,1024]{3,2,1,0:T(8,128)(2,1)S(1)}, u32[]{:S(2)}, u32[]{:S(2)}) collective-permute-start(bf16[1,2,8,1024]{3,2,1,0:T(8,128)(2,1)S(1)} %get-tuple-element.26), channel_id=1, source_target_pairs={{0,4},{1,5},{2,6},{3,7},{4,0},{5,1},{6,2},{7,3},{8,12},{9,13},{10,... | collective-permute-start | bytes 98312 | tf_op jit(solution)/shard_map/ppermute | solution.py:255
  4.8 1.8 %collective-permute-start = (bf16[4,2,8,1024]{3,2,1,0:T(8,128)(2,1)S(1)}, bf16[4,2,8,1024]{3,2,1,0:T(8,128)(2,1)S(1)}, u32[]{:S(2)}, u32[]{:S(2)}) collective-permute-start(bf16[4,2,8,1024]{3,2,1,0:T(8,128)(2,1)S(1)} %get-tuple-element.22), channel_id=1, source_target_pairs={{0,8},{1,9},{2,10},{3,11},{4,12},{5,13},{6,14},{7,15},{8,0},{9,1},... | collective-permute-start | bytes 393224 | tf_op jit(solution)/shard_map/ppermute | solution.py:255
  6.6 2.6 %collective-permute-start.1 = (bf16[4,2,8,1024]{3,2,1,0:T(8,128)(2,1)S(1)}, bf16[4,2,8,1024]{3,2,1,0:T(8,128)(2,1)S(1)}, u32[]{:S(2)}, u32[]{:S(2)}) collective-permute-start(bf16[4,2,8,1024]{3,2,1,0:T(8,128)(2,1)S(1)} %get-tuple-element.23), channel_id=1, source_target_pairs={{0,16},{1,17},{2,18},{3,19},{4,20},{5,21},{6,22},{7,23},{8,24},{9,... | collective-permute-start | bytes 393224 | tf_op jit(solution)/shard_map/ppermute | solution.py:255
  9.2 2.5 %collective-permute-start.8 = (bf16[4,2,8,1024]{3,2,1,0:T(8,128)(2,1)S(1)}, bf16[4,2,8,1024]{3,2,1,0:T(8,128)(2,1)S(1)}, u32[]{:S(2)}, u32[]{:S(2)}) collective-permute-start(bf16[4,2,8,1024]{3,2,1,0:T(8,128)(2,1)S(1)} %pad_maximum_fusion), channel_id=1, source_target_pairs={{0,24},{1,25},{2,26},{3,27},{4,28},{5,29},{6,30},{7,31},{8,16},{9,... | collective-permute-start | bytes 393224 | tf_op jit(solution)/shard_map/ppermute | solution.py:255
  11.8 0.9 %collective-permute-done.refs_1_ = bf16[4,2,8,1024]{3,2,1,0:T(8,128)(2,1)S(1)} collective-permute-done((bf16[4,2,8,1024]{3,2,1,0:T(8,128)(2,1)S(1)}, bf16[4,2,8,1024]{3,2,1,0:T(8,128)(2,1)S(1)}, u32[]{:S(2)}, u32[]{:S(2)}) %collective-permute-start) | collective-permute-done | bytes 131104 | tf_op jit(solution)/shard_map/ppermute | solution.py:255
  12.7 6.8 %collective-permute-done.1.refs_2_ = bf16[4,2,8,1024]{3,2,1,0:T(8,128)(2,1)S(1)} collective-permute-done((bf16[4,2,8,1024]{3,2,1,0:T(8,128)(2,1)S(1)}, bf16[4,2,8,1024]{3,2,1,0:T(8,128)(2,1)S(1)}, u32[]{:S(2)}, u32[]{:S(2)}) %collective-permute-start.1) | collective-permute-done | bytes 131104 | tf_op jit(solution)/shard_map/ppermute | solution.py:255
  19.7 1.6 %collective-permute-start.3 = (bf16[3,2,8,1024]{3,2,1,0:T(8,128)(2,1)S(1)}, bf16[3,2,8,1024]{3,2,1,0:T(8,128)(2,1)S(1)}, u32[]{:S(2)}, u32[]{:S(2)}) collective-permute-start(bf16[3,2,8,1024]{3,2,1,0:T(8,128)(2,1)S(1)} %pad_maximum_fusion.2), channel_id=1, source_target_pairs={{0,4},{1,5},{2,6},{3,7},{4,0},{5,1},{6,2},{7,3},{8,12},{9,13},{10,... | collective-permute-start | bytes 294920 | tf_op jit(solution)/shard_map/ppermute | solution.py:255
  21.2 0.4 collective-permute-start.4
  21.7 2.2 %prepare.1 = (bf16[2048,2048]{1,0:T(8,128)(2,1)S(1)}, bf16[2048,768]{1,0:T(8,128)(2,1)S(1)}) custom-call(s32[1,2048]{1,0:T(1,128)} %bitcast.47, bf16[2,3,2048,128]{3,2,1,0:T(8,128)(2,1)} %weights_hbm.1), custom_call_target="tpu_custom_call" | custom-call | flops 2000000000 | bytes 10000000 | tf_op jit(solution)/shard_map/prepare/pallas_call | solution.py:105
  23.9 1.5 %collective-permute-done.3.refs_4_ = bf16[3,2,8,1024]{3,2,1,0:T(8,128)(2,1)S(1)} collective-permute-done((bf16[3,2,8,1024]{3,2,1,0:T(8,128)(2,1)S(1)}, bf16[3,2,8,1024]{3,2,1,0:T(8,128)(2,1)S(1)}, u32[]{:S(2)}, u32[]{:S(2)}) %collective-permute-start.3) | collective-permute-done | bytes 98336 | tf_op jit(solution)/shard_map/ppermute | solution.py:255
  25.4 1.1 %collective-permute-done.4.refs_5_ = bf16[3,2,8,1024]{3,2,1,0:T(8,128)(2,1)S(1)} collective-permute-done((bf16[3,2,8,1024]{3,2,1,0:T(8,128)(2,1)S(1)}, bf16[3,2,8,1024]{3,2,1,0:T(8,128)(2,1)S(1)}, u32[]{:S(2)}, u32[]{:S(2)}) %collective-permute-start.4) | collective-permute-done | bytes 98336 | tf_op jit(solution)/shard_map/ppermute | solution.py:255
  26.5 5.9 %bands.1 = (bf16[2048,512]{1,0:T(8,128)(2,1)S(1)}, bf16[2,768,256]{2,1,0:T(8,128)(2,1)S(1)}) custom-call(s32[16]{0:T(128)S(1)} %copy-done, bf16[2048,768]{1,0:T(8,128)(2,1)S(1)} %get-tuple-element.19.joined_ref, bf16[2048,2048]{1,0:T(8,128)(2,1)S(1)} %get-tuple-element.20.select_ref, bf16[4,2,8,1024]{3,2,1,0:T(8,128)(2,1)S(1)} %get-tuple-element.21.refs_0_, ...), custom_call_target="tpu_custom_call" | custom-call | flops 4000000000 | bytes 10000000 | tf_op jit(solution)/shard_map/bands/pallas_call | solution.py:197
  32.9 1.8 %order.4 = bf16[2,768,256]{2,1,0:T(8,128)(2,1)S(1)} custom-call(bf16[2048,512]{1,0:T(8,128)(2,1)S(1)} %get-tuple-element.28.banded_ref, bf16[2048,2048]{1,0:T(8,128)(2,1)S(1)} %get-tuple-element.20.select_ref), custom_call_target="tpu_custom_call" | custom-call | flops 1000000000 | bytes 5000000 | tf_op jit(solution)/shard_map/order/pallas_call | solution.py:218
  35.0 0.7 %order.5 = bf16[2,256,256]{2,1,0:T(8,128)(2,1)S(1)} custom-call(bf16[2048,512]{1,0:T(8,128)(2,1)S(1)} %get-tuple-element.28.banded_ref, bf16[2048,2048]{1,0:T(8,128)(2,1)S(1)} %get-tuple-element.20.select_ref, bf16[1,3,128,256]{3,2,1,0:T(8,128)(2,1)S(1)} %get-tuple-element.35.refs_0_, bf16[1,3,128,256]{3,2,1,0:T(8,128)(2,1)S(1)} %get-tuple-element.34.refs_1_, ...), custom_call_target="tpu_custom_call" | custom-call | flops 1000000000 | bytes 5000000 | tf_op jit(solution)/shard_map/order/pallas_call | solution.py:218
  36.1 0.7 %order.3 = bf16[2,256,256]{2,1,0:T(8,128)(2,1)S(1)} custom-call(bf16[2048,512]{1,0:T(8,128)(2,1)S(1)} %get-tuple-element.28.banded_ref, bf16[2048,2048]{1,0:T(8,128)(2,1)S(1)} %get-tuple-element.20.select_ref), custom_call_target="tpu_custom_call" | custom-call | flops 1000000000 | bytes 5000000 | tf_op jit(solution)/shard_map/order/pallas_call | solution.py:218
  36.8 1.6 %collective-permute-start.16 = (bf16[1,3,128,256]{3,2,1,0:T(8,128)(2,1)S(1)}, bf16[1,3,128,256]{3,2,1,0:T(8,128)(2,1)S(1)}, u32[]{:S(2)}, u32[]{:S(2)}) collective-permute-start(bf16[1,3,128,256]{3,2,1,0:T(8,128)(2,1)S(1)} %get-tuple-element.33.refs_2_), channel_id=1, source_target_pairs={{0,1},{1,0},{2,3},{3,2},{4,5},{5,4},{6,7},{7,6},{8,9},{9,8},{10,11... | collective-permute-start | bytes 589832 | tf_op jit(solution)/shard_map/ppermute | solution.py:255
  38.4 1.5 %collective-permute-start.15 = (bf16[1,3,128,256]{3,2,1,0:T(8,128)(2,1)S(1)}, bf16[1,3,128,256]{3,2,1,0:T(8,128)(2,1)S(1)}, u32[]{:S(2)}, u32[]{:S(2)}) collective-permute-start(bf16[1,3,128,256]{3,2,1,0:T(8,128)(2,1)S(1)} %get-tuple-element.34.refs_1_), channel_id=1, source_target_pairs={{0,4},{1,5},{2,6},{3,7},{4,0},{5,1},{6,2},{7,3},{8,12},{9,13},{10,... | collective-permute-start | bytes 589832 | tf_op jit(solution)/shard_map/ppermute | solution.py:255
  39.9 0.5 collective-permute-start.14
  40.4 3.5 %collective-permute-done.16.refs_2_ = bf16[1,3,128,256]{3,2,1,0:T(8,128)(2,1)S(1)} collective-permute-done((bf16[1,3,128,256]{3,2,1,0:T(8,128)(2,1)S(1)}, bf16[1,3,128,256]{3,2,1,0:T(8,128)(2,1)S(1)}, u32[]{:S(2)}, u32[]{:S(2)}) %collective-permute-start.16) | collective-permute-done | bytes 196640 | tf_op jit(solution)/shard_map/ppermute | solution.py:255
  43.9 2.3 %collective-permute-done.15.refs_1_ = bf16[1,3,128,256]{3,2,1,0:T(8,128)(2,1)S(1)} collective-permute-done((bf16[1,3,128,256]{3,2,1,0:T(8,128)(2,1)S(1)}, bf16[1,3,128,256]{3,2,1,0:T(8,128)(2,1)S(1)}, u32[]{:S(2)}, u32[]{:S(2)}) %collective-permute-start.15) | collective-permute-done | bytes 196640 | tf_op jit(solution)/shard_map/ppermute | solution.py:255
  46.2 3.1 %collective-permute-done.14.refs_0_ = bf16[1,3,128,256]{3,2,1,0:T(8,128)(2,1)S(1)} collective-permute-done((bf16[1,3,128,256]{3,2,1,0:T(8,128)(2,1)S(1)}, bf16[1,3,128,256]{3,2,1,0:T(8,128)(2,1)S(1)}, u32[]{:S(2)}, u32[]{:S(2)}) %collective-permute-start.14) | collective-permute-done | bytes 196640 | tf_op jit(solution)/shard_map/ppermute | solution.py:255
  49.4 2.6 %collective-permute-start.17 = (bf16[1,128,256]{2,1,0:T(8,128)(2,1)S(1)}, bf16[1,128,256]{2,1,0:T(8,128)(2,1)S(1)}, u32[]{:S(2)}, u32[]{:S(2)}) collective-permute-start(bf16[1,128,256]{2,1,0:T(8,128)(2,1)S(1)} %get-tuple-element.30), channel_id=1, source_target_pairs={{0,24},{1,25},{2,26},{3,27},{4,28},{5,29},{6,30},{7,31},{8,16},{9,... | collective-permute-start | bytes 196616 | tf_op jit(solution)/shard_map/ppermute | solution.py:255
  52.0 1.5 %collective-permute-start.13 = (bf16[1,1,128,256]{3,2,1,0:T(8,128)(2,1)S(1)}, bf16[1,1,128,256]{3,2,1,0:T(8,128)(2,1)S(1)}, u32[]{:S(2)}, u32[]{:S(2)}) collective-permute-start(bf16[1,1,128,256]{3,2,1,0:T(8,128)(2,1)S(1)} %get-tuple-element.36.refs_5_), channel_id=1, source_target_pairs={{0,1},{1,0},{2,3},{3,2},{4,5},{5,4},{6,7},{7,6},{8,9},{9,8},{10,11... | collective-permute-start | bytes 196616 | tf_op jit(solution)/shard_map/ppermute | solution.py:255
  53.5 1.9 %collective-permute-start.19 = (bf16[1,128,256]{2,1,0:T(8,128)(2,1)S(1)}, bf16[1,128,256]{2,1,0:T(8,128)(2,1)S(1)}, u32[]{:S(2)}, u32[]{:S(2)}) collective-permute-start(bf16[1,128,256]{2,1,0:T(8,128)(2,1)S(1)} %get-tuple-element.32), channel_id=1, source_target_pairs={{0,8},{1,9},{2,10},{3,11},{4,12},{5,13},{6,14},{7,15},{8,0},{9,1},... | collective-permute-start | bytes 196616 | tf_op jit(solution)/shard_map/ppermute | solution.py:255
  55.4 1.5 %collective-permute-start.12 = (bf16[1,1,128,256]{3,2,1,0:T(8,128)(2,1)S(1)}, bf16[1,1,128,256]{3,2,1,0:T(8,128)(2,1)S(1)}, u32[]{:S(2)}, u32[]{:S(2)}) collective-permute-start(bf16[1,1,128,256]{3,2,1,0:T(8,128)(2,1)S(1)} %get-tuple-element.37.refs_4_), channel_id=1, source_target_pairs={{0,4},{1,5},{2,6},{3,7},{4,0},{5,1},{6,2},{7,3},{8,12},{9,13},{10,... | collective-permute-start | bytes 196616 | tf_op jit(solution)/shard_map/ppermute | solution.py:255
  56.9 1.2 %collective-permute-start.11 = (bf16[1,1,128,256]{3,2,1,0:T(8,128)(2,1)S(1)}, bf16[1,1,128,256]{3,2,1,0:T(8,128)(2,1)S(1)}, u32[]{:S(2)}, u32[]{:S(2)}) collective-permute-start(bf16[1,1,128,256]{3,2,1,0:T(8,128)(2,1)S(1)} %get-tuple-element.38.refs_3_), channel_id=1, source_target_pairs={{0,5},{1,4},{2,7},{3,6},{4,1},{5,0},{6,3},{7,2},{8,13},{9,12},{10,... | collective-permute-start | bytes 196616 | tf_op jit(solution)/shard_map/ppermute | solution.py:255
  58.1 0.5 collective-permute-done.18
  58.7 1.0 %collective-permute-done.12 = bf16[1,1,128,256]{3,2,1,0:T(8,128)(2,1)S(1)} collective-permute-done((bf16[1,1,128,256]{3,2,1,0:T(8,128)(2,1)S(1)}, bf16[1,1,128,256]{3,2,1,0:T(8,128)(2,1)S(1)}, u32[]{:S(2)}, u32[]{:S(2)}) %collective-permute-start.12) | collective-permute-done | bytes 65568 | tf_op jit(solution)/shard_map/ppermute | solution.py:255
  59.7 2.4 %collective-permute-done.11 = bf16[1,1,128,256]{3,2,1,0:T(8,128)(2,1)S(1)} collective-permute-done((bf16[1,1,128,256]{3,2,1,0:T(8,128)(2,1)S(1)}, bf16[1,1,128,256]{3,2,1,0:T(8,128)(2,1)S(1)}, u32[]{:S(2)}, u32[]{:S(2)}) %collective-permute-start.11) | collective-permute-done | bytes 65568 | tf_op jit(solution)/shard_map/ppermute | solution.py:255
  62.1 0.7 %fusion.5 = f32[128,256]{1,0:T(8,128)} fusion(bf16[1,128,256]{2,1,0:T(8,128)(2,1)S(1)} %collective-permute-done.19, bf16[1,128,256]{2,1,0:T(8,128)(2,1)S(1)} %collective-permute-done.18, bf16[1,128,256]{2,1,0:T(8,128)(2,1)S(1)} %collective-permute-done.17, bf16[1,1,128,256]{3,2,1,0:T(8,128)(2,1)S(1)} %collective-permute-done.13, ...), kind=kLoop, calls=%fused_computation.10 | loop fusion | flops 491520 | bytes 655360 | tf_op jit(solution)/shard_map/squeeze | solution.py:313
  (27 shorter events, 1.5 us)
Async XLA Ops:
  1.6 7.6 %collective-permute-start.5 = (bf16[1,2,8,1024]{3,2,1,0:T(8,128)(2,1)S(1)}, bf16[1,2,8,1024]{3,2,1,0:T(8,128)(2,1)S(1)}, u32[]{:S(2)}, u32[]{:S(2)}) collective-permute-start(bf16[1,2,8,1024]{3,2,1,0:T(8,128)(2,1)S(1)} %get-tuple-element.25), channel_id=1, source_target_pairs={{0,2},{1,3},{2,0},{3,1},{4,6},{5,7},{6,4},{7,5},{8,10},{9,11},{10,... | collective-permute-start | bytes 98312 | tf_op jit(solution)/shard_map/ppermute | solution.py:255
  2.2 7.0 %collective-permute-start.6 = (bf16[1,2,8,1024]{3,2,1,0:T(8,128)(2,1)S(1)}, bf16[1,2,8,1024]{3,2,1,0:T(8,128)(2,1)S(1)}, u32[]{:S(2)}, u32[]{:S(2)}) collective-permute-start(bf16[1,2,8,1024]{3,2,1,0:T(8,128)(2,1)S(1)} %get-tuple-element.26), channel_id=1, source_target_pairs={{0,4},{1,5},{2,6},{3,7},{4,0},{5,1},{6,2},{7,3},{8,12},{9,13},{10,... | collective-permute-start | bytes 98312 | tf_op jit(solution)/shard_map/ppermute | solution.py:255
  4.7 4.5 %collective-permute-start.7 = (bf16[1,2,8,1024]{3,2,1,0:T(8,128)(2,1)S(1)}, bf16[1,2,8,1024]{3,2,1,0:T(8,128)(2,1)S(1)}, u32[]{:S(2)}, u32[]{:S(2)}) collective-permute-start(bf16[1,2,8,1024]{3,2,1,0:T(8,128)(2,1)S(1)} %get-tuple-element.27), channel_id=1, source_target_pairs={{0,6},{1,7},{2,4},{3,5},{4,2},{5,3},{6,0},{7,1},{8,14},{9,15},{10,... | collective-permute-start | bytes 98312 | tf_op jit(solution)/shard_map/ppermute | solution.py:255
  4.8 7.9 %collective-permute-start = (bf16[4,2,8,1024]{3,2,1,0:T(8,128)(2,1)S(1)}, bf16[4,2,8,1024]{3,2,1,0:T(8,128)(2,1)S(1)}, u32[]{:S(2)}, u32[]{:S(2)}) collective-permute-start(bf16[4,2,8,1024]{3,2,1,0:T(8,128)(2,1)S(1)} %get-tuple-element.22), channel_id=1, source_target_pairs={{0,8},{1,9},{2,10},{3,11},{4,12},{5,13},{6,14},{7,15},{8,0},{9,1},... | collective-permute-start | bytes 393224 | tf_op jit(solution)/shard_map/ppermute | solution.py:255
  6.6 12.9 %collective-permute-start.1 = (bf16[4,2,8,1024]{3,2,1,0:T(8,128)(2,1)S(1)}, bf16[4,2,8,1024]{3,2,1,0:T(8,128)(2,1)S(1)}, u32[]{:S(2)}, u32[]{:S(2)}) collective-permute-start(bf16[4,2,8,1024]{3,2,1,0:T(8,128)(2,1)S(1)} %get-tuple-element.23), channel_id=1, source_target_pairs={{0,16},{1,17},{2,18},{3,19},{4,20},{5,21},{6,22},{7,23},{8,24},{9,... | collective-permute-start | bytes 393224 | tf_op jit(solution)/shard_map/ppermute | solution.py:255
  9.2 14.6 %collective-permute-start.8 = (bf16[4,2,8,1024]{3,2,1,0:T(8,128)(2,1)S(1)}, bf16[4,2,8,1024]{3,2,1,0:T(8,128)(2,1)S(1)}, u32[]{:S(2)}, u32[]{:S(2)}) collective-permute-start(bf16[4,2,8,1024]{3,2,1,0:T(8,128)(2,1)S(1)} %pad_maximum_fusion), channel_id=1, source_target_pairs={{0,24},{1,25},{2,26},{3,27},{4,28},{5,29},{6,30},{7,31},{8,16},{9,... | collective-permute-start | bytes 393224 | tf_op jit(solution)/shard_map/ppermute | solution.py:255
  19.6 4.3 %collective-permute-start.2 = (bf16[3,2,8,1024]{3,2,1,0:T(8,128)(2,1)S(1)}, bf16[3,2,8,1024]{3,2,1,0:T(8,128)(2,1)S(1)}, u32[]{:S(2)}, u32[]{:S(2)}) collective-permute-start(bf16[3,2,8,1024]{3,2,1,0:T(8,128)(2,1)S(1)} %pad_maximum_fusion.1), channel_id=1, source_target_pairs={{0,2},{1,3},{2,0},{3,1},{4,6},{5,7},{6,4},{7,5},{8,10},{9,11},{10,... | collective-permute-start | bytes 294920 | tf_op jit(solution)/shard_map/ppermute | solution.py:255
  19.7 5.7 %collective-permute-start.3 = (bf16[3,2,8,1024]{3,2,1,0:T(8,128)(2,1)S(1)}, bf16[3,2,8,1024]{3,2,1,0:T(8,128)(2,1)S(1)}, u32[]{:S(2)}, u32[]{:S(2)}) collective-permute-start(bf16[3,2,8,1024]{3,2,1,0:T(8,128)(2,1)S(1)} %pad_maximum_fusion.2), channel_id=1, source_target_pairs={{0,4},{1,5},{2,6},{3,7},{4,0},{5,1},{6,2},{7,3},{8,12},{9,13},{10,... | collective-permute-start | bytes 294920 | tf_op jit(solution)/shard_map/ppermute | solution.py:255
  21.2 5.3 %collective-permute-start.4 = (bf16[3,2,8,1024]{3,2,1,0:T(8,128)(2,1)S(1)}, bf16[3,2,8,1024]{3,2,1,0:T(8,128)(2,1)S(1)}, u32[]{:S(2)}, u32[]{:S(2)}) collective-permute-start(bf16[3,2,8,1024]{3,2,1,0:T(8,128)(2,1)S(1)} %pad_maximum_fusion.3), channel_id=1, source_target_pairs={{0,6},{1,7},{2,4},{3,5},{4,2},{5,3},{6,0},{7,1},{8,14},{9,15},{10,... | collective-permute-start | bytes 294920 | tf_op jit(solution)/shard_map/ppermute | solution.py:255
  21.6 4.9 %copy-start = (s32[16]{0:T(128)S(1)}, s32[16]{0:T(128)}, u32[]{:S(2)}) copy-start(s32[16]{0:T(128)} %lags_ref.1) | copy-start | bytes 196
  32.5 2.4 %collective-permute-start.9 = (bf16[2,768,256]{2,1,0:T(8,128)(2,1)S(1)}, bf16[2,768,256]{2,1,0:T(8,128)(2,1)S(1)}, u32[]{:S(2)}, u32[]{:S(2)}) collective-permute-start(bf16[2,768,256]{2,1,0:T(8,128)(2,1)S(1)} %get-tuple-element.29), channel_id=1, source_target_pairs={{0,2},{1,3},{2,0},{3,1},{4,6},{5,7},{6,4},{7,5},{8,10},{9,11},{10,... | collective-permute-start | bytes 2359304 | tf_op jit(solution)/shard_map/ppermute | solution.py:255
  35.7 4.7 %collective-permute-start.10 = (bf16[2,256,256]{2,1,0:T(8,128)(2,1)S(1)}, bf16[2,256,256]{2,1,0:T(8,128)(2,1)S(1)}, u32[]{:S(2)}, u32[]{:S(2)}) collective-permute-start(bf16[2,256,256]{2,1,0:T(8,128)(2,1)S(1)} %order.5), channel_id=1, source_target_pairs={{0,2},{1,3},{2,0},{3,1},{4,6},{5,7},{6,4},{7,5},{8,10},{9,11},{10,... | collective-permute-start | bytes 786440 | tf_op jit(solution)/shard_map/ppermute | solution.py:255
  36.8 7.1 %collective-permute-start.16 = (bf16[1,3,128,256]{3,2,1,0:T(8,128)(2,1)S(1)}, bf16[1,3,128,256]{3,2,1,0:T(8,128)(2,1)S(1)}, u32[]{:S(2)}, u32[]{:S(2)}) collective-permute-start(bf16[1,3,128,256]{3,2,1,0:T(8,128)(2,1)S(1)} %get-tuple-element.33.refs_2_), channel_id=1, source_target_pairs={{0,1},{1,0},{2,3},{3,2},{4,5},{5,4},{6,7},{7,6},{8,9},{9,8},{10,11... | collective-permute-start | bytes 589832 | tf_op jit(solution)/shard_map/ppermute | solution.py:255
  38.4 7.8 %collective-permute-start.15 = (bf16[1,3,128,256]{3,2,1,0:T(8,128)(2,1)S(1)}, bf16[1,3,128,256]{3,2,1,0:T(8,128)(2,1)S(1)}, u32[]{:S(2)}, u32[]{:S(2)}) collective-permute-start(bf16[1,3,128,256]{3,2,1,0:T(8,128)(2,1)S(1)} %get-tuple-element.34.refs_1_), channel_id=1, source_target_pairs={{0,4},{1,5},{2,6},{3,7},{4,0},{5,1},{6,2},{7,3},{8,12},{9,13},{10,... | collective-permute-start | bytes 589832 | tf_op jit(solution)/shard_map/ppermute | solution.py:255
  39.9 9.4 %collective-permute-start.14 = (bf16[1,3,128,256]{3,2,1,0:T(8,128)(2,1)S(1)}, bf16[1,3,128,256]{3,2,1,0:T(8,128)(2,1)S(1)}, u32[]{:S(2)}, u32[]{:S(2)}) collective-permute-start(bf16[1,3,128,256]{3,2,1,0:T(8,128)(2,1)S(1)} %get-tuple-element.35.refs_0_), channel_id=1, source_target_pairs={{0,5},{1,4},{2,7},{3,6},{4,1},{5,0},{6,3},{7,2},{8,13},{9,12},{10,... | collective-permute-start | bytes 589832 | tf_op jit(solution)/shard_map/ppermute | solution.py:255
  49.4 7.4 %collective-permute-start.17 = (bf16[1,128,256]{2,1,0:T(8,128)(2,1)S(1)}, bf16[1,128,256]{2,1,0:T(8,128)(2,1)S(1)}, u32[]{:S(2)}, u32[]{:S(2)}) collective-permute-start(bf16[1,128,256]{2,1,0:T(8,128)(2,1)S(1)} %get-tuple-element.30), channel_id=1, source_target_pairs={{0,24},{1,25},{2,26},{3,27},{4,28},{5,29},{6,30},{7,31},{8,16},{9,... | collective-permute-start | bytes 196616 | tf_op jit(solution)/shard_map/ppermute | solution.py:255
  52.0 6.7 %collective-permute-start.13 = (bf16[1,1,128,256]{3,2,1,0:T(8,128)(2,1)S(1)}, bf16[1,1,128,256]{3,2,1,0:T(8,128)(2,1)S(1)}, u32[]{:S(2)}, u32[]{:S(2)}) collective-permute-start(bf16[1,1,128,256]{3,2,1,0:T(8,128)(2,1)S(1)} %get-tuple-element.36.refs_5_), channel_id=1, source_target_pairs={{0,1},{1,0},{2,3},{3,2},{4,5},{5,4},{6,7},{7,6},{8,9},{9,8},{10,11... | collective-permute-start | bytes 196616 | tf_op jit(solution)/shard_map/ppermute | solution.py:255
  53.5 5.2 %collective-permute-start.18 = (bf16[1,128,256]{2,1,0:T(8,128)(2,1)S(1)}, bf16[1,128,256]{2,1,0:T(8,128)(2,1)S(1)}, u32[]{:S(2)}, u32[]{:S(2)}) collective-permute-start(bf16[1,128,256]{2,1,0:T(8,128)(2,1)S(1)} %get-tuple-element.31), channel_id=1, source_target_pairs={{0,16},{1,17},{2,18},{3,19},{4,20},{5,21},{6,22},{7,23},{8,24},{9,... | collective-permute-start | bytes 196616 | tf_op jit(solution)/shard_map/ppermute | solution.py:255
  53.5 5.2 %collective-permute-start.19 = (bf16[1,128,256]{2,1,0:T(8,128)(2,1)S(1)}, bf16[1,128,256]{2,1,0:T(8,128)(2,1)S(1)}, u32[]{:S(2)}, u32[]{:S(2)}) collective-permute-start(bf16[1,128,256]{2,1,0:T(8,128)(2,1)S(1)} %get-tuple-element.32), channel_id=1, source_target_pairs={{0,8},{1,9},{2,10},{3,11},{4,12},{5,13},{6,14},{7,15},{8,0},{9,1},... | collective-permute-start | bytes 196616 | tf_op jit(solution)/shard_map/ppermute | solution.py:255
  55.4 4.3 %collective-permute-start.12 = (bf16[1,1,128,256]{3,2,1,0:T(8,128)(2,1)S(1)}, bf16[1,1,128,256]{3,2,1,0:T(8,128)(2,1)S(1)}, u32[]{:S(2)}, u32[]{:S(2)}) collective-permute-start(bf16[1,1,128,256]{3,2,1,0:T(8,128)(2,1)S(1)} %get-tuple-element.37.refs_4_), channel_id=1, source_target_pairs={{0,4},{1,5},{2,6},{3,7},{4,0},{5,1},{6,2},{7,3},{8,12},{9,13},{10,... | collective-permute-start | bytes 196616 | tf_op jit(solution)/shard_map/ppermute | solution.py:255
  56.9 5.2 %collective-permute-start.11 = (bf16[1,1,128,256]{3,2,1,0:T(8,128)(2,1)S(1)}, bf16[1,1,128,256]{3,2,1,0:T(8,128)(2,1)S(1)}, u32[]{:S(2)}, u32[]{:S(2)}) collective-permute-start(bf16[1,1,128,256]{3,2,1,0:T(8,128)(2,1)S(1)} %get-tuple-element.38.refs_3_), channel_id=1, source_target_pairs={{0,5},{1,4},{2,7},{3,6},{4,1},{5,0},{6,3},{7,2},{8,13},{9,12},{10,... | collective-permute-start | bytes 196616 | tf_op jit(solution)/shard_map/ppermute | solution.py:255

commit v6 on v5

--- a/solution.py
+++ b/solution.py
@@ -10,7 +10,7 @@
 
 LANES = 128
 AXES = ("cfd", "ac")
-MIDDLE = ((1, 1), (1, 0), (0, 1))
+MIDDLE = ((1, 0), (0, 1), (1, 1))
 MIB = 1024 * 1024
 SMEM = pl.BlockSpec(memory_space=pltpu.SMEM)
 VMEM = pl.BlockSpec(memory_space=pltpu.VMEM)
@@ -274,7 +274,8 @@
     taps, _, count, _ = kernel_weights.shape
     out_len = steps // 2
     each = count // ranks
-    chunks = (range(1, high), range(1))
+    half = high // 2
+    chunks = (range(half, high), range(half))
     layout = [(z * 2 + x) * 2 + c for zs in chunks for c in (1, 0) for x in range(2) for z in zs]
     parts = sides if out_len // sides % LANES == 0 else 1
     far_rows, near_rows = [len(zs) * 2 * each for zs in chunks]
@@ -298,7 +299,10 @@
         return keep, got, total(0, 0), [total(x, y).astype(jnp.bfloat16) for x, y in MIDDLE]
 
     def over_middle(sends):
-        return [swap(send, ranks, sides, 2 * x, y) for (x, y), send in zip(MIDDLE, sends)]
+        got = []
+        for (x, y), send in zip(MIDDLE, sends):
+            got.append(swap(send, ranks, sides, 2 * x, y))
+        return got
 
     keep, got, _, far_sends = over_core(far_send, far_rows, far_shape)
     near_send = order_more(banded, select, 2 * far_rows, near_shape, far_sends)
@@ -309,7 +313,8 @@
         total = total + moved.astype(jnp.float32)
     result = total[:, 0]
     for z in range(high - 1, 0, -1):
-        result = result + swap(far[z - 1], ranks, sides, 4 * z).astype(jnp.float32)
+        send = far[z - half] if z >= half else total[:, z].astype(jnp.bfloat16)
+        result = result + swap(send, ranks, sides, 4 * z).astype(jnp.float32)
     out = result[0]
     for y in range(sides // 2 - 1, 0, -1):
         out = out + swap(result[y].astype(jnp.bfloat16), ranks, sides, 0, 2 * y).astype(jnp.float32)

time: 62.9 us -> 57.2 us (0.909)
  waiting for transfers between devices: 23.4 us -> 18.7 us
  starting transfers between devices: 25.1 us -> 24.1 us
    ppermute x20, waiting for transfers between devices: 23.4 us -> 18.7 us  [swap(): return lax.ppermute(value, AXES, pairs)]
    ppermute x20, starting transfers between devices: 25.1 us -> 24.1 us  [swap(): return lax.ppermute(value, AXES, pairs)]
  transfers between devices with their start and end apart: 20 -> 20, of which waited for: 11 -> 13; matrix products, arithmetic and copies ran while one was open for 0% -> 0% of each run, Pallas kernels for 8% -> 8%
where the time goes in v6:
time: 57.2 us; the launch traced here: 57 us
  starting transfers between devices  24.1 us (42%)
  waiting for transfers between devices  18.7 us (33%)
  Pallas kernels  13 us (23%)
  other arithmetic  1.03 us (2%)
    ppermute x20, starting transfers between devices, swap(): return lax.ppermute(value, AXES, pairs)  24.1 us
    ppermute x20, waiting for transfers between devices, swap(): return lax.ppermute(value, AXES, pairs)  18.7 us
    pallas_call x1, Pallas kernels, bands(): pl.pallas_call(functools.partial(bands_kernel, taps, direct, high, first_...  5.4 us
    pallas_call x3, Pallas kernels, order_more(): pl.pallas_call(functools.partial(order_kernel, first_row), out_shape=shap...  3.76 us
    pallas_call x1, Pallas kernels, prepare(): pl.pallas_call(functools.partial(prepare_kernel, ranks, layout), out_shap...  2.19 us
    pallas_call x1, Pallas kernels, outgoing(): pl.pallas_call(functools.partial(outgoing_kernel, direct, high), out_shap...  1.6 us
  transfers between devices with their start and end apart: 20, of which 13 were waited for; matrix products, arithmetic and copies ran while one was open for 0% of the time, Pallas kernels for 8%

profile of v6, /device:TPU:0, one launch (start us, length us, event | category | flops | bytes accessed | tf_op | source)
XLA Modules:
  0.0 57.0 jit_solution(12511444584687773826)
XLA Ops:
  0.0 1.6 %outgoing.1 = (bf16[4,2,8,1024]{3,2,1,0:T(8,128)(2,1)S(1)}, bf16[4,2,8,1024]{3,2,1,0:T(8,128)(2,1)S(1)}, bf16[4,2,8,1024]{3,2,1,0:T(8,128)(2,1)S(1)}, bf16[1,2,8...) custom-call(s32[1,16]{1,0:T(1,128)} %bitcast.48, ...), custom_call_target="tpu_custom_call" | custom-call | tf_op jit(solution)/shard_map/outgoing/pallas_call | solution.py:60
  1.6 0.6 collective-permute-start.5
  2.2 2.6 %collective-permute-start.6 = (bf16[1,2,8,1024]{3,2,1,0:T(8,128)(2,1)S(1)}, bf16[1,2,8,1024]{3,2,1,0:T(8,128)(2,1)S(1)}, u32[]{:S(2)}, u32[]{:S(2)}) collective-permute-start(bf16[1,2,8,1024]{3,2,1,0:T(8,128)(2,1)S(1)} %get-tuple-element.25), channel_id=1, source_target_pairs={{0,4},{1,5},{2,6},{3,7},{4,0},{5,1},{6,2},{7,3},{8,12},{9,13},{10,... | collective-permute-start | bytes 98312 | tf_op jit(solution)/shard_map/ppermute | solution.py:255
  4.8 1.8 %collective-permute-start = (bf16[4,2,8,1024]{3,2,1,0:T(8,128)(2,1)S(1)}, bf16[4,2,8,1024]{3,2,1,0:T(8,128)(2,1)S(1)}, u32[]{:S(2)}, u32[]{:S(2)}) collective-permute-start(bf16[4,2,8,1024]{3,2,1,0:T(8,128)(2,1)S(1)} %get-tuple-element.21), channel_id=1, source_target_pairs={{0,8},{1,9},{2,10},{3,11},{4,12},{5,13},{6,14},{7,15},{8,0},{9,1},... | collective-permute-start | bytes 393224 | tf_op jit(solution)/shard_map/ppermute | solution.py:255
  6.6 2.6 %collective-permute-start.1 = (bf16[4,2,8,1024]{3,2,1,0:T(8,128)(2,1)S(1)}, bf16[4,2,8,1024]{3,2,1,0:T(8,128)(2,1)S(1)}, u32[]{:S(2)}, u32[]{:S(2)}) collective-permute-start(bf16[4,2,8,1024]{3,2,1,0:T(8,128)(2,1)S(1)} %get-tuple-element.22), channel_id=1, source_target_pairs={{0,16},{1,17},{2,18},{3,19},{4,20},{5,21},{6,22},{7,23},{8,24},{9,... | collective-permute-start | bytes 393224 | tf_op jit(solution)/shard_map/ppermute | solution.py:255
  9.2 2.5 %collective-permute-start.8 = (bf16[4,2,8,1024]{3,2,1,0:T(8,128)(2,1)S(1)}, bf16[4,2,8,1024]{3,2,1,0:T(8,128)(2,1)S(1)}, u32[]{:S(2)}, u32[]{:S(2)}) collective-permute-start(bf16[4,2,8,1024]{3,2,1,0:T(8,128)(2,1)S(1)} %pad_maximum_fusion), channel_id=1, source_target_pairs={{0,24},{1,25},{2,26},{3,27},{4,28},{5,29},{6,30},{7,31},{8,16},{9,... | collective-permute-start | bytes 393224 | tf_op jit(solution)/shard_map/ppermute | solution.py:255
  11.8 0.9 %collective-permute-done.refs_1_ = bf16[4,2,8,1024]{3,2,1,0:T(8,128)(2,1)S(1)} collective-permute-done((bf16[4,2,8,1024]{3,2,1,0:T(8,128)(2,1)S(1)}, bf16[4,2,8,1024]{3,2,1,0:T(8,128)(2,1)S(1)}, u32[]{:S(2)}, u32[]{:S(2)}) %collective-permute-start) | collective-permute-done | bytes 131104 | tf_op jit(solution)/shard_map/ppermute | solution.py:255
  12.7 6.8 %collective-permute-done.1.refs_2_ = bf16[4,2,8,1024]{3,2,1,0:T(8,128)(2,1)S(1)} collective-permute-done((bf16[4,2,8,1024]{3,2,1,0:T(8,128)(2,1)S(1)}, bf16[4,2,8,1024]{3,2,1,0:T(8,128)(2,1)S(1)}, u32[]{:S(2)}, u32[]{:S(2)}) %collective-permute-start.1) | collective-permute-done | bytes 131104 | tf_op jit(solution)/shard_map/ppermute | solution.py:255
  19.7 1.6 %collective-permute-start.3 = (bf16[3,2,8,1024]{3,2,1,0:T(8,128)(2,1)S(1)}, bf16[3,2,8,1024]{3,2,1,0:T(8,128)(2,1)S(1)}, u32[]{:S(2)}, u32[]{:S(2)}) collective-permute-start(bf16[3,2,8,1024]{3,2,1,0:T(8,128)(2,1)S(1)} %pad_maximum_fusion.2), channel_id=1, source_target_pairs={{0,4},{1,5},{2,6},{3,7},{4,0},{5,1},{6,2},{7,3},{8,12},{9,13},{10,... | collective-permute-start | bytes 294920 | tf_op jit(solution)/shard_map/ppermute | solution.py:255
  21.2 0.4 collective-permute-start.4
  21.7 2.2 %prepare.1 = (bf16[2048,2048]{1,0:T(8,128)(2,1)S(1)}, bf16[2048,768]{1,0:T(8,128)(2,1)S(1)}) custom-call(s32[1,2048]{1,0:T(1,128)} %bitcast.49, bf16[2,3,2048,128]{3,2,1,0:T(8,128)(2,1)} %weights_hbm.1), custom_call_target="tpu_custom_call" | custom-call | flops 2000000000 | bytes 10000000 | tf_op jit(solution)/shard_map/prepare/pallas_call | solution.py:105
  23.9 1.5 %collective-permute-done.3.refs_4_ = bf16[3,2,8,1024]{3,2,1,0:T(8,128)(2,1)S(1)} collective-permute-done((bf16[3,2,8,1024]{3,2,1,0:T(8,128)(2,1)S(1)}, bf16[3,2,8,1024]{3,2,1,0:T(8,128)(2,1)S(1)}, u32[]{:S(2)}, u32[]{:S(2)}) %collective-permute-start.3) | collective-permute-done | bytes 98336 | tf_op jit(solution)/shard_map/ppermute | solution.py:255
  25.4 1.1 %collective-permute-done.4.refs_5_ = bf16[3,2,8,1024]{3,2,1,0:T(8,128)(2,1)S(1)} collective-permute-done((bf16[3,2,8,1024]{3,2,1,0:T(8,128)(2,1)S(1)}, bf16[3,2,8,1024]{3,2,1,0:T(8,128)(2,1)S(1)}, u32[]{:S(2)}, u32[]{:S(2)}) %collective-permute-start.4) | collective-permute-done | bytes 98336 | tf_op jit(solution)/shard_map/ppermute | solution.py:255
  26.5 5.4 %bands.1 = (bf16[2048,512]{1,0:T(8,128)(2,1)S(1)}, bf16[2,512,256]{2,1,0:T(8,128)(2,1)S(1)}) custom-call(s32[16]{0:T(128)S(1)} %copy-done, bf16[2048,768]{1,0:T(8,128)(2,1)S(1)} %get-tuple-element.18.joined_ref, bf16[2048,2048]{1,0:T(8,128)(2,1)S(1)} %get-tuple-element.19.select_ref, bf16[4,2,8,1024]{3,2,1,0:T(8,128)(2,1)S(1)} %get-tuple-element.20.refs_0_, ...), custom_call_target="tpu_custom_call" | custom-call | flops 4000000000 | bytes 10000000 | tf_op jit(solution)/shard_map/bands/pallas_call | solution.py:197
  31.9 0.4 collective-permute-start.9
  32.3 1.2 %order.4 = bf16[2,512,256]{2,1,0:T(8,128)(2,1)S(1)} custom-call(bf16[2048,512]{1,0:T(8,128)(2,1)S(1)} %get-tuple-element.27.banded_ref, bf16[2048,2048]{1,0:T(8,128)(2,1)S(1)} %get-tuple-element.19.select_ref), custom_call_target="tpu_custom_call" | custom-call | flops 1000000000 | bytes 5000000 | tf_op jit(solution)/shard_map/order/pallas_call | solution.py:218
  34.0 1.3 %order.5 = bf16[2,512,256]{2,1,0:T(8,128)(2,1)S(1)} custom-call(bf16[2048,512]{1,0:T(8,128)(2,1)S(1)} %get-tuple-element.27.banded_ref, bf16[2048,2048]{1,0:T(8,128)(2,1)S(1)} %get-tuple-element.19.select_ref, bf16[1,2,128,256]{3,2,1,0:T(8,128)(2,1)S(1)} %get-tuple-element.36.refs_0_, bf16[1,2,128,256]{3,2,1,0:T(8,128)(2,1)S(1)} %get-tuple-element.35.refs_1_, ...), custom_call_target="tpu_custom_call" | custom-call | flops 1000000000 | bytes 5000000 | tf_op jit(solution)/shard_map/order/pallas_call | solution.py:218
  35.7 1.3 %order.3 = bf16[2,512,256]{2,1,0:T(8,128)(2,1)S(1)} custom-call(bf16[2048,512]{1,0:T(8,128)(2,1)S(1)} %get-tuple-element.27.banded_ref, bf16[2048,2048]{1,0:T(8,128)(2,1)S(1)} %get-tuple-element.19.select_ref), custom_call_target="tpu_custom_call" | custom-call | flops 1000000000 | bytes 5000000 | tf_op jit(solution)/shard_map/order/pallas_call | solution.py:218
  36.9 2.5 %collective-permute-start.16 = (bf16[1,2,128,256]{3,2,1,0:T(8,128)(2,1)S(1)}, bf16[1,2,128,256]{3,2,1,0:T(8,128)(2,1)S(1)}, u32[]{:S(2)}, u32[]{:S(2)}) collective-permute-start(bf16[1,2,128,256]{3,2,1,0:T(8,128)(2,1)S(1)} %get-tuple-element.34.refs_2_), channel_id=1, source_target_pairs={{0,5},{1,4},{2,7},{3,6},{4,1},{5,0},{6,3},{7,2},{8,13},{9,12},{10,... | collective-permute-start | bytes 393224 | tf_op jit(solution)/shard_map/ppermute | solution.py:255
  39.5 0.5 collective-permute-start.15
  40.0 0.5 collective-permute-start.14
  40.6 1.6 %collective-permute-start.11 = (bf16[1,2,128,256]{3,2,1,0:T(8,128)(2,1)S(1)}, bf16[1,2,128,256]{3,2,1,0:T(8,128)(2,1)S(1)}, u32[]{:S(2)}, u32[]{:S(2)}) collective-permute-start(bf16[1,2,128,256]{3,2,1,0:T(8,128)(2,1)S(1)} %get-tuple-element.31.refs_3_), channel_id=1, source_target_pairs={{0,4},{1,5},{2,6},{3,7},{4,0},{5,1},{6,2},{7,3},{8,12},{9,13},{10,... | collective-permute-start | bytes 393224 | tf_op jit(solution)/shard_map/ppermute | solution.py:255
  42.1 1.5 %collective-permute-start.13 = (bf16[1,2,128,256]{3,2,1,0:T(8,128)(2,1)S(1)}, bf16[1,2,128,256]{3,2,1,0:T(8,128)(2,1)S(1)}, u32[]{:S(2)}, u32[]{:S(2)}) collective-permute-start(bf16[1,2,128,256]{3,2,1,0:T(8,128)(2,1)S(1)} %get-tuple-element.32.refs_5_), channel_id=1, source_target_pairs={{0,5},{1,4},{2,7},{3,6},{4,1},{5,0},{6,3},{7,2},{8,13},{9,12},{10,... | collective-permute-start | bytes 393224 | tf_op jit(solution)/shard_map/ppermute | solution.py:255
  43.8 2.0 %collective-permute-start.12 = (bf16[1,2,128,256]{3,2,1,0:T(8,128)(2,1)S(1)}, bf16[1,2,128,256]{3,2,1,0:T(8,128)(2,1)S(1)}, u32[]{:S(2)}, u32[]{:S(2)}) collective-permute-start(bf16[1,2,128,256]{3,2,1,0:T(8,128)(2,1)S(1)} %get-tuple-element.33.refs_4_), channel_id=1, source_target_pairs={{0,1},{1,0},{2,3},{3,2},{4,5},{5,4},{6,7},{7,6},{8,9},{9,8},{10,11... | collective-permute-start | bytes 393224 | tf_op jit(solution)/shard_map/ppermute | solution.py:255
  45.8 0.6 collective-permute-done.15.refs_1_
  46.4 0.8 %collective-permute-done.14.refs_0_ = bf16[1,2,128,256]{3,2,1,0:T(8,128)(2,1)S(1)} collective-permute-done((bf16[1,2,128,256]{3,2,1,0:T(8,128)(2,1)S(1)}, bf16[1,2,128,256]{3,2,1,0:T(8,128)(2,1)S(1)}, u32[]{:S(2)}, u32[]{:S(2)}) %collective-permute-start.14) | collective-permute-done | bytes 131104 | tf_op jit(solution)/shard_map/ppermute | solution.py:255
  47.3 2.5 %collective-permute-start.17 = (bf16[1,128,256]{2,1,0:T(8,128)(2,1)S(1)}, bf16[1,128,256]{2,1,0:T(8,128)(2,1)S(1)}, u32[]{:S(2)}, u32[]{:S(2)}) collective-permute-start(bf16[1,128,256]{2,1,0:T(8,128)(2,1)S(1)} %get-tuple-element.29), channel_id=1, source_target_pairs={{0,24},{1,25},{2,26},{3,27},{4,28},{5,29},{6,30},{7,31},{8,16},{9,... | collective-permute-start | bytes 196616 | tf_op jit(solution)/shard_map/ppermute | solution.py:255
  50.0 1.9 %collective-permute-done.13 = bf16[1,2,128,256]{3,2,1,0:T(8,128)(2,1)S(1)} collective-permute-done((bf16[1,2,128,256]{3,2,1,0:T(8,128)(2,1)S(1)}, bf16[1,2,128,256]{3,2,1,0:T(8,128)(2,1)S(1)}, u32[]{:S(2)}, u32[]{:S(2)}) %collective-permute-start.13) | collective-permute-done | bytes 131104 | tf_op jit(solution)/shard_map/ppermute | solution.py:255
  52.1 1.3 %collective-permute-done.17 = bf16[1,128,256]{2,1,0:T(8,128)(2,1)S(1)} collective-permute-done((bf16[1,128,256]{2,1,0:T(8,128)(2,1)S(1)}, bf16[1,128,256]{2,1,0:T(8,128)(2,1)S(1)}, u32[]{:S(2)}, u32[]{:S(2)}) %collective-permute-start.17) | collective-permute-done | bytes 65568 | tf_op jit(solution)/shard_map/ppermute | solution.py:255
  53.4 1.8 %collective-permute-done.18 = bf16[1,128,256]{2,1,0:T(8,128)(2,1)S(1)} collective-permute-done((bf16[1,128,256]{2,1,0:T(8,128)(2,1)S(1)}, bf16[1,128,256]{2,1,0:T(8,128)(2,1)S(1)}, u32[]{:S(2)}, u32[]{:S(2)}) %collective-permute-start.18) | collective-permute-done | bytes 65568 | tf_op jit(solution)/shard_map/ppermute | solution.py:255
  55.2 1.2 %collective-permute-done.19 = bf16[1,128,256]{2,1,0:T(8,128)(2,1)S(1)} collective-permute-done((bf16[1,128,256]{2,1,0:T(8,128)(2,1)S(1)}, bf16[1,128,256]{2,1,0:T(8,128)(2,1)S(1)}, u32[]{:S(2)}, u32[]{:S(2)}) %collective-permute-start.19) | collective-permute-done | bytes 65568 | tf_op jit(solution)/shard_map/ppermute | solution.py:255
  56.4 0.7 %fusion.11 = f32[128,256]{1,0:T(8,128)} fusion(f32[1,2,128,256]{3,2,1,0:T(8,128)S(1)} %fusion.1, bf16[1,128,256]{2,1,0:T(8,128)(2,1)S(1)} %collective-permute-done.19, bf16[1,128,256]{2,1,0:T(8,128)(2,1)S(1)} %collective-permute-done.18, bf16[1,128,256]{2,1,0:T(8,128)(2,1)S(1)} %collective-permute-done.17), kind=kLoop, calls=%fused_computation.20 | loop fusion | flops 196608 | bytes 458752 | tf_op jit(solution)/shard_map/squeeze | solution.py:318
  (29 shorter events, 1.7 us)
Async XLA Ops:
  1.6 7.6 %collective-permute-start.5 = (bf16[1,2,8,1024]{3,2,1,0:T(8,128)(2,1)S(1)}, bf16[1,2,8,1024]{3,2,1,0:T(8,128)(2,1)S(1)}, u32[]{:S(2)}, u32[]{:S(2)}) collective-permute-start(bf16[1,2,8,1024]{3,2,1,0:T(8,128)(2,1)S(1)} %get-tuple-element.24), channel_id=1, source_target_pairs={{0,2},{1,3},{2,0},{3,1},{4,6},{5,7},{6,4},{7,5},{8,10},{9,11},{10,... | collective-permute-start | bytes 98312 | tf_op jit(solution)/shard_map/ppermute | solution.py:255
  2.2 7.0 %collective-permute-start.6 = (bf16[1,2,8,1024]{3,2,1,0:T(8,128)(2,1)S(1)}, bf16[1,2,8,1024]{3,2,1,0:T(8,128)(2,1)S(1)}, u32[]{:S(2)}, u32[]{:S(2)}) collective-permute-start(bf16[1,2,8,1024]{3,2,1,0:T(8,128)(2,1)S(1)} %get-tuple-element.25), channel_id=1, source_target_pairs={{0,4},{1,5},{2,6},{3,7},{4,0},{5,1},{6,2},{7,3},{8,12},{9,13},{10,... | collective-permute-start | bytes 98312 | tf_op jit(solution)/shard_map/ppermute | solution.py:255
  4.7 4.5 %collective-permute-start.7 = (bf16[1,2,8,1024]{3,2,1,0:T(8,128)(2,1)S(1)}, bf16[1,2,8,1024]{3,2,1,0:T(8,128)(2,1)S(1)}, u32[]{:S(2)}, u32[]{:S(2)}) collective-permute-start(bf16[1,2,8,1024]{3,2,1,0:T(8,128)(2,1)S(1)} %get-tuple-element.26), channel_id=1, source_target_pairs={{0,6},{1,7},{2,4},{3,5},{4,2},{5,3},{6,0},{7,1},{8,14},{9,15},{10,... | collective-permute-start | bytes 98312 | tf_op jit(solution)/shard_map/ppermute | solution.py:255
  4.8 7.9 %collective-permute-start = (bf16[4,2,8,1024]{3,2,1,0:T(8,128)(2,1)S(1)}, bf16[4,2,8,1024]{3,2,1,0:T(8,128)(2,1)S(1)}, u32[]{:S(2)}, u32[]{:S(2)}) collective-permute-start(bf16[4,2,8,1024]{3,2,1,0:T(8,128)(2,1)S(1)} %get-tuple-element.21), channel_id=1, source_target_pairs={{0,8},{1,9},{2,10},{3,11},{4,12},{5,13},{6,14},{7,15},{8,0},{9,1},... | collective-permute-start | bytes 393224 | tf_op jit(solution)/shard_map/ppermute | solution.py:255
  6.6 12.9 %collective-permute-start.1 = (bf16[4,2,8,1024]{3,2,1,0:T(8,128)(2,1)S(1)}, bf16[4,2,8,1024]{3,2,1,0:T(8,128)(2,1)S(1)}, u32[]{:S(2)}, u32[]{:S(2)}) collective-permute-start(bf16[4,2,8,1024]{3,2,1,0:T(8,128)(2,1)S(1)} %get-tuple-element.22), channel_id=1, source_target_pairs={{0,16},{1,17},{2,18},{3,19},{4,20},{5,21},{6,22},{7,23},{8,24},{9,... | collective-permute-start | bytes 393224 | tf_op jit(solution)/shard_map/ppermute | solution.py:255
  9.2 14.6 %collective-permute-start.8 = (bf16[4,2,8,1024]{3,2,1,0:T(8,128)(2,1)S(1)}, bf16[4,2,8,1024]{3,2,1,0:T(8,128)(2,1)S(1)}, u32[]{:S(2)}, u32[]{:S(2)}) collective-permute-start(bf16[4,2,8,1024]{3,2,1,0:T(8,128)(2,1)S(1)} %pad_maximum_fusion), channel_id=1, source_target_pairs={{0,24},{1,25},{2,26},{3,27},{4,28},{5,29},{6,30},{7,31},{8,16},{9,... | collective-permute-start | bytes 393224 | tf_op jit(solution)/shard_map/ppermute | solution.py:255
  19.6 4.3 %collective-permute-start.2 = (bf16[3,2,8,1024]{3,2,1,0:T(8,128)(2,1)S(1)}, bf16[3,2,8,1024]{3,2,1,0:T(8,128)(2,1)S(1)}, u32[]{:S(2)}, u32[]{:S(2)}) collective-permute-start(bf16[3,2,8,1024]{3,2,1,0:T(8,128)(2,1)S(1)} %pad_maximum_fusion.1), channel_id=1, source_target_pairs={{0,2},{1,3},{2,0},{3,1},{4,6},{5,7},{6,4},{7,5},{8,10},{9,11},{10,... | collective-permute-start | bytes 294920 | tf_op jit(solution)/shard_map/ppermute | solution.py:255
  19.7 5.7 %collective-permute-start.3 = (bf16[3,2,8,1024]{3,2,1,0:T(8,128)(2,1)S(1)}, bf16[3,2,8,1024]{3,2,1,0:T(8,128)(2,1)S(1)}, u32[]{:S(2)}, u32[]{:S(2)}) collective-permute-start(bf16[3,2,8,1024]{3,2,1,0:T(8,128)(2,1)S(1)} %pad_maximum_fusion.2), channel_id=1, source_target_pairs={{0,4},{1,5},{2,6},{3,7},{4,0},{5,1},{6,2},{7,3},{8,12},{9,13},{10,... | collective-permute-start | bytes 294920 | tf_op jit(solution)/shard_map/ppermute | solution.py:255
  21.2 5.3 %collective-permute-start.4 = (bf16[3,2,8,1024]{3,2,1,0:T(8,128)(2,1)S(1)}, bf16[3,2,8,1024]{3,2,1,0:T(8,128)(2,1)S(1)}, u32[]{:S(2)}, u32[]{:S(2)}) collective-permute-start(bf16[3,2,8,1024]{3,2,1,0:T(8,128)(2,1)S(1)} %pad_maximum_fusion.3), channel_id=1, source_target_pairs={{0,6},{1,7},{2,4},{3,5},{4,2},{5,3},{6,0},{7,1},{8,14},{9,15},{10,... | collective-permute-start | bytes 294920 | tf_op jit(solution)/shard_map/ppermute | solution.py:255
  21.6 4.9 %copy-start = (s32[16]{0:T(128)S(1)}, s32[16]{0:T(128)}, u32[]{:S(2)}) copy-start(s32[16]{0:T(128)} %lags_ref.1) | copy-start | bytes 196
  31.9 2.0 %collective-permute-start.9 = (bf16[2,512,256]{2,1,0:T(8,128)(2,1)S(1)}, bf16[2,512,256]{2,1,0:T(8,128)(2,1)S(1)}, u32[]{:S(2)}, u32[]{:S(2)}) collective-permute-start(bf16[2,512,256]{2,1,0:T(8,128)(2,1)S(1)} %get-tuple-element.28), channel_id=1, source_target_pairs={{0,2},{1,3},{2,0},{3,1},{4,6},{5,7},{6,4},{7,5},{8,10},{9,11},{10,... | collective-permute-start | bytes 1572872 | tf_op jit(solution)/shard_map/ppermute | solution.py:255
  35.3 5.2 %collective-permute-start.10 = (bf16[2,512,256]{2,1,0:T(8,128)(2,1)S(1)}, bf16[2,512,256]{2,1,0:T(8,128)(2,1)S(1)}, u32[]{:S(2)}, u32[]{:S(2)}) collective-permute-start(bf16[2,512,256]{2,1,0:T(8,128)(2,1)S(1)} %order.5), channel_id=1, source_target_pairs={{0,2},{1,3},{2,0},{3,1},{4,6},{5,7},{6,4},{7,5},{8,10},{9,11},{10,... | collective-permute-start | bytes 1572872 | tf_op jit(solution)/shard_map/ppermute | solution.py:255
  36.9 6.9 %collective-permute-start.16 = (bf16[1,2,128,256]{3,2,1,0:T(8,128)(2,1)S(1)}, bf16[1,2,128,256]{3,2,1,0:T(8,128)(2,1)S(1)}, u32[]{:S(2)}, u32[]{:S(2)}) collective-permute-start(bf16[1,2,128,256]{3,2,1,0:T(8,128)(2,1)S(1)} %get-tuple-element.34.refs_2_), channel_id=1, source_target_pairs={{0,5},{1,4},{2,7},{3,6},{4,1},{5,0},{6,3},{7,2},{8,13},{9,12},{10,... | collective-permute-start | bytes 393224 | tf_op jit(solution)/shard_map/ppermute | solution.py:255
  39.5 6.9 %collective-permute-start.15 = (bf16[1,2,128,256]{3,2,1,0:T(8,128)(2,1)S(1)}, bf16[1,2,128,256]{3,2,1,0:T(8,128)(2,1)S(1)}, u32[]{:S(2)}, u32[]{:S(2)}) collective-permute-start(bf16[1,2,128,256]{3,2,1,0:T(8,128)(2,1)S(1)} %get-tuple-element.35.refs_1_), channel_id=1, source_target_pairs={{0,1},{1,0},{2,3},{3,2},{4,5},{5,4},{6,7},{7,6},{8,9},{9,8},{10,11... | collective-permute-start | bytes 393224 | tf_op jit(solution)/shard_map/ppermute | solution.py:255
  40.0 7.2 %collective-permute-start.14 = (bf16[1,2,128,256]{3,2,1,0:T(8,128)(2,1)S(1)}, bf16[1,2,128,256]{3,2,1,0:T(8,128)(2,1)S(1)}, u32[]{:S(2)}, u32[]{:S(2)}) collective-permute-start(bf16[1,2,128,256]{3,2,1,0:T(8,128)(2,1)S(1)} %get-tuple-element.36.refs_0_), channel_id=1, source_target_pairs={{0,4},{1,5},{2,6},{3,7},{4,0},{5,1},{6,2},{7,3},{8,12},{9,13},{10,... | collective-permute-start | bytes 393224 | tf_op jit(solution)/shard_map/ppermute | solution.py:255
  40.6 9.4 %collective-permute-start.11 = (bf16[1,2,128,256]{3,2,1,0:T(8,128)(2,1)S(1)}, bf16[1,2,128,256]{3,2,1,0:T(8,128)(2,1)S(1)}, u32[]{:S(2)}, u32[]{:S(2)}) collective-permute-start(bf16[1,2,128,256]{3,2,1,0:T(8,128)(2,1)S(1)} %get-tuple-element.31.refs_3_), channel_id=1, source_target_pairs={{0,4},{1,5},{2,6},{3,7},{4,0},{5,1},{6,2},{7,3},{8,12},{9,13},{10,... | collective-permute-start | bytes 393224 | tf_op jit(solution)/shard_map/ppermute | solution.py:255
  42.1 9.8 %collective-permute-start.13 = (bf16[1,2,128,256]{3,2,1,0:T(8,128)(2,1)S(1)}, bf16[1,2,128,256]{3,2,1,0:T(8,128)(2,1)S(1)}, u32[]{:S(2)}, u32[]{:S(2)}) collective-permute-start(bf16[1,2,128,256]{3,2,1,0:T(8,128)(2,1)S(1)} %get-tuple-element.32.refs_5_), channel_id=1, source_target_pairs={{0,5},{1,4},{2,7},{3,6},{4,1},{5,0},{6,3},{7,2},{8,13},{9,12},{10,... | collective-permute-start | bytes 393224 | tf_op jit(solution)/shard_map/ppermute | solution.py:255
  43.8 8.1 %collective-permute-start.12 = (bf16[1,2,128,256]{3,2,1,0:T(8,128)(2,1)S(1)}, bf16[1,2,128,256]{3,2,1,0:T(8,128)(2,1)S(1)}, u32[]{:S(2)}, u32[]{:S(2)}) collective-permute-start(bf16[1,2,128,256]{3,2,1,0:T(8,128)(2,1)S(1)} %get-tuple-element.33.refs_4_), channel_id=1, source_target_pairs={{0,1},{1,0},{2,3},{3,2},{4,5},{5,4},{6,7},{7,6},{8,9},{9,8},{10,11... | collective-permute-start | bytes 393224 | tf_op jit(solution)/shard_map/ppermute | solution.py:255
  47.3 6.1 %collective-permute-start.17 = (bf16[1,128,256]{2,1,0:T(8,128)(2,1)S(1)}, bf16[1,128,256]{2,1,0:T(8,128)(2,1)S(1)}, u32[]{:S(2)}, u32[]{:S(2)}) collective-permute-start(bf16[1,128,256]{2,1,0:T(8,128)(2,1)S(1)} %get-tuple-element.29), channel_id=1, source_target_pairs={{0,24},{1,25},{2,26},{3,27},{4,28},{5,29},{6,30},{7,31},{8,16},{9,... | collective-permute-start | bytes 196616 | tf_op jit(solution)/shard_map/ppermute | solution.py:255
  49.8 5.4 %collective-permute-start.18 = (bf16[1,128,256]{2,1,0:T(8,128)(2,1)S(1)}, bf16[1,128,256]{2,1,0:T(8,128)(2,1)S(1)}, u32[]{:S(2)}, u32[]{:S(2)}) collective-permute-start(bf16[1,128,256]{2,1,0:T(8,128)(2,1)S(1)} %get-tuple-element.30), channel_id=1, source_target_pairs={{0,16},{1,17},{2,18},{3,19},{4,20},{5,21},{6,22},{7,23},{8,24},{9,... | collective-permute-start | bytes 196616 | tf_op jit(solution)/shard_map/ppermute | solution.py:255
  52.0 4.3 %collective-permute-start.19 = (bf16[1,128,256]{2,1,0:T(8,128)(2,1)S(1)}, bf16[1,128,256]{2,1,0:T(8,128)(2,1)S(1)}, u32[]{:S(2)}, u32[]{:S(2)}) collective-permute-start(bf16[1,128,256]{2,1,0:T(8,128)(2,1)S(1)} %fusion.12), channel_id=1, source_target_pairs={{0,8},{1,9},{2,10},{3,11},{4,12},{5,13},{6,14},{7,15},{8,0},{9,1},... | collective-permute-start | bytes 196616 | tf_op jit(solution)/shard_map/ppermute | solution.py:255

commit v7 on v5

--- a/solution.py
+++ b/solution.py
@@ -274,7 +274,8 @@
     taps, _, count, _ = kernel_weights.shape
     out_len = steps // 2
     each = count // ranks
-    chunks = (range(1, high), range(1))
+    half = high // 2
+    chunks = (range(half, high), range(half))
     layout = [(z * 2 + x) * 2 + c for zs in chunks for c in (1, 0) for x in range(2) for z in zs]
     parts = sides if out_len // sides % LANES == 0 else 1
     far_rows, near_rows = [len(zs) * 2 * each for zs in chunks]
@@ -309,7 +310,8 @@
         total = total + moved.astype(jnp.float32)
     result = total[:, 0]
     for z in range(high - 1, 0, -1):
-        result = result + swap(far[z - 1], ranks, sides, 4 * z).astype(jnp.float32)
+        send = far[z - half] if z >= half else total[:, z].astype(jnp.bfloat16)
+        result = result + swap(send, ranks, sides, 4 * z).astype(jnp.float32)
     out = result[0]
     for y in range(sides // 2 - 1, 0, -1):
         out = out + swap(result[y].astype(jnp.bfloat16), ranks, sides, 0, 2 * y).astype(jnp.float32)

time: 62.9 us -> 57.6 us (0.916)
  waiting for transfers between devices: 23.4 us -> 20.6 us
  starting transfers between devices: 25.1 us -> 22.6 us
    ppermute x20, waiting for transfers between devices: 23.4 us -> 20.6 us  [swap(): return lax.ppermute(value, AXES, pairs)]
    ppermute x20, starting transfers between devices: 25.1 us -> 22.6 us  [swap(): return lax.ppermute(value, AXES, pairs)]
  transfers between devices with their start and end apart: 20 -> 20, of which waited for: 11 -> 13; matrix products, arithmetic and copies ran while one was open for 0% -> 0% of each run, Pallas kernels for 8% -> 8%
where the time goes in v7:
time: 57.6 us; the launch traced here: 57.4 us
  starting transfers between devices  22.6 us (39%)
  waiting for transfers between devices  20.6 us (36%)
  Pallas kernels  13 us (23%)
  other arithmetic  1.03 us (2%)
    ppermute x20, starting transfers between devices, swap(): return lax.ppermute(value, AXES, pairs)  22.6 us
    ppermute x20, waiting for transfers between devices, swap(): return lax.ppermute(value, AXES, pairs)  20.6 us
    pallas_call x1, Pallas kernels, bands(): pl.pallas_call(functools.partial(bands_kernel, taps, direct, high, first_...  5.4 us
    pallas_call x3, Pallas kernels, order_more(): pl.pallas_call(functools.partial(order_kernel, first_row), out_shape=shap...  3.76 us
    pallas_call x1, Pallas kernels, prepare(): pl.pallas_call(functools.partial(prepare_kernel, ranks, layout), out_shap...  2.19 us
    pallas_call x1, Pallas kernels, outgoing(): pl.pallas_call(functools.partial(outgoing_kernel, direct, high), out_shap...  1.6 us
  transfers between devices with their start and end apart: 20, of which 13 were waited for; matrix products, arithmetic and copies ran while one was open for 0% of the time, Pallas kernels for 8%

profile of v7, /device:TPU:0, one launch (start us, length us, event | category | flops | bytes accessed | tf_op | source)
XLA Modules:
  0.0 57.4 jit_solution(8285738390737691219)
XLA Ops:
  0.0 1.6 %outgoing.1 = (bf16[4,2,8,1024]{3,2,1,0:T(8,128)(2,1)S(1)}, bf16[4,2,8,1024]{3,2,1,0:T(8,128)(2,1)S(1)}, bf16[4,2,8,1024]{3,2,1,0:T(8,128)(2,1)S(1)}, bf16[1,2,8...) custom-call(s32[1,16]{1,0:T(1,128)} %bitcast.48, ...), custom_call_target="tpu_custom_call" | custom-call | tf_op jit(solution)/shard_map/outgoing/pallas_call | solution.py:60
  1.6 0.6 collective-permute-start.5
  2.2 2.6 %collective-permute-start.6 = (bf16[1,2,8,1024]{3,2,1,0:T(8,128)(2,1)S(1)}, bf16[1,2,8,1024]{3,2,1,0:T(8,128)(2,1)S(1)}, u32[]{:S(2)}, u32[]{:S(2)}) collective-permute-start(bf16[1,2,8,1024]{3,2,1,0:T(8,128)(2,1)S(1)} %get-tuple-element.25), channel_id=1, source_target_pairs={{0,4},{1,5},{2,6},{3,7},{4,0},{5,1},{6,2},{7,3},{8,12},{9,13},{10,... | collective-permute-start | bytes 98312 | tf_op jit(solution)/shard_map/ppermute | solution.py:255
  4.8 1.8 %collective-permute-start = (bf16[4,2,8,1024]{3,2,1,0:T(8,128)(2,1)S(1)}, bf16[4,2,8,1024]{3,2,1,0:T(8,128)(2,1)S(1)}, u32[]{:S(2)}, u32[]{:S(2)}) collective-permute-start(bf16[4,2,8,1024]{3,2,1,0:T(8,128)(2,1)S(1)} %get-tuple-element.21), channel_id=1, source_target_pairs={{0,8},{1,9},{2,10},{3,11},{4,12},{5,13},{6,14},{7,15},{8,0},{9,1},... | collective-permute-start | bytes 393224 | tf_op jit(solution)/shard_map/ppermute | solution.py:255
  6.6 2.6 %collective-permute-start.1 = (bf16[4,2,8,1024]{3,2,1,0:T(8,128)(2,1)S(1)}, bf16[4,2,8,1024]{3,2,1,0:T(8,128)(2,1)S(1)}, u32[]{:S(2)}, u32[]{:S(2)}) collective-permute-start(bf16[4,2,8,1024]{3,2,1,0:T(8,128)(2,1)S(1)} %get-tuple-element.22), channel_id=1, source_target_pairs={{0,16},{1,17},{2,18},{3,19},{4,20},{5,21},{6,22},{7,23},{8,24},{9,... | collective-permute-start | bytes 393224 | tf_op jit(solution)/shard_map/ppermute | solution.py:255
  9.2 2.5 %collective-permute-start.8 = (bf16[4,2,8,1024]{3,2,1,0:T(8,128)(2,1)S(1)}, bf16[4,2,8,1024]{3,2,1,0:T(8,128)(2,1)S(1)}, u32[]{:S(2)}, u32[]{:S(2)}) collective-permute-start(bf16[4,2,8,1024]{3,2,1,0:T(8,128)(2,1)S(1)} %pad_maximum_fusion), channel_id=1, source_target_pairs={{0,24},{1,25},{2,26},{3,27},{4,28},{5,29},{6,30},{7,31},{8,16},{9,... | collective-permute-start | bytes 393224 | tf_op jit(solution)/shard_map/ppermute | solution.py:255
  11.8 0.9 %collective-permute-done.refs_1_ = bf16[4,2,8,1024]{3,2,1,0:T(8,128)(2,1)S(1)} collective-permute-done((bf16[4,2,8,1024]{3,2,1,0:T(8,128)(2,1)S(1)}, bf16[4,2,8,1024]{3,2,1,0:T(8,128)(2,1)S(1)}, u32[]{:S(2)}, u32[]{:S(2)}) %collective-permute-start) | collective-permute-done | bytes 131104 | tf_op jit(solution)/shard_map/ppermute | solution.py:255
  12.7 6.8 %collective-permute-done.1.refs_2_ = bf16[4,2,8,1024]{3,2,1,0:T(8,128)(2,1)S(1)} collective-permute-done((bf16[4,2,8,1024]{3,2,1,0:T(8,128)(2,1)S(1)}, bf16[4,2,8,1024]{3,2,1,0:T(8,128)(2,1)S(1)}, u32[]{:S(2)}, u32[]{:S(2)}) %collective-permute-start.1) | collective-permute-done | bytes 131104 | tf_op jit(solution)/shard_map/ppermute | solution.py:255
  19.7 1.6 %collective-permute-start.3 = (bf16[3,2,8,1024]{3,2,1,0:T(8,128)(2,1)S(1)}, bf16[3,2,8,1024]{3,2,1,0:T(8,128)(2,1)S(1)}, u32[]{:S(2)}, u32[]{:S(2)}) collective-permute-start(bf16[3,2,8,1024]{3,2,1,0:T(8,128)(2,1)S(1)} %pad_maximum_fusion.2), channel_id=1, source_target_pairs={{0,4},{1,5},{2,6},{3,7},{4,0},{5,1},{6,2},{7,3},{8,12},{9,13},{10,... | collective-permute-start | bytes 294920 | tf_op jit(solution)/shard_map/ppermute | solution.py:255
  21.2 0.4 collective-permute-start.4
  21.7 2.2 %prepare.1 = (bf16[2048,2048]{1,0:T(8,128)(2,1)S(1)}, bf16[2048,768]{1,0:T(8,128)(2,1)S(1)}) custom-call(s32[1,2048]{1,0:T(1,128)} %bitcast.49, bf16[2,3,2048,128]{3,2,1,0:T(8,128)(2,1)} %weights_hbm.1), custom_call_target="tpu_custom_call" | custom-call | flops 2000000000 | bytes 10000000 | tf_op jit(solution)/shard_map/prepare/pallas_call | solution.py:105
  23.9 1.5 %collective-permute-done.3.refs_4_ = bf16[3,2,8,1024]{3,2,1,0:T(8,128)(2,1)S(1)} collective-permute-done((bf16[3,2,8,1024]{3,2,1,0:T(8,128)(2,1)S(1)}, bf16[3,2,8,1024]{3,2,1,0:T(8,128)(2,1)S(1)}, u32[]{:S(2)}, u32[]{:S(2)}) %collective-permute-start.3) | collective-permute-done | bytes 98336 | tf_op jit(solution)/shard_map/ppermute | solution.py:255
  25.4 1.1 %collective-permute-done.4.refs_5_ = bf16[3,2,8,1024]{3,2,1,0:T(8,128)(2,1)S(1)} collective-permute-done((bf16[3,2,8,1024]{3,2,1,0:T(8,128)(2,1)S(1)}, bf16[3,2,8,1024]{3,2,1,0:T(8,128)(2,1)S(1)}, u32[]{:S(2)}, u32[]{:S(2)}) %collective-permute-start.4) | collective-permute-done | bytes 98336 | tf_op jit(solution)/shard_map/ppermute | solution.py:255
  26.5 5.4 %bands.1 = (bf16[2048,512]{1,0:T(8,128)(2,1)S(1)}, bf16[2,512,256]{2,1,0:T(8,128)(2,1)S(1)}) custom-call(s32[16]{0:T(128)S(1)} %copy-done, bf16[2048,768]{1,0:T(8,128)(2,1)S(1)} %get-tuple-element.18.joined_ref, bf16[2048,2048]{1,0:T(8,128)(2,1)S(1)} %get-tuple-element.19.select_ref, bf16[4,2,8,1024]{3,2,1,0:T(8,128)(2,1)S(1)} %get-tuple-element.20.refs_0_, ...), custom_call_target="tpu_custom_call" | custom-call | flops 4000000000 | bytes 10000000 | tf_op jit(solution)/shard_map/bands/pallas_call | solution.py:197
  31.9 0.4 collective-permute-start.9
  32.3 1.2 %order.4 = bf16[2,512,256]{2,1,0:T(8,128)(2,1)S(1)} custom-call(bf16[2048,512]{1,0:T(8,128)(2,1)S(1)} %get-tuple-element.27.banded_ref, bf16[2048,2048]{1,0:T(8,128)(2,1)S(1)} %get-tuple-element.19.select_ref), custom_call_target="tpu_custom_call" | custom-call | flops 1000000000 | bytes 5000000 | tf_op jit(solution)/shard_map/order/pallas_call | solution.py:218
  34.0 1.3 %order.5 = bf16[2,512,256]{2,1,0:T(8,128)(2,1)S(1)} custom-call(bf16[2048,512]{1,0:T(8,128)(2,1)S(1)} %get-tuple-element.27.banded_ref, bf16[2048,2048]{1,0:T(8,128)(2,1)S(1)} %get-tuple-element.19.select_ref, bf16[1,2,128,256]{3,2,1,0:T(8,128)(2,1)S(1)} %get-tuple-element.36.refs_0_, bf16[1,2,128,256]{3,2,1,0:T(8,128)(2,1)S(1)} %get-tuple-element.35.refs_1_, ...), custom_call_target="tpu_custom_call" | custom-call | flops 1000000000 | bytes 5000000 | tf_op jit(solution)/shard_map/order/pallas_call | solution.py:218
  35.7 1.3 %order.3 = bf16[2,512,256]{2,1,0:T(8,128)(2,1)S(1)} custom-call(bf16[2048,512]{1,0:T(8,128)(2,1)S(1)} %get-tuple-element.27.banded_ref, bf16[2048,2048]{1,0:T(8,128)(2,1)S(1)} %get-tuple-element.19.select_ref), custom_call_target="tpu_custom_call" | custom-call | flops 1000000000 | bytes 5000000 | tf_op jit(solution)/shard_map/order/pallas_call | solution.py:218
  36.9 1.6 %collective-permute-start.16 = (bf16[1,2,128,256]{3,2,1,0:T(8,128)(2,1)S(1)}, bf16[1,2,128,256]{3,2,1,0:T(8,128)(2,1)S(1)}, u32[]{:S(2)}, u32[]{:S(2)}) collective-permute-start(bf16[1,2,128,256]{3,2,1,0:T(8,128)(2,1)S(1)} %get-tuple-element.34.refs_2_), channel_id=1, source_target_pairs={{0,1},{1,0},{2,3},{3,2},{4,5},{5,4},{6,7},{7,6},{8,9},{9,8},{10,11... | collective-permute-start | bytes 393224 | tf_op jit(solution)/shard_map/ppermute | solution.py:255
  38.5 1.5 %collective-permute-start.15 = (bf16[1,2,128,256]{3,2,1,0:T(8,128)(2,1)S(1)}, bf16[1,2,128,256]{3,2,1,0:T(8,128)(2,1)S(1)}, u32[]{:S(2)}, u32[]{:S(2)}) collective-permute-start(bf16[1,2,128,256]{3,2,1,0:T(8,128)(2,1)S(1)} %get-tuple-element.35.refs_1_), channel_id=1, source_target_pairs={{0,4},{1,5},{2,6},{3,7},{4,0},{5,1},{6,2},{7,3},{8,12},{9,13},{10,... | collective-permute-start | bytes 393224 | tf_op jit(solution)/shard_map/ppermute | solution.py:255
  40.0 0.4 collective-permute-start.14
  40.6 2.5 %collective-permute-start.11 = (bf16[1,2,128,256]{3,2,1,0:T(8,128)(2,1)S(1)}, bf16[1,2,128,256]{3,2,1,0:T(8,128)(2,1)S(1)}, u32[]{:S(2)}, u32[]{:S(2)}) collective-permute-start(bf16[1,2,128,256]{3,2,1,0:T(8,128)(2,1)S(1)} %get-tuple-element.31.refs_3_), channel_id=1, source_target_pairs={{0,5},{1,4},{2,7},{3,6},{4,1},{5,0},{6,3},{7,2},{8,13},{9,12},{10,... | collective-permute-start | bytes 393224 | tf_op jit(solution)/shard_map/ppermute | solution.py:255
  43.1 0.5 collective-permute-start.13
  43.6 0.5 collective-permute-start.12
  44.1 0.8 %collective-permute-done.15.refs_1_ = bf16[1,2,128,256]{3,2,1,0:T(8,128)(2,1)S(1)} collective-permute-done((bf16[1,2,128,256]{3,2,1,0:T(8,128)(2,1)S(1)}, bf16[1,2,128,256]{3,2,1,0:T(8,128)(2,1)S(1)}, u32[]{:S(2)}, u32[]{:S(2)}) %collective-permute-start.15) | collective-permute-done | bytes 131104 | tf_op jit(solution)/shard_map/ppermute | solution.py:255
  44.9 2.5 %collective-permute-done.14.refs_0_ = bf16[1,2,128,256]{3,2,1,0:T(8,128)(2,1)S(1)} collective-permute-done((bf16[1,2,128,256]{3,2,1,0:T(8,128)(2,1)S(1)}, bf16[1,2,128,256]{3,2,1,0:T(8,128)(2,1)S(1)}, u32[]{:S(2)}, u32[]{:S(2)}) %collective-permute-start.14) | collective-permute-done | bytes 131104 | tf_op jit(solution)/shard_map/ppermute | solution.py:255
  47.5 2.5 %collective-permute-start.17 = (bf16[1,128,256]{2,1,0:T(8,128)(2,1)S(1)}, bf16[1,128,256]{2,1,0:T(8,128)(2,1)S(1)}, u32[]{:S(2)}, u32[]{:S(2)}) collective-permute-start(bf16[1,128,256]{2,1,0:T(8,128)(2,1)S(1)} %get-tuple-element.29), channel_id=1, source_target_pairs={{0,24},{1,25},{2,26},{3,27},{4,28},{5,29},{6,30},{7,31},{8,16},{9,... | collective-permute-start | bytes 196616 | tf_op jit(solution)/shard_map/ppermute | solution.py:255
  50.2 2.1 %collective-permute-done.13 = bf16[1,2,128,256]{3,2,1,0:T(8,128)(2,1)S(1)} collective-permute-done((bf16[1,2,128,256]{3,2,1,0:T(8,128)(2,1)S(1)}, bf16[1,2,128,256]{3,2,1,0:T(8,128)(2,1)S(1)}, u32[]{:S(2)}, u32[]{:S(2)}) %collective-permute-start.13) | collective-permute-done | bytes 131104 | tf_op jit(solution)/shard_map/ppermute | solution.py:255
  52.5 1.2 %collective-permute-done.17 = bf16[1,128,256]{2,1,0:T(8,128)(2,1)S(1)} collective-permute-done((bf16[1,128,256]{2,1,0:T(8,128)(2,1)S(1)}, bf16[1,128,256]{2,1,0:T(8,128)(2,1)S(1)}, u32[]{:S(2)}, u32[]{:S(2)}) %collective-permute-start.17) | collective-permute-done | bytes 65568 | tf_op jit(solution)/shard_map/ppermute | solution.py:255
  53.7 1.5 %collective-permute-done.18 = bf16[1,128,256]{2,1,0:T(8,128)(2,1)S(1)} collective-permute-done((bf16[1,128,256]{2,1,0:T(8,128)(2,1)S(1)}, bf16[1,128,256]{2,1,0:T(8,128)(2,1)S(1)}, u32[]{:S(2)}, u32[]{:S(2)}) %collective-permute-start.18) | collective-permute-done | bytes 65568 | tf_op jit(solution)/shard_map/ppermute | solution.py:255
  55.2 1.6 %collective-permute-done.19 = bf16[1,128,256]{2,1,0:T(8,128)(2,1)S(1)} collective-permute-done((bf16[1,128,256]{2,1,0:T(8,128)(2,1)S(1)}, bf16[1,128,256]{2,1,0:T(8,128)(2,1)S(1)}, u32[]{:S(2)}, u32[]{:S(2)}) %collective-permute-start.19) | collective-permute-done | bytes 65568 | tf_op jit(solution)/shard_map/ppermute | solution.py:255
  56.8 0.7 %fusion.11 = f32[128,256]{1,0:T(8,128)} fusion(f32[1,2,128,256]{3,2,1,0:T(8,128)S(1)} %fusion.1, bf16[1,128,256]{2,1,0:T(8,128)(2,1)S(1)} %collective-permute-done.19, bf16[1,128,256]{2,1,0:T(8,128)(2,1)S(1)} %collective-permute-done.18, bf16[1,128,256]{2,1,0:T(8,128)(2,1)S(1)} %collective-permute-done.17), kind=kLoop, calls=%fused_computation.20 | loop fusion | flops 196608 | bytes 458752 | tf_op jit(solution)/shard_map/squeeze | solution.py:315
  (29 shorter events, 1.6 us)
Async XLA Ops:
  1.6 7.6 %collective-permute-start.5 = (bf16[1,2,8,1024]{3,2,1,0:T(8,128)(2,1)S(1)}, bf16[1,2,8,1024]{3,2,1,0:T(8,128)(2,1)S(1)}, u32[]{:S(2)}, u32[]{:S(2)}) collective-permute-start(bf16[1,2,8,1024]{3,2,1,0:T(8,128)(2,1)S(1)} %get-tuple-element.24), channel_id=1, source_target_pairs={{0,2},{1,3},{2,0},{3,1},{4,6},{5,7},{6,4},{7,5},{8,10},{9,11},{10,... | collective-permute-start | bytes 98312 | tf_op jit(solution)/shard_map/ppermute | solution.py:255
  2.2 7.0 %collective-permute-start.6 = (bf16[1,2,8,1024]{3,2,1,0:T(8,128)(2,1)S(1)}, bf16[1,2,8,1024]{3,2,1,0:T(8,128)(2,1)S(1)}, u32[]{:S(2)}, u32[]{:S(2)}) collective-permute-start(bf16[1,2,8,1024]{3,2,1,0:T(8,128)(2,1)S(1)} %get-tuple-element.25), channel_id=1, source_target_pairs={{0,4},{1,5},{2,6},{3,7},{4,0},{5,1},{6,2},{7,3},{8,12},{9,13},{10,... | collective-permute-start | bytes 98312 | tf_op jit(solution)/shard_map/ppermute | solution.py:255
  4.7 4.5 %collective-permute-start.7 = (bf16[1,2,8,1024]{3,2,1,0:T(8,128)(2,1)S(1)}, bf16[1,2,8,1024]{3,2,1,0:T(8,128)(2,1)S(1)}, u32[]{:S(2)}, u32[]{:S(2)}) collective-permute-start(bf16[1,2,8,1024]{3,2,1,0:T(8,128)(2,1)S(1)} %get-tuple-element.26), channel_id=1, source_target_pairs={{0,6},{1,7},{2,4},{3,5},{4,2},{5,3},{6,0},{7,1},{8,14},{9,15},{10,... | collective-permute-start | bytes 98312 | tf_op jit(solution)/shard_map/ppermute | solution.py:255
  4.8 7.9 %collective-permute-start = (bf16[4,2,8,1024]{3,2,1,0:T(8,128)(2,1)S(1)}, bf16[4,2,8,1024]{3,2,1,0:T(8,128)(2,1)S(1)}, u32[]{:S(2)}, u32[]{:S(2)}) collective-permute-start(bf16[4,2,8,1024]{3,2,1,0:T(8,128)(2,1)S(1)} %get-tuple-element.21), channel_id=1, source_target_pairs={{0,8},{1,9},{2,10},{3,11},{4,12},{5,13},{6,14},{7,15},{8,0},{9,1},... | collective-permute-start | bytes 393224 | tf_op jit(solution)/shard_map/ppermute | solution.py:255
  6.6 12.9 %collective-permute-start.1 = (bf16[4,2,8,1024]{3,2,1,0:T(8,128)(2,1)S(1)}, bf16[4,2,8,1024]{3,2,1,0:T(8,128)(2,1)S(1)}, u32[]{:S(2)}, u32[]{:S(2)}) collective-permute-start(bf16[4,2,8,1024]{3,2,1,0:T(8,128)(2,1)S(1)} %get-tuple-element.22), channel_id=1, source_target_pairs={{0,16},{1,17},{2,18},{3,19},{4,20},{5,21},{6,22},{7,23},{8,24},{9,... | collective-permute-start | bytes 393224 | tf_op jit(solution)/shard_map/ppermute | solution.py:255
  9.2 14.6 %collective-permute-start.8 = (bf16[4,2,8,1024]{3,2,1,0:T(8,128)(2,1)S(1)}, bf16[4,2,8,1024]{3,2,1,0:T(8,128)(2,1)S(1)}, u32[]{:S(2)}, u32[]{:S(2)}) collective-permute-start(bf16[4,2,8,1024]{3,2,1,0:T(8,128)(2,1)S(1)} %pad_maximum_fusion), channel_id=1, source_target_pairs={{0,24},{1,25},{2,26},{3,27},{4,28},{5,29},{6,30},{7,31},{8,16},{9,... | collective-permute-start | bytes 393224 | tf_op jit(solution)/shard_map/ppermute | solution.py:255
  19.6 4.3 %collective-permute-start.2 = (bf16[3,2,8,1024]{3,2,1,0:T(8,128)(2,1)S(1)}, bf16[3,2,8,1024]{3,2,1,0:T(8,128)(2,1)S(1)}, u32[]{:S(2)}, u32[]{:S(2)}) collective-permute-start(bf16[3,2,8,1024]{3,2,1,0:T(8,128)(2,1)S(1)} %pad_maximum_fusion.1), channel_id=1, source_target_pairs={{0,2},{1,3},{2,0},{3,1},{4,6},{5,7},{6,4},{7,5},{8,10},{9,11},{10,... | collective-permute-start | bytes 294920 | tf_op jit(solution)/shard_map/ppermute | solution.py:255
  19.7 5.7 %collective-permute-start.3 = (bf16[3,2,8,1024]{3,2,1,0:T(8,128)(2,1)S(1)}, bf16[3,2,8,1024]{3,2,1,0:T(8,128)(2,1)S(1)}, u32[]{:S(2)}, u32[]{:S(2)}) collective-permute-start(bf16[3,2,8,1024]{3,2,1,0:T(8,128)(2,1)S(1)} %pad_maximum_fusion.2), channel_id=1, source_target_pairs={{0,4},{1,5},{2,6},{3,7},{4,0},{5,1},{6,2},{7,3},{8,12},{9,13},{10,... | collective-permute-start | bytes 294920 | tf_op jit(solution)/shard_map/ppermute | solution.py:255
  21.2 5.3 %collective-permute-start.4 = (bf16[3,2,8,1024]{3,2,1,0:T(8,128)(2,1)S(1)}, bf16[3,2,8,1024]{3,2,1,0:T(8,128)(2,1)S(1)}, u32[]{:S(2)}, u32[]{:S(2)}) collective-permute-start(bf16[3,2,8,1024]{3,2,1,0:T(8,128)(2,1)S(1)} %pad_maximum_fusion.3), channel_id=1, source_target_pairs={{0,6},{1,7},{2,4},{3,5},{4,2},{5,3},{6,0},{7,1},{8,14},{9,15},{10,... | collective-permute-start | bytes 294920 | tf_op jit(solution)/shard_map/ppermute | solution.py:255
  21.6 4.9 %copy-start = (s32[16]{0:T(128)S(1)}, s32[16]{0:T(128)}, u32[]{:S(2)}) copy-start(s32[16]{0:T(128)} %lags_ref.1) | copy-start | bytes 196
  31.9 2.0 %collective-permute-start.9 = (bf16[2,512,256]{2,1,0:T(8,128)(2,1)S(1)}, bf16[2,512,256]{2,1,0:T(8,128)(2,1)S(1)}, u32[]{:S(2)}, u32[]{:S(2)}) collective-permute-start(bf16[2,512,256]{2,1,0:T(8,128)(2,1)S(1)} %get-tuple-element.28), channel_id=1, source_target_pairs={{0,2},{1,3},{2,0},{3,1},{4,6},{5,7},{6,4},{7,5},{8,10},{9,11},{10,... | collective-permute-start | bytes 1572872 | tf_op jit(solution)/shard_map/ppermute | solution.py:255
  35.3 5.2 %collective-permute-start.10 = (bf16[2,512,256]{2,1,0:T(8,128)(2,1)S(1)}, bf16[2,512,256]{2,1,0:T(8,128)(2,1)S(1)}, u32[]{:S(2)}, u32[]{:S(2)}) collective-permute-start(bf16[2,512,256]{2,1,0:T(8,128)(2,1)S(1)} %order.5), channel_id=1, source_target_pairs={{0,2},{1,3},{2,0},{3,1},{4,6},{5,7},{6,4},{7,5},{8,10},{9,11},{10,... | collective-permute-start | bytes 1572872 | tf_op jit(solution)/shard_map/ppermute | solution.py:255
  36.9 6.7 %collective-permute-start.16 = (bf16[1,2,128,256]{3,2,1,0:T(8,128)(2,1)S(1)}, bf16[1,2,128,256]{3,2,1,0:T(8,128)(2,1)S(1)}, u32[]{:S(2)}, u32[]{:S(2)}) collective-permute-start(bf16[1,2,128,256]{3,2,1,0:T(8,128)(2,1)S(1)} %get-tuple-element.34.refs_2_), channel_id=1, source_target_pairs={{0,1},{1,0},{2,3},{3,2},{4,5},{5,4},{6,7},{7,6},{8,9},{9,8},{10,11... | collective-permute-start | bytes 393224 | tf_op jit(solution)/shard_map/ppermute | solution.py:255
  38.5 6.4 %collective-permute-start.15 = (bf16[1,2,128,256]{3,2,1,0:T(8,128)(2,1)S(1)}, bf16[1,2,128,256]{3,2,1,0:T(8,128)(2,1)S(1)}, u32[]{:S(2)}, u32[]{:S(2)}) collective-permute-start(bf16[1,2,128,256]{3,2,1,0:T(8,128)(2,1)S(1)} %get-tuple-element.35.refs_1_), channel_id=1, source_target_pairs={{0,4},{1,5},{2,6},{3,7},{4,0},{5,1},{6,2},{7,3},{8,12},{9,13},{10,... | collective-permute-start | bytes 393224 | tf_op jit(solution)/shard_map/ppermute | solution.py:255
  40.0 7.4 %collective-permute-start.14 = (bf16[1,2,128,256]{3,2,1,0:T(8,128)(2,1)S(1)}, bf16[1,2,128,256]{3,2,1,0:T(8,128)(2,1)S(1)}, u32[]{:S(2)}, u32[]{:S(2)}) collective-permute-start(bf16[1,2,128,256]{3,2,1,0:T(8,128)(2,1)S(1)} %get-tuple-element.36.refs_0_), channel_id=1, source_target_pairs={{0,5},{1,4},{2,7},{3,6},{4,1},{5,0},{6,3},{7,2},{8,13},{9,12},{10,... | collective-permute-start | bytes 393224 | tf_op jit(solution)/shard_map/ppermute | solution.py:255
  40.6 9.6 %collective-permute-start.11 = (bf16[1,2,128,256]{3,2,1,0:T(8,128)(2,1)S(1)}, bf16[1,2,128,256]{3,2,1,0:T(8,128)(2,1)S(1)}, u32[]{:S(2)}, u32[]{:S(2)}) collective-permute-start(bf16[1,2,128,256]{3,2,1,0:T(8,128)(2,1)S(1)} %get-tuple-element.31.refs_3_), channel_id=1, source_target_pairs={{0,5},{1,4},{2,7},{3,6},{4,1},{5,0},{6,3},{7,2},{8,13},{9,12},{10,... | collective-permute-start | bytes 393224 | tf_op jit(solution)/shard_map/ppermute | solution.py:255
  43.1 9.1 %collective-permute-start.13 = (bf16[1,2,128,256]{3,2,1,0:T(8,128)(2,1)S(1)}, bf16[1,2,128,256]{3,2,1,0:T(8,128)(2,1)S(1)}, u32[]{:S(2)}, u32[]{:S(2)}) collective-permute-start(bf16[1,2,128,256]{3,2,1,0:T(8,128)(2,1)S(1)} %get-tuple-element.32.refs_5_), channel_id=1, source_target_pairs={{0,1},{1,0},{2,3},{3,2},{4,5},{5,4},{6,7},{7,6},{8,9},{9,8},{10,11... | collective-permute-start | bytes 393224 | tf_op jit(solution)/shard_map/ppermute | solution.py:255
  43.6 8.7 %collective-permute-start.12 = (bf16[1,2,128,256]{3,2,1,0:T(8,128)(2,1)S(1)}, bf16[1,2,128,256]{3,2,1,0:T(8,128)(2,1)S(1)}, u32[]{:S(2)}, u32[]{:S(2)}) collective-permute-start(bf16[1,2,128,256]{3,2,1,0:T(8,128)(2,1)S(1)} %get-tuple-element.33.refs_4_), channel_id=1, source_target_pairs={{0,4},{1,5},{2,6},{3,7},{4,0},{5,1},{6,2},{7,3},{8,12},{9,13},{10,... | collective-permute-start | bytes 393224 | tf_op jit(solution)/shard_map/ppermute | solution.py:255
  47.5 6.2 %collective-permute-start.17 = (bf16[1,128,256]{2,1,0:T(8,128)(2,1)S(1)}, bf16[1,128,256]{2,1,0:T(8,128)(2,1)S(1)}, u32[]{:S(2)}, u32[]{:S(2)}) collective-permute-start(bf16[1,128,256]{2,1,0:T(8,128)(2,1)S(1)} %get-tuple-element.29), channel_id=1, source_target_pairs={{0,24},{1,25},{2,26},{3,27},{4,28},{5,29},{6,30},{7,31},{8,16},{9,... | collective-permute-start | bytes 196616 | tf_op jit(solution)/shard_map/ppermute | solution.py:255
  50.0 5.2 %collective-permute-start.18 = (bf16[1,128,256]{2,1,0:T(8,128)(2,1)S(1)}, bf16[1,128,256]{2,1,0:T(8,128)(2,1)S(1)}, u32[]{:S(2)}, u32[]{:S(2)}) collective-permute-start(bf16[1,128,256]{2,1,0:T(8,128)(2,1)S(1)} %get-tuple-element.30), channel_id=1, source_target_pairs={{0,16},{1,17},{2,18},{3,19},{4,20},{5,21},{6,22},{7,23},{8,24},{9,... | collective-permute-start | bytes 196616 | tf_op jit(solution)/shard_map/ppermute | solution.py:255
  52.4 4.3 %collective-permute-start.19 = (bf16[1,128,256]{2,1,0:T(8,128)(2,1)S(1)}, bf16[1,128,256]{2,1,0:T(8,128)(2,1)S(1)}, u32[]{:S(2)}, u32[]{:S(2)}) collective-permute-start(bf16[1,128,256]{2,1,0:T(8,128)(2,1)S(1)} %fusion.12), channel_id=1, source_target_pairs={{0,8},{1,9},{2,10},{3,11},{4,12},{5,13},{6,14},{7,15},{8,0},{9,1},... | collective-permute-start | bytes 196616 | tf_op jit(solution)/shard_map/ppermute | solution.py:255
